TPU v7x, 32 devices: a whole 2x2x4 slice. The times are simulated.
32 devices in a mesh: seq: 8 (over z, core), dp: 4 (over y, x).
Axes of the slice: x: 2, y: 2, z: 4, core: 2. Of those that a mesh axis runs over, the one named last changes fastest.
Arguments:
- block_input: bfloat16 [4, 1024, 4096], P('dp', 'seq'), may hold values from -8 to 8
- cotangent: bfloat16 [4, 1024, 4096], P('dp', 'seq'), may hold values from -6 to 6
- pool_weight: float32 [4, 4, 4096], P(None, None, 'dp'), may hold values from 0.1 to 0.6
Outputs:
- input_grad: bfloat16 [4, 1024, 4096], P('dp', 'seq')
- weight_grad: float32 [4, 4, 4096], P(None, None, 'dp')
All inputs are finite; a program needn't handle non-finite values.
Results may differ from a plain program's by a relative error of at most 0.009.
Values may be sent and summed in bfloat16 or wider, within the bound.
No kernel may reach another device: no remote copies, remote signals or barrier semaphores. Data moves between devices by JAX's collectives and lax.ppermute only.
A program may use at most 64 MiB of HBM per device.

v0:
```python
import functools

import jax
import jax.numpy as jnp
from jax import lax
from jax.experimental import pallas as pl
from jax.experimental.pallas import tpu as pltpu
from jax.sharding import PartitionSpec as P


HEAD_DIM = 128
POOL = 4
KINDS = 4
CHUNKS = 2
BF16 = jnp.bfloat16
F32 = jnp.float32


VMEM = pl.BlockSpec(memory_space=pltpu.VMEM)
ANY = pl.BlockSpec(memory_space=pl.ANY)


def dot(a, b, ca, cb):
    return lax.dot_general(a, b, (((ca,), (cb,)), ((), ())), preferred_element_type=F32)


def messages(n):
    nz = n // 2
    steps = sorted(range(nz), key=lambda d: (-min(d, nz - d), d))
    return [(d, c) for d in steps for c in range(2) if (d, c) != (0, 0)]


def target(s, n, message, sign=1):
    nz = n // 2
    step, flip = message
    if isinstance(s, int):
        half, core = divmod(s, 2)
        chip = (half + (step if sign > 0 else nz - step)) % nz
    else:
        half, core = lax.div(s, 2), lax.rem(s, 2)
        chip = lax.rem(half + (step if sign > 0 else nz - step), nz)
    return 2 * chip + (1 - core if flip else core)


def send(block, n, message):
    pairs = [(s, target(s, n, message)) for s in range(n)]
    return lax.ppermute(block, "seq", pairs)


def places(n, sign=1):
    me = lax.axis_index("seq")
    return [me] + [target(me, n, m, sign) for m in messages(n)]


def interleave_matrix(rows):
    r = lax.broadcasted_iota(jnp.int32, (rows, rows), 0)
    t = lax.broadcasted_iota(jnp.int32, (rows, rows), 1)
    hit = t == POOL * r
    for j in range(1, POOL):
        hit = hit | (t - j == POOL * r - j * rows)
    return jnp.where(hit, 1.0, 0.0).astype(BF16)


def aligned(index, size):
    return pl.ds(pl.multiple_of(index * size, size), size)


def cut_kernel(n, wide, first, x_ref, y_ref, *refs):
    outs, sem = refs[:n], refs[n]
    rows = x_ref.shape[0]
    cw = outs[0].shape[1]
    copies = []
    goal = places(n)
    for i in range(n):
        cols = pl.ds(pl.multiple_of(goal[i] * wide + first, HEAD_DIM), cw)
        for t, ref in enumerate((x_ref, y_ref)):
            copy = pltpu.make_async_copy(ref.at[:, cols], outs[i].at[t * rows : (t + 1) * rows, :], sem.at[2 * i + t])
            copy.start()
            copies.append(copy)
    for copy in copies:
        copy.wait()


def block_kernel(n, nd, rc, wide, first, weight, *refs):
    blocks = refs[:n]
    outs = refs[n : 2 * n]
    q_ref, k_ref, v_ref, x_ref, y_ref, g_ref, a_ref, qg, kg, vg, wg_ref = refs[2 * n :]
    length, width = q_ref.shape
    rows = rc * POOL
    place, goal = places(n, -1), places(n)
    me, col, share = lax.axis_index("seq"), lax.axis_index("dp"), n // nd
    w = weight[
        lax.rem(col - lax.div(me, share) + nd, nd),
        :,
        pl.ds(pl.multiple_of(lax.rem(me, share) * wide + first, HEAD_DIM), width),
    ]
    sel = interleave_matrix(rows)
    for i in range(n):
        at = aligned(place[i], rc)
        x = dot(sel, blocks[i][:rows, :], 1, 0)
        y = dot(sel, blocks[i][rows:, :], 1, 0)
        for j in range(POOL):
            x_ref[j, at, :] = x[j * rc : (j + 1) * rc].astype(BF16)
            y_ref[j, at, :] = y[j * rc : (j + 1) * rc].astype(BF16)
        for t, (ref, src) in enumerate(((q_ref, x), (k_ref, x), (v_ref, x), (g_ref, y))):
            total = src[:rc] * w[t * POOL][None, :]
            for j in range(1, POOL):
                total = total + src[j * rc : (j + 1) * rc] * w[t * POOL + j][None, :]
            ref[at, :] = total.astype(BF16).astype(ref.dtype)
    g_ref[length:, :] = jnp.zeros((8, width), F32)
    g_ref[:length, :] = g_ref[1 : length + 1, :]
    a_ref[:8, :] = jnp.zeros((8, width), F32)
    scale = HEAD_DIM**-0.5
    step = min(length, 256)
    many = length > step
    if many:
        kg[...] = jnp.zeros_like(kg)
        vg[...] = jnp.zeros_like(vg)
    for h in range(width // HEAD_DIM):
        cols = slice(h * HEAD_DIM, (h + 1) * HEAD_DIM)

        def body(start):
            at = pl.ds(start, step)
            q, k, v = q_ref[at, cols], k_ref[:, cols], v_ref[:, cols]
            s = dot(q, k, 1, 1) * scale
            qi = lax.broadcasted_iota(jnp.int32, s.shape, 0) + start
            ki = lax.broadcasted_iota(jnp.int32, s.shape, 1)
            s = jnp.where(qi >= ki, s, -1e30)
            e = jnp.exp(s - jnp.max(s, -1, keepdims=True))
            p = e * (1.0 / jnp.sum(e, -1, keepdims=True))
            p_low = p.astype(BF16)
            attended = dot(p_low, v, 1, 0)
            later = g_ref[at, cols]
            low = later.astype(BF16)
            delta = jnp.sum(later * attended, -1, keepdims=True)
            sg = (p * (dot(low, v, 1, 1) - delta)).astype(BF16)
            a_ref[pl.ds(start + 8, step), cols] = attended
            qg[at, cols] = (dot(sg, k, 1, 0) * scale).astype(BF16).astype(F32)
            new_k = dot(sg, q, 0, 0) * scale
            new_v = dot(p_low, low, 0, 0)
            if many:
                kg[:, cols] += new_k
                vg[:, cols] += new_v
            else:
                kg[:, cols] = new_k.astype(BF16).astype(F32)
                vg[:, cols] = new_v.astype(BF16).astype(F32)

        if many:

            def run(i, carry):
                body(pl.multiple_of(i * step, step))
                return carry

            lax.fori_loop(0, length // step, run, 0)
        else:
            body(0)
    if many:
        kg[...] = kg[...].astype(BF16).astype(F32)
        vg[...] = vg[...].astype(BF16).astype(F32)
    for t, ref in enumerate((qg, kg, vg)):
        for i in range(n):
            outs[i][t * rc : (t + 1) * rc, :] = ref[aligned(goal[i], rc), :].astype(BF16)
        for j in range(POOL):
            wg_ref[t * POOL + j, :] = jnp.sum(ref[...] * x_ref[j].astype(F32), 0)
    shifted = a_ref[7 : length + 7, :].astype(BF16).astype(F32)
    for j in range(POOL):
        wg_ref[3 * POOL + j, :] = jnp.sum(shifted * y_ref[j].astype(F32), 0)
    low = wg_ref[...].astype(BF16)
    for i in range(n):
        outs[i][3 * rc :, :] = low


def collect_kernel(n, nd, wide, *refs):
    blocks, outs, held = refs[: -nd - 1], refs[-nd - 1 : -1], refs[-1]
    place, col, share = places(n, -1), lax.axis_index("dp"), n // nd
    cw = blocks[0].shape[1]
    for c in range(len(blocks) // n):
        for i in range(n):
            part = blocks[c * n + i][...].astype(F32)
            cols = pl.ds(pl.multiple_of(lax.rem(place[i], share) * wide + c * cw, HEAD_DIM), cw)
            for t in range(KINDS):
                held[lax.div(place[i], share), t, :, cols] = part[t * POOL : (t + 1) * POOL]
    for k in range(nd):
        outs[k][...] = held[lax.rem(col + k, nd)]


def spread_kernel(n, nd, wide, weight, *refs):
    blocks, out = refs[:-1], refs[-1]
    place, col, share = places(n, -1), lax.axis_index("dp"), n // nd
    rc = out.shape[0] // POOL
    cw = blocks[0].shape[1]
    sel = interleave_matrix(rc * POOL)
    for c in range(len(blocks) // n):
        for i in range(n):
            ref = blocks[c * n + i]
            cols = pl.ds(pl.multiple_of(place[i] * wide + c * cw, HEAD_DIM), cw)
            w = weight[
                lax.rem(col - lax.div(place[i], share) + nd, nd),
                :,
                pl.ds(pl.multiple_of(lax.rem(place[i], share) * wide + c * cw, HEAD_DIM), cw),
            ]
            parts = [ref[t * rc : (t + 1) * rc, :].astype(F32) for t in range(3)]
            made = []
            for j in range(POOL):
                total = parts[0] * w[j][None, :]
                for t in range(1, 3):
                    total = total + parts[t] * w[t * POOL + j][None, :]
                made.append(total.astype(BF16))
            out[:, cols] = dot(sel, jnp.concatenate(made, 0), 0, 0).astype(BF16)


def per_device(n, nd, block_input, cotangent, pool_weight):
    inputs = block_input[0]
    upstream = cotangent[0]
    rows, width = inputs.shape
    wide = width // n
    rc = rows // POOL
    length = rc * n
    heads = wide // HEAD_DIM
    chunks = CHUNKS if heads % CHUNKS == 0 else 1
    cw = wide // chunks
    todo = messages(n)
    shape = jax.ShapeDtypeStruct

    arrived = []
    for c in range(chunks):
        cut = pl.pallas_call(
            functools.partial(cut_kernel, n, wide, c * cw),
            out_shape=[shape((2 * rows, cw), BF16)] * n,
            in_specs=[ANY, ANY],
            out_specs=[VMEM] * n,
            scratch_shapes=[pltpu.SemaphoreType.DMA((2 * n,))],
        )(inputs, upstream)
        arrived.append([cut[0]] + [send(b, n, m) for b, m in zip(cut[1:], todo)])
    own = pool_weight.reshape(KINDS * POOL, -1)
    pieces = [own] + [lax.ppermute(own, "dp", [(d, (d + k) % nd) for d in range(nd)]) for k in range(1, nd)]
    weights = jnp.stack(pieces)

    back = []
    for c in range(chunks):
        full = lambda kind: pltpu.VMEM((length, cw), kind)
        made = pl.pallas_call(
            functools.partial(block_kernel, n, nd, rc, wide, c * cw),
            out_shape=[shape((3 * rc + KINDS * POOL, cw), BF16)] * n,
            in_specs=[VMEM] * (1 + n),
            out_specs=[VMEM] * n,
            scratch_shapes=[full(BF16)] * 3
            + [pltpu.VMEM((POOL, length, cw), BF16)] * 2
            + [pltpu.VMEM((length + 8, cw), F32)] * 2
            + [full(F32)] * 3
            + [pltpu.VMEM((KINDS * POOL, cw), F32)],
        )(weights, *arrived[c])
        back += [made[0]] + [send(b, n, m) for b, m in zip(made[1:], todo)]

    tail = pl.BlockSpec((KINDS * POOL, cw), lambda i: (3 * rc // (KINDS * POOL), 0))
    owned = (KINDS, POOL, width // nd)
    part = pl.BlockSpec(owned, lambda i: (0, 0, 0))
    shares = pl.pallas_call(
        functools.partial(collect_kernel, n, nd, wide),
        out_shape=[shape(owned, F32)] * nd,
        grid=(1,),
        in_specs=[tail] * len(back),
        out_specs=[part] * nd,
        scratch_shapes=[pltpu.VMEM((nd,) + owned, F32)],
    )(*back)
    weight_grad = shares[0]
    for k in range(1, nd):
        weight_grad = weight_grad + lax.ppermute(shares[k], "dp", [(d, (d + k) % nd) for d in range(nd)])
    input_grad = pl.pallas_call(
        functools.partial(spread_kernel, n, nd, wide),
        out_shape=shape((rows, width), BF16),
        in_specs=[VMEM] * (1 + len(back)),
        out_specs=VMEM,
    )(weights, *back)
    return input_grad[None], weight_grad


def solution(mesh):
    n, nd = mesh.shape["seq"], mesh.shape["dp"]
    if n % 2 or n % nd:
        raise ValueError("unsupported mesh")
    placed = (P("dp", "seq", None), P("dp", "seq", None), P(None, None, "dp"))

    def whole_step(*arrays):
        return per_device(n, nd, *arrays)

    return jax.shard_map(
        whole_step,
        mesh=mesh,
        in_specs=placed,
        out_specs=(P("dp", "seq", None), P(None, None, "dp")),
        check_vma=False,
    )
```

profile of v0, /device:TPU:0, one launch (start us, length us, event | category | flops | bytes accessed | tf_op | source)
XLA Modules:
  0.0 93.8 jit_solution(17052866195938382636)
XLA Ops:
  0.6 0.9 reshape.7
  1.5 4.0 %collective-permute-start.2 = (f32[16,1024]{1,0:T(8,128)S(1)}, f32[16,1024]{1,0:T(8,128)S(1)}, u32[]{:S(2)}, u32[]{:S(2)}) collective-permute-start(f32[16,1024]{1,0:T(8,128)S(1)} %reshape.7), channel_id=1, source_target_pairs={{0,3},{1,0},{2,1},{3,2},{4,7},{5,4},{6,5},{7,6},{8,11},{9,8},{10,9... | collective-permute-start | bytes 196616 | tf_op jit(solution)/shard_map/ppermute | solution.py:236
  5.5 0.5 collective-permute-start.1
  6.0 2.3 %shard_map.50 = (bf16[256,256]{1,0:T(8,128)(2,1)}, bf16[256,256]{1,0:T(8,128)(2,1)}, bf16[256,256]{1,0:T(8,128)(2,1)}, bf16[256,256]{1,0:T(8,128)(2,1)}, bf16[25...) custom-call(bf16[128,4096]{1,0:T(8,128)(2,1)} %bitcast.11, ...), custom_call_target="tpu_custom_call" | custom-call | tf_op jit(solution)/shard_map/pallas_call | solution.py:227
  8.3 2.7 %collective-permute-start.3 = (bf16[256,256]{1,0:T(8,128)(2,1)}, bf16[256,256]{1,0:T(8,128)(2,1)S(1)}, u32[]{:S(2)}, u32[]{:S(2)}) collective-permute-start(bf16[256,256]{1,0:T(8,128)(2,1)} %get-tuple-element.39), channel_id=1, source_target_pairs={{0,16},{4,20},{8,24},{12,28},{16,0},{20,4},{24,8},{28,12},{1,17},{... | collective-permute-start | bytes 393224 | tf_op jit(solution)/shard_map/ppermute | solution.py:47
  11.0 1.6 %collective-permute-start.5 = (bf16[256,256]{1,0:T(8,128)(2,1)}, bf16[256,256]{1,0:T(8,128)(2,1)S(1)}, u32[]{:S(2)}, u32[]{:S(2)}) collective-permute-start(bf16[256,256]{1,0:T(8,128)(2,1)} %get-tuple-element.41), channel_id=1, source_target_pairs={{0,8},{4,12},{8,16},{12,20},{16,24},{20,28},{24,0},{28,4},{1,9},{5... | collective-permute-start | bytes 393224 | tf_op jit(solution)/shard_map/ppermute | solution.py:47
  12.6 0.0 copy-start
  12.6 1.4 %collective-permute-start.6 = (bf16[256,256]{1,0:T(8,128)(2,1)}, bf16[256,256]{1,0:T(8,128)(2,1)S(1)}, u32[]{:S(2)}, u32[]{:S(2)}) collective-permute-start(bf16[256,256]{1,0:T(8,128)(2,1)} %get-tuple-element.42), channel_id=1, source_target_pairs={{0,12},{4,8},{8,20},{12,16},{16,28},{20,24},{24,4},{28,0},{1,13},{... | collective-permute-start | bytes 393224 | tf_op jit(solution)/shard_map/ppermute | solution.py:47
  14.0 0.0 collective-permute-done.1
  14.0 0.6 collective-permute-start
  14.6 2.4 %shard_map.52 = (bf16[256,256]{1,0:T(8,128)(2,1)}, bf16[256,256]{1,0:T(8,128)(2,1)}, bf16[256,256]{1,0:T(8,128)(2,1)}, bf16[256,256]{1,0:T(8,128)(2,1)}, bf16[25...) custom-call(bf16[128,4096]{1,0:T(8,128)(2,1)} %bitcast.12, ...), custom_call_target="tpu_custom_call" | custom-call | tf_op jit(solution)/shard_map/pallas_call | solution.py:227
  17.0 2.2 %collective-permute-done = f32[16,1024]{1,0:T(8,128)S(1)} collective-permute-done((f32[16,1024]{1,0:T(8,128)S(1)}, f32[16,1024]{1,0:T(8,128)S(1)}, u32[]{:S(2)}, u32[]{:S(2)}) %collective-permute-start) | collective-permute-done | bytes 65568 | tf_op jit(solution)/shard_map/ppermute | solution.py:236
  19.2 2.3 %collective-permute-start.7 = (bf16[256,256]{1,0:T(8,128)(2,1)S(1)}, bf16[256,256]{1,0:T(8,128)(2,1)S(1)}, u32[]{:S(2)}, u32[]{:S(2)}) collective-permute-start(bf16[256,256]{1,0:T(8,128)(2,1)S(1)} %copy-done.33), channel_id=1, source_target_pairs={{0,24},{4,28},{8,0},{12,4},{16,8},{20,12},{24,16},{28,20},{1,25},{... | collective-permute-start | bytes 393224 | tf_op jit(solution)/shard_map/ppermute | solution.py:47
  21.5 5.1 %collective-permute-done.3.refs_1_ = bf16[256,256]{1,0:T(8,128)(2,1)S(1)} collective-permute-done((bf16[256,256]{1,0:T(8,128)(2,1)}, bf16[256,256]{1,0:T(8,128)(2,1)S(1)}, u32[]{:S(2)}, u32[]{:S(2)}) %collective-permute-start.3) | collective-permute-done | bytes 131104 | tf_op jit(solution)/shard_map/ppermute | solution.py:47
  26.6 0.0 collective-permute-start.8
  26.6 0.6 collective-permute-done.4.refs_2_
  27.2 2.0 %collective-permute-start.9 = (bf16[256,256]{1,0:T(8,128)(2,1)S(1)}, bf16[256,256]{1,0:T(8,128)(2,1)S(1)}, u32[]{:S(2)}, u32[]{:S(2)}) collective-permute-start(bf16[256,256]{1,0:T(8,128)(2,1)S(1)} %copy-done.31), channel_id=1, source_target_pairs={{0,4},{4,0},{8,12},{12,8},{16,20},{20,16},{24,28},{28,24},{1,5},{5... | collective-permute-start | bytes 393224 | tf_op jit(solution)/shard_map/ppermute | solution.py:47
  29.2 0.0 collective-permute-done.5.refs_3_
  29.2 4.6 %collective-permute-start.17 = (bf16[256,256]{1,0:T(8,128)(2,1)}, bf16[256,256]{1,0:T(8,128)(2,1)S(1)}, u32[]{:S(2)}, u32[]{:S(2)}) collective-permute-start(bf16[256,256]{1,0:T(8,128)(2,1)} %get-tuple-element.55), channel_id=1, source_target_pairs={{0,16},{4,20},{8,24},{12,28},{16,0},{20,4},{24,8},{28,12},{1,17},{... | collective-permute-start | bytes 393224 | tf_op jit(solution)/shard_map/ppermute | solution.py:47
  33.8 2.3 %collective-permute-start.18 = (bf16[256,256]{1,0:T(8,128)(2,1)}, bf16[256,256]{1,0:T(8,128)(2,1)S(1)}, u32[]{:S(2)}, u32[]{:S(2)}) collective-permute-start(bf16[256,256]{1,0:T(8,128)(2,1)} %get-tuple-element.56), channel_id=1, source_target_pairs={{0,20},{4,16},{8,28},{12,24},{16,4},{20,0},{24,12},{28,8},{1,21},{... | collective-permute-start | bytes 393224 | tf_op jit(solution)/shard_map/ppermute | solution.py:47
  36.1 0.0 collective-permute-done.7.refs_5_
  36.1 0.0 collective-permute-start.19
  36.1 0.6 collective-permute-start.20
  36.7 0.0 collective-permute-done.9.refs_7_
  36.7 3.3 %collective-permute-start.21 = (bf16[256,256]{1,0:T(8,128)(2,1)}, bf16[256,256]{1,0:T(8,128)(2,1)S(1)}, u32[]{:S(2)}, u32[]{:S(2)}) collective-permute-start(bf16[256,256]{1,0:T(8,128)(2,1)} %get-tuple-element.59), channel_id=1, source_target_pairs={{0,24},{4,28},{8,0},{12,4},{16,8},{20,12},{24,16},{28,20},{1,25},{... | collective-permute-start | bytes 393224 | tf_op jit(solution)/shard_map/ppermute | solution.py:47
  40.0 9.2 %collective-permute-done.17.refs_1_ = bf16[256,256]{1,0:T(8,128)(2,1)S(1)} collective-permute-done((bf16[256,256]{1,0:T(8,128)(2,1)}, bf16[256,256]{1,0:T(8,128)(2,1)S(1)}, u32[]{:S(2)}, u32[]{:S(2)}) %collective-permute-start.17) | collective-permute-done | bytes 131104 | tf_op jit(solution)/shard_map/ppermute | solution.py:47
  49.3 0.0 collective-permute-start.22
  49.3 2.0 %collective-permute-done.18.refs_2_ = bf16[256,256]{1,0:T(8,128)(2,1)S(1)} collective-permute-done((bf16[256,256]{1,0:T(8,128)(2,1)}, bf16[256,256]{1,0:T(8,128)(2,1)S(1)}, u32[]{:S(2)}, u32[]{:S(2)}) %collective-permute-start.18) | collective-permute-done | bytes 131104 | tf_op jit(solution)/shard_map/ppermute | solution.py:47
  51.3 0.5 collective-permute-start.23
  51.8 0.7 pad_maximum_fusion.weight
  52.6 4.4 %shard_map.51 = (bf16[112,256]{1,0:T(8,128)(2,1)}, bf16[112,256]{1,0:T(8,128)(2,1)}, bf16[112,256]{1,0:T(8,128)(2,1)}, bf16[112,256]{1,0:T(8,128)(2,1)}, bf16[11...) custom-call(f32[4,16,1024]{2,1,0:T(8,128)} %pad_maximum_fusion.weight, ...), custom_call_target="tpu_custom_call" | custom-call | tf_op jit(solution)/shard_map/pallas_call | solution.py:242
  57.0 0.0 copy-start.21
  57.0 0.1 collective-permute-start.10
  57.1 2.3 %collective-permute-start.11 = (bf16[112,256]{1,0:T(8,128)(2,1)}, bf16[112,256]{1,0:T(8,128)(2,1)S(1)}, u32[]{:S(2)}, u32[]{:S(2)}) collective-permute-start(bf16[112,256]{1,0:T(8,128)(2,1)} %get-tuple-element.48), channel_id=1, source_target_pairs={{0,20},{4,16},{8,28},{12,24},{16,4},{20,0},{24,12},{28,8},{1,21},{... | collective-permute-start | bytes 172040 | tf_op jit(solution)/shard_map/ppermute | solution.py:47
  59.4 0.0 collective-permute-done.22.refs_6_
  59.4 0.7 collective-permute-start.13
  60.1 0.0 collective-permute-done.23.refs_7_
  60.1 3.5 %collective-permute-start.14 = (bf16[112,256]{1,0:T(8,128)(2,1)}, bf16[112,256]{1,0:T(8,128)(2,1)S(1)}, u32[]{:S(2)}, u32[]{:S(2)}) collective-permute-start(bf16[112,256]{1,0:T(8,128)(2,1)} %get-tuple-element.51), channel_id=1, source_target_pairs={{0,24},{4,28},{8,0},{12,4},{16,8},{20,12},{24,16},{28,20},{1,25},{... | collective-permute-start | bytes 172040 | tf_op jit(solution)/shard_map/ppermute | solution.py:47
  63.7 4.4 %shard_map.53 = (bf16[112,256]{1,0:T(8,128)(2,1)}, bf16[112,256]{1,0:T(8,128)(2,1)}, bf16[112,256]{1,0:T(8,128)(2,1)}, bf16[112,256]{1,0:T(8,128)(2,1)}, bf16[11...) custom-call(f32[4,16,1024]{2,1,0:T(8,128)} %pad_maximum_fusion.weight, ...), custom_call_target="tpu_custom_call" | custom-call | tf_op jit(solution)/shard_map/pallas_call | solution.py:242
  68.1 1.1 %collective-permute-start.15 = (bf16[112,256]{1,0:T(8,128)(2,1)S(1)}, bf16[112,256]{1,0:T(8,128)(2,1)S(1)}, u32[]{:S(2)}, u32[]{:S(2)}) collective-permute-start(bf16[112,256]{1,0:T(8,128)(2,1)S(1)} %copy-done.35), channel_id=1, source_target_pairs={{0,28},{4,24},{8,4},{12,0},{16,12},{20,8},{24,20},{28,16},{1,29},{... | collective-permute-start | bytes 172040 | tf_op jit(solution)/shard_map/ppermute | solution.py:47
  69.2 0.0 collective-permute-done.11.refs_2_
  69.2 0.8 collective-permute-start.16
  70.0 0.0 collective-permute-done.12.refs_3_
  70.0 0.0 collective-permute-start.24
  70.1 2.3 %collective-permute-start.25 = (bf16[112,256]{1,0:T(8,128)(2,1)}, bf16[112,256]{1,0:T(8,128)(2,1)S(1)}, u32[]{:S(2)}, u32[]{:S(2)}) collective-permute-start(bf16[112,256]{1,0:T(8,128)(2,1)} %get-tuple-element.64), channel_id=1, source_target_pairs={{0,20},{4,16},{8,28},{12,24},{16,4},{20,0},{24,12},{28,8},{1,21},{... | collective-permute-start | bytes 172040 | tf_op jit(solution)/shard_map/ppermute | solution.py:47
  72.4 0.0 collective-permute-done.14.refs_5_
  72.4 0.3 collective-permute-start.26
  72.8 0.4 collective-permute-start.27
  73.1 3.5 %collective-permute-start.28 = (bf16[112,256]{1,0:T(8,128)(2,1)}, bf16[112,256]{1,0:T(8,128)(2,1)S(1)}, u32[]{:S(2)}, u32[]{:S(2)}) collective-permute-start(bf16[112,256]{1,0:T(8,128)(2,1)} %get-tuple-element.67), channel_id=1, source_target_pairs={{0,24},{4,28},{8,0},{12,4},{16,8},{20,12},{24,16},{28,20},{1,25},{... | collective-permute-start | bytes 172040 | tf_op jit(solution)/shard_map/ppermute | solution.py:47
  76.6 1.1 %collective-permute-done.24.refs_9_ = bf16[112,256]{1,0:T(8,128)(2,1)S(1)} collective-permute-done((bf16[112,256]{1,0:T(8,128)(2,1)}, bf16[112,256]{1,0:T(8,128)(2,1)S(1)}, u32[]{:S(2)}, u32[]{:S(2)}) %collective-permute-start.24) | collective-permute-done | bytes 57376 | tf_op jit(solution)/shard_map/ppermute | solution.py:47
  77.7 0.0 collective-permute-start.29
  77.7 3.1 %collective-permute-done.25.refs_10_ = bf16[112,256]{1,0:T(8,128)(2,1)S(1)} collective-permute-done((bf16[112,256]{1,0:T(8,128)(2,1)}, bf16[112,256]{1,0:T(8,128)(2,1)S(1)}, u32[]{:S(2)}, u32[]{:S(2)}) %collective-permute-start.25) | collective-permute-done | bytes 57376 | tf_op jit(solution)/shard_map/ppermute | solution.py:47
  80.8 0.3 collective-permute-start.30
  81.1 1.1 %collective-permute-done.28.refs_13_ = bf16[112,256]{1,0:T(8,128)(2,1)S(1)} collective-permute-done((bf16[112,256]{1,0:T(8,128)(2,1)}, bf16[112,256]{1,0:T(8,128)(2,1)S(1)}, u32[]{:S(2)}, u32[]{:S(2)}) %collective-permute-start.28) | collective-permute-done | bytes 57376 | tf_op jit(solution)/shard_map/ppermute | solution.py:47
  82.3 1.2 %collective-permute-done.29.refs_14_ = bf16[112,256]{1,0:T(8,128)(2,1)S(1)} collective-permute-done((bf16[112,256]{1,0:T(8,128)(2,1)}, bf16[112,256]{1,0:T(8,128)(2,1)S(1)}, u32[]{:S(2)}, u32[]{:S(2)}) %collective-permute-start.29) | collective-permute-done | bytes 57376 | tf_op jit(solution)/shard_map/ppermute | solution.py:47
  83.5 0.5 copy-done.13
  84.1 0.0 copy-done.14
  84.1 1.6 %shard_map.55 = (f32[4,4,1024]{2,1,0:T(4,128)}, f32[4,4,1024]{2,1,0:T(4,128)}, f32[4,4,1024]{2,1,0:T(4,128)}, f32[4,4,1024]{2,1,0:T(4,128)}) custom-call(bf16[112,256]{1,0:T(8,128)(2,1)} %get-tuple-element.46.refs_0_, bf16[112,256]{1,0:T(8,128)(2,1)} %copy-done.1, bf16[112,256]{1,0:T(8,128)(2,1)} %copy-done.2, bf16[112,256]{1,0:T(8,128)(2,1)} %copy-done.3, ...), custom_call_target="tpu_custom_call" | custom-call | tf_op jit(solution)/shard_map/pallas_call | solution.py:258
  85.7 0.6 collective-permute-start.33
  86.3 1.5 %collective-permute-start.32 = (f32[4,4,1024]{2,1,0:T(4,128)}, f32[4,4,1024]{2,1,0:T(4,128)S(1)}, u32[]{:S(2)}, u32[]{:S(2)}) collective-permute-start(f32[4,4,1024]{2,1,0:T(4,128)} %get-tuple-element.72), channel_id=1, source_target_pairs={{0,2},{1,3},{2,0},{3,1},{4,6},{5,7},{6,4},{7,5},{8,10},{9,11},{10,... | collective-permute-start | bytes 196616 | tf_op jit(solution)/shard_map/ppermute | solution.py:268
  87.8 1.5 %collective-permute-start.31 = (f32[4,4,1024]{2,1,0:T(4,128)}, f32[4,4,1024]{2,1,0:T(4,128)S(1)}, u32[]{:S(2)}, u32[]{:S(2)}) collective-permute-start(f32[4,4,1024]{2,1,0:T(4,128)} %get-tuple-element.71), channel_id=1, source_target_pairs={{0,1},{1,2},{2,3},{3,0},{4,5},{5,6},{6,7},{7,4},{8,9},{9,10},{10,1... | collective-permute-start | bytes 196616 | tf_op jit(solution)/shard_map/ppermute | solution.py:268
  89.3 3.0 %shard_map.54 = bf16[128,4096]{1,0:T(8,128)(2,1)} custom-call(f32[4,16,1024]{2,1,0:T(8,128)} %pad_maximum_fusion.weight, bf16[112,256]{1,0:T(8,128)(2,1)} %get-tuple-element.46.refs_0_, bf16[112,256]{1,0:T(8,128)(2,1)} %copy-done.1, bf16[112,256]{1,0:T(8,128)(2,1)} %copy-done.2, bf16[112,256]{1,0:T(8,128)(2,1)} %copy-done.3, bf16[112,256]{1,0:T(8,128)(2,1)} %copy-done.4, ...), custom_call_target="tpu_custom_call" | custom-call | tf_op jit(solution)/shard_map/pallas_call | solution.py:269
  92.3 0.8 collective-permute-done.31
  93.2 0.6 add_add_fusion
  (86 shorter events, 0.2 us)
Async XLA Ops:
  1.5 11.1 %collective-permute-start.2 = (f32[16,1024]{1,0:T(8,128)S(1)}, f32[16,1024]{1,0:T(8,128)S(1)}, u32[]{:S(2)}, u32[]{:S(2)}) collective-permute-start(f32[16,1024]{1,0:T(8,128)S(1)} %reshape.7), channel_id=1, source_target_pairs={{0,3},{1,0},{2,1},{3,2},{4,7},{5,4},{6,5},{7,6},{8,11},{9,8},{10,9... | collective-permute-start | bytes 196616 | tf_op jit(solution)/shard_map/ppermute | solution.py:236
  5.5 8.5 %collective-permute-start.1 = (f32[16,1024]{1,0:T(8,128)S(1)}, f32[16,1024]{1,0:T(8,128)S(1)}, u32[]{:S(2)}, u32[]{:S(2)}) collective-permute-start(f32[16,1024]{1,0:T(8,128)S(1)} %reshape.7), channel_id=1, source_target_pairs={{0,2},{1,3},{2,0},{3,1},{4,6},{5,7},{6,4},{7,5},{8,10},{9,11},{10,... | collective-permute-start | bytes 196616 | tf_op jit(solution)/shard_map/ppermute | solution.py:236
  8.3 18.3 %collective-permute-start.3 = (bf16[256,256]{1,0:T(8,128)(2,1)}, bf16[256,256]{1,0:T(8,128)(2,1)S(1)}, u32[]{:S(2)}, u32[]{:S(2)}) collective-permute-start(bf16[256,256]{1,0:T(8,128)(2,1)} %get-tuple-element.39), channel_id=1, source_target_pairs={{0,16},{4,20},{8,24},{12,28},{16,0},{20,4},{24,8},{28,12},{1,17},{... | collective-permute-start | bytes 393224 | tf_op jit(solution)/shard_map/ppermute | solution.py:47
  11.0 16.2 %collective-permute-start.4 = (bf16[256,256]{1,0:T(8,128)(2,1)}, bf16[256,256]{1,0:T(8,128)(2,1)S(1)}, u32[]{:S(2)}, u32[]{:S(2)}) collective-permute-start(bf16[256,256]{1,0:T(8,128)(2,1)} %get-tuple-element.40), channel_id=1, source_target_pairs={{0,20},{4,16},{8,28},{12,24},{16,4},{20,0},{24,12},{28,8},{1,21},{... | collective-permute-start | bytes 393224 | tf_op jit(solution)/shard_map/ppermute | solution.py:47
  11.0 18.2 %collective-permute-start.5 = (bf16[256,256]{1,0:T(8,128)(2,1)}, bf16[256,256]{1,0:T(8,128)(2,1)S(1)}, u32[]{:S(2)}, u32[]{:S(2)}) collective-permute-start(bf16[256,256]{1,0:T(8,128)(2,1)} %get-tuple-element.41), channel_id=1, source_target_pairs={{0,8},{4,12},{8,16},{12,20},{16,24},{20,28},{24,0},{28,4},{1,9},{5... | collective-permute-start | bytes 393224 | tf_op jit(solution)/shard_map/ppermute | solution.py:47
  12.6 6.6 %copy-start.33 = (bf16[256,256]{1,0:T(8,128)(2,1)S(1)}, bf16[256,256]{1,0:T(8,128)(2,1)}, u32[]{:S(2)}) copy-start(bf16[256,256]{1,0:T(8,128)(2,1)} %get-tuple-element.43) | copy-start | bytes 393220
  12.6 14.1 %copy-start.32 = (bf16[256,256]{1,0:T(8,128)(2,1)S(1)}, bf16[256,256]{1,0:T(8,128)(2,1)}, u32[]{:S(2)}) copy-start(bf16[256,256]{1,0:T(8,128)(2,1)} %get-tuple-element.44) | copy-start | bytes 393220
  12.6 14.6 %copy-start.31 = (bf16[256,256]{1,0:T(8,128)(2,1)S(1)}, bf16[256,256]{1,0:T(8,128)(2,1)}, u32[]{:S(2)}) copy-start(bf16[256,256]{1,0:T(8,128)(2,1)} %get-tuple-element.45) | copy-start | bytes 393220
  12.6 36.7 %copy-start = (f32[4,4,1024]{2,1,0:T(4,128)S(1)}, f32[4,4,1024]{2,1,0:T(4,128)}, u32[]{:S(2)}) copy-start(f32[4,4,1024]{2,1,0:T(4,128)} %param.5) | copy-start | bytes 196612
  12.6 21.2 %collective-permute-start.6 = (bf16[256,256]{1,0:T(8,128)(2,1)}, bf16[256,256]{1,0:T(8,128)(2,1)S(1)}, u32[]{:S(2)}, u32[]{:S(2)}) collective-permute-start(bf16[256,256]{1,0:T(8,128)(2,1)} %get-tuple-element.42), channel_id=1, source_target_pairs={{0,12},{4,8},{8,20},{12,16},{16,28},{20,24},{24,4},{28,0},{1,13},{... | collective-permute-start | bytes 393224 | tf_op jit(solution)/shard_map/ppermute | solution.py:47
  14.0 5.2 %collective-permute-start = (f32[16,1024]{1,0:T(8,128)S(1)}, f32[16,1024]{1,0:T(8,128)S(1)}, u32[]{:S(2)}, u32[]{:S(2)}) collective-permute-start(f32[16,1024]{1,0:T(8,128)S(1)} %reshape.7), channel_id=1, source_target_pairs={{0,1},{1,2},{2,3},{3,0},{4,5},{5,6},{6,7},{7,4},{8,9},{9,10},{10,1... | collective-permute-start | bytes 196616 | tf_op jit(solution)/shard_map/ppermute | solution.py:236
  17.0 34.4 %copy-start.30 = (bf16[256,256]{1,0:T(8,128)(2,1)S(1)}, bf16[256,256]{1,0:T(8,128)(2,1)}, u32[]{:S(2)}) copy-start(bf16[256,256]{1,0:T(8,128)(2,1)} %get-tuple-element.61) | copy-start | bytes 393220
  19.2 16.9 %collective-permute-start.7 = (bf16[256,256]{1,0:T(8,128)(2,1)S(1)}, bf16[256,256]{1,0:T(8,128)(2,1)S(1)}, u32[]{:S(2)}, u32[]{:S(2)}) collective-permute-start(bf16[256,256]{1,0:T(8,128)(2,1)S(1)} %copy-done.33), channel_id=1, source_target_pairs={{0,24},{4,28},{8,0},{12,4},{16,8},{20,12},{24,16},{28,20},{1,25},{... | collective-permute-start | bytes 393224 | tf_op jit(solution)/shard_map/ppermute | solution.py:47
  26.6 25.9 %copy-start.15 = (bf16[256,256]{1,0:T(8,128)(2,1)}, bf16[256,256]{1,0:T(8,128)(2,1)S(1)}, u32[]{:S(2)}) copy-start(bf16[256,256]{1,0:T(8,128)(2,1)S(1)} %collective-permute-done.3.refs_1_) | copy-start | bytes 393220
  26.6 9.5 %collective-permute-start.8 = (bf16[256,256]{1,0:T(8,128)(2,1)S(1)}, bf16[256,256]{1,0:T(8,128)(2,1)S(1)}, u32[]{:S(2)}, u32[]{:S(2)}) collective-permute-start(bf16[256,256]{1,0:T(8,128)(2,1)S(1)} %copy-done.32), channel_id=1, source_target_pairs={{0,28},{4,24},{8,4},{12,0},{16,12},{20,8},{24,20},{28,16},{1,29},{... | collective-permute-start | bytes 393224 | tf_op jit(solution)/shard_map/ppermute | solution.py:47
  27.2 25.4 %copy-start.16 = (bf16[256,256]{1,0:T(8,128)(2,1)}, bf16[256,256]{1,0:T(8,128)(2,1)S(1)}, u32[]{:S(2)}) copy-start(bf16[256,256]{1,0:T(8,128)(2,1)S(1)} %collective-permute-done.4.refs_2_) | copy-start | bytes 393220
  27.2 9.5 %collective-permute-start.9 = (bf16[256,256]{1,0:T(8,128)(2,1)S(1)}, bf16[256,256]{1,0:T(8,128)(2,1)S(1)}, u32[]{:S(2)}, u32[]{:S(2)}) collective-permute-start(bf16[256,256]{1,0:T(8,128)(2,1)S(1)} %copy-done.31), channel_id=1, source_target_pairs={{0,4},{4,0},{8,12},{12,8},{16,20},{20,16},{24,28},{28,24},{1,5},{5... | collective-permute-start | bytes 393224 | tf_op jit(solution)/shard_map/ppermute | solution.py:47
  29.2 23.4 %copy-start.18 = (bf16[256,256]{1,0:T(8,128)(2,1)}, bf16[256,256]{1,0:T(8,128)(2,1)S(1)}, u32[]{:S(2)}) copy-start(bf16[256,256]{1,0:T(8,128)(2,1)S(1)} %collective-permute-done.5.refs_3_) | copy-start | bytes 393220
  29.2 20.1 %collective-permute-start.17 = (bf16[256,256]{1,0:T(8,128)(2,1)}, bf16[256,256]{1,0:T(8,128)(2,1)S(1)}, u32[]{:S(2)}, u32[]{:S(2)}) collective-permute-start(bf16[256,256]{1,0:T(8,128)(2,1)} %get-tuple-element.55), channel_id=1, source_target_pairs={{0,16},{4,20},{8,24},{12,28},{16,0},{20,4},{24,8},{28,12},{1,17},{... | collective-permute-start | bytes 393224 | tf_op jit(solution)/shard_map/ppermute | solution.py:47
  33.8 18.8 %copy-start.19 = (bf16[256,256]{1,0:T(8,128)(2,1)}, bf16[256,256]{1,0:T(8,128)(2,1)S(1)}, u32[]{:S(2)}) copy-start(bf16[256,256]{1,0:T(8,128)(2,1)S(1)} %collective-permute-done.6.refs_4_) | copy-start | bytes 393220
  33.8 17.6 %collective-permute-start.18 = (bf16[256,256]{1,0:T(8,128)(2,1)}, bf16[256,256]{1,0:T(8,128)(2,1)S(1)}, u32[]{:S(2)}, u32[]{:S(2)}) collective-permute-start(bf16[256,256]{1,0:T(8,128)(2,1)} %get-tuple-element.56), channel_id=1, source_target_pairs={{0,20},{4,16},{8,28},{12,24},{16,4},{20,0},{24,12},{28,8},{1,21},{... | collective-permute-start | bytes 393224 | tf_op jit(solution)/shard_map/ppermute | solution.py:47
  36.1 16.5 %copy-start.24 = (bf16[256,256]{1,0:T(8,128)(2,1)}, bf16[256,256]{1,0:T(8,128)(2,1)S(1)}, u32[]{:S(2)}) copy-start(bf16[256,256]{1,0:T(8,128)(2,1)S(1)} %collective-permute-done.7.refs_5_) | copy-start | bytes 393220
  36.1 20.9 %collective-permute-start.19 = (bf16[256,256]{1,0:T(8,128)(2,1)}, bf16[256,256]{1,0:T(8,128)(2,1)S(1)}, u32[]{:S(2)}, u32[]{:S(2)}) collective-permute-start(bf16[256,256]{1,0:T(8,128)(2,1)} %get-tuple-element.57), channel_id=1, source_target_pairs={{0,8},{4,12},{8,16},{12,20},{16,24},{20,28},{24,0},{28,4},{1,9},{5... | collective-permute-start | bytes 393224 | tf_op jit(solution)/shard_map/ppermute | solution.py:47
  36.1 16.5 %copy-start.26 = (bf16[256,256]{1,0:T(8,128)(2,1)}, bf16[256,256]{1,0:T(8,128)(2,1)S(1)}, u32[]{:S(2)}) copy-start(bf16[256,256]{1,0:T(8,128)(2,1)S(1)} %collective-permute-done.8.refs_6_) | copy-start | bytes 393220
  36.1 20.9 %collective-permute-start.20 = (bf16[256,256]{1,0:T(8,128)(2,1)}, bf16[256,256]{1,0:T(8,128)(2,1)S(1)}, u32[]{:S(2)}, u32[]{:S(2)}) collective-permute-start(bf16[256,256]{1,0:T(8,128)(2,1)} %get-tuple-element.58), channel_id=1, source_target_pairs={{0,12},{4,8},{8,20},{12,16},{16,28},{20,24},{24,4},{28,0},{1,13},{... | collective-permute-start | bytes 393224 | tf_op jit(solution)/shard_map/ppermute | solution.py:47
  36.7 15.9 %copy-start.28 = (bf16[256,256]{1,0:T(8,128)(2,1)}, bf16[256,256]{1,0:T(8,128)(2,1)S(1)}, u32[]{:S(2)}) copy-start(bf16[256,256]{1,0:T(8,128)(2,1)S(1)} %collective-permute-done.9.refs_7_) | copy-start | bytes 393220
  36.7 22.6 %collective-permute-start.21 = (bf16[256,256]{1,0:T(8,128)(2,1)}, bf16[256,256]{1,0:T(8,128)(2,1)S(1)}, u32[]{:S(2)}, u32[]{:S(2)}) collective-permute-start(bf16[256,256]{1,0:T(8,128)(2,1)} %get-tuple-element.59), channel_id=1, source_target_pairs={{0,24},{4,28},{8,0},{12,4},{16,8},{20,12},{24,16},{28,20},{1,25},{... | collective-permute-start | bytes 393224 | tf_op jit(solution)/shard_map/ppermute | solution.py:47
  49.3 3.3 %copy-start.17 = (bf16[256,256]{1,0:T(8,128)(2,1)}, bf16[256,256]{1,0:T(8,128)(2,1)S(1)}, u32[]{:S(2)}) copy-start(bf16[256,256]{1,0:T(8,128)(2,1)S(1)} %collective-permute-done.17.refs_1_) | copy-start | bytes 393220
  49.3 10.1 %collective-permute-start.22 = (bf16[256,256]{1,0:T(8,128)(2,1)}, bf16[256,256]{1,0:T(8,128)(2,1)S(1)}, u32[]{:S(2)}, u32[]{:S(2)}) collective-permute-start(bf16[256,256]{1,0:T(8,128)(2,1)} %get-tuple-element.60), channel_id=1, source_target_pairs={{0,28},{4,24},{8,4},{12,0},{16,12},{20,8},{24,20},{28,16},{1,29},{... | collective-permute-start | bytes 393224 | tf_op jit(solution)/shard_map/ppermute | solution.py:47
  51.3 5.6 %copy-start.20 = (bf16[256,256]{1,0:T(8,128)(2,1)}, bf16[256,256]{1,0:T(8,128)(2,1)S(1)}, u32[]{:S(2)}) copy-start(bf16[256,256]{1,0:T(8,128)(2,1)S(1)} %collective-permute-done.18.refs_2_) | copy-start | bytes 393220
  51.3 8.8 %collective-permute-start.23 = (bf16[256,256]{1,0:T(8,128)(2,1)S(1)}, bf16[256,256]{1,0:T(8,128)(2,1)S(1)}, u32[]{:S(2)}, u32[]{:S(2)}) collective-permute-start(bf16[256,256]{1,0:T(8,128)(2,1)S(1)} %copy-done.30), channel_id=1, source_target_pairs={{0,4},{4,0},{8,12},{12,8},{16,20},{20,16},{24,28},{28,24},{1,5},{5... | collective-permute-start | bytes 393224 | tf_op jit(solution)/shard_map/ppermute | solution.py:47
  57.0 6.6 %copy-start.21 = (bf16[256,256]{1,0:T(8,128)(2,1)}, bf16[256,256]{1,0:T(8,128)(2,1)S(1)}, u32[]{:S(2)}) copy-start(bf16[256,256]{1,0:T(8,128)(2,1)S(1)} %collective-permute-done.19.refs_3_) | copy-start | bytes 393220
  57.0 11.1 %collective-permute-start.10 = (bf16[112,256]{1,0:T(8,128)(2,1)}, bf16[112,256]{1,0:T(8,128)(2,1)S(1)}, u32[]{:S(2)}, u32[]{:S(2)}) collective-permute-start(bf16[112,256]{1,0:T(8,128)(2,1)} %get-tuple-element.47), channel_id=1, source_target_pairs={{0,16},{4,20},{8,24},{12,28},{16,0},{20,4},{24,8},{28,12},{1,17},{... | collective-permute-start | bytes 172040 | tf_op jit(solution)/shard_map/ppermute | solution.py:47
  57.1 6.5 %copy-start.22 = (bf16[256,256]{1,0:T(8,128)(2,1)}, bf16[256,256]{1,0:T(8,128)(2,1)S(1)}, u32[]{:S(2)}) copy-start(bf16[256,256]{1,0:T(8,128)(2,1)S(1)} %collective-permute-done.20.refs_4_) | copy-start | bytes 393220
  57.1 12.1 %collective-permute-start.11 = (bf16[112,256]{1,0:T(8,128)(2,1)}, bf16[112,256]{1,0:T(8,128)(2,1)S(1)}, u32[]{:S(2)}, u32[]{:S(2)}) collective-permute-start(bf16[112,256]{1,0:T(8,128)(2,1)} %get-tuple-element.48), channel_id=1, source_target_pairs={{0,20},{4,16},{8,28},{12,24},{16,4},{20,0},{24,12},{28,8},{1,21},{... | collective-permute-start | bytes 172040 | tf_op jit(solution)/shard_map/ppermute | solution.py:47
  59.4 4.3 %copy-start.23 = (bf16[256,256]{1,0:T(8,128)(2,1)}, bf16[256,256]{1,0:T(8,128)(2,1)S(1)}, u32[]{:S(2)}) copy-start(bf16[256,256]{1,0:T(8,128)(2,1)S(1)} %collective-permute-done.21.refs_5_) | copy-start | bytes 393220
  59.4 10.7 %collective-permute-start.12 = (bf16[112,256]{1,0:T(8,128)(2,1)}, bf16[112,256]{1,0:T(8,128)(2,1)S(1)}, u32[]{:S(2)}, u32[]{:S(2)}) collective-permute-start(bf16[112,256]{1,0:T(8,128)(2,1)} %get-tuple-element.49), channel_id=1, source_target_pairs={{0,8},{4,12},{8,16},{12,20},{16,24},{20,28},{24,0},{28,4},{1,9},{5... | collective-permute-start | bytes 172040 | tf_op jit(solution)/shard_map/ppermute | solution.py:47
  59.4 4.3 %copy-start.25 = (bf16[256,256]{1,0:T(8,128)(2,1)}, bf16[256,256]{1,0:T(8,128)(2,1)S(1)}, u32[]{:S(2)}) copy-start(bf16[256,256]{1,0:T(8,128)(2,1)S(1)} %collective-permute-done.22.refs_6_) | copy-start | bytes 393220
  59.4 10.7 %collective-permute-start.13 = (bf16[112,256]{1,0:T(8,128)(2,1)}, bf16[112,256]{1,0:T(8,128)(2,1)S(1)}, u32[]{:S(2)}, u32[]{:S(2)}) collective-permute-start(bf16[112,256]{1,0:T(8,128)(2,1)} %get-tuple-element.50), channel_id=1, source_target_pairs={{0,12},{4,8},{8,20},{12,16},{16,28},{20,24},{24,4},{28,0},{1,13},{... | collective-permute-start | bytes 172040 | tf_op jit(solution)/shard_map/ppermute | solution.py:47
  60.1 3.5 %copy-start.27 = (bf16[256,256]{1,0:T(8,128)(2,1)}, bf16[256,256]{1,0:T(8,128)(2,1)S(1)}, u32[]{:S(2)}) copy-start(bf16[256,256]{1,0:T(8,128)(2,1)S(1)} %collective-permute-done.23.refs_7_) | copy-start | bytes 393220
  60.1 12.3 %collective-permute-start.14 = (bf16[112,256]{1,0:T(8,128)(2,1)}, bf16[112,256]{1,0:T(8,128)(2,1)S(1)}, u32[]{:S(2)}, u32[]{:S(2)}) collective-permute-start(bf16[112,256]{1,0:T(8,128)(2,1)} %get-tuple-element.51), channel_id=1, source_target_pairs={{0,24},{4,28},{8,0},{12,4},{16,8},{20,12},{24,16},{28,20},{1,25},{... | collective-permute-start | bytes 172040 | tf_op jit(solution)/shard_map/ppermute | solution.py:47
  63.7 4.5 %copy-start.35 = (bf16[112,256]{1,0:T(8,128)(2,1)S(1)}, bf16[112,256]{1,0:T(8,128)(2,1)}, u32[]{:S(2)}) copy-start(bf16[112,256]{1,0:T(8,128)(2,1)} %get-tuple-element.52) | copy-start | bytes 172036
  63.7 5.5 %copy-start.34 = (bf16[112,256]{1,0:T(8,128)(2,1)S(1)}, bf16[112,256]{1,0:T(8,128)(2,1)}, u32[]{:S(2)}) copy-start(bf16[112,256]{1,0:T(8,128)(2,1)} %get-tuple-element.53) | copy-start | bytes 172036
  68.1 15.3 %copy-start.1 = (bf16[112,256]{1,0:T(8,128)(2,1)}, bf16[112,256]{1,0:T(8,128)(2,1)S(1)}, u32[]{:S(2)}) copy-start(bf16[112,256]{1,0:T(8,128)(2,1)S(1)} %collective-permute-done.10.refs_1_) | copy-start | bytes 172036
  68.1 4.6 %collective-permute-start.15 = (bf16[112,256]{1,0:T(8,128)(2,1)S(1)}, bf16[112,256]{1,0:T(8,128)(2,1)S(1)}, u32[]{:S(2)}, u32[]{:S(2)}) collective-permute-start(bf16[112,256]{1,0:T(8,128)(2,1)S(1)} %copy-done.35), channel_id=1, source_target_pairs={{0,28},{4,24},{8,4},{12,0},{16,12},{20,8},{24,20},{28,16},{1,29},{... | collective-permute-start | bytes 172040 | tf_op jit(solution)/shard_map/ppermute | solution.py:47
  69.2 14.2 %copy-start.2 = (bf16[112,256]{1,0:T(8,128)(2,1)}, bf16[112,256]{1,0:T(8,128)(2,1)S(1)}, u32[]{:S(2)}) copy-start(bf16[112,256]{1,0:T(8,128)(2,1)S(1)} %collective-permute-done.11.refs_2_) | copy-start | bytes 172036
  69.2 3.9 %collective-permute-start.16 = (bf16[112,256]{1,0:T(8,128)(2,1)S(1)}, bf16[112,256]{1,0:T(8,128)(2,1)S(1)}, u32[]{:S(2)}, u32[]{:S(2)}) collective-permute-start(bf16[112,256]{1,0:T(8,128)(2,1)S(1)} %copy-done.34), channel_id=1, source_target_pairs={{0,4},{4,0},{8,12},{12,8},{16,20},{20,16},{24,28},{28,24},{1,5},{5... | collective-permute-start | bytes 172040 | tf_op jit(solution)/shard_map/ppermute | solution.py:47
  70.0 13.4 %copy-start.3 = (bf16[112,256]{1,0:T(8,128)(2,1)}, bf16[112,256]{1,0:T(8,128)(2,1)S(1)}, u32[]{:S(2)}) copy-start(bf16[112,256]{1,0:T(8,128)(2,1)S(1)} %collective-permute-done.12.refs_3_) | copy-start | bytes 172036
  70.0 7.6 %collective-permute-start.24 = (bf16[112,256]{1,0:T(8,128)(2,1)}, bf16[112,256]{1,0:T(8,128)(2,1)S(1)}, u32[]{:S(2)}, u32[]{:S(2)}) collective-permute-start(bf16[112,256]{1,0:T(8,128)(2,1)} %get-tuple-element.63), channel_id=1, source_target_pairs={{0,16},{4,20},{8,24},{12,28},{16,0},{20,4},{24,8},{28,12},{1,17},{... | collective-permute-start | bytes 172040 | tf_op jit(solution)/shard_map/ppermute | solution.py:47
  70.1 13.4 %copy-start.4 = (bf16[112,256]{1,0:T(8,128)(2,1)}, bf16[112,256]{1,0:T(8,128)(2,1)S(1)}, u32[]{:S(2)}) copy-start(bf16[112,256]{1,0:T(8,128)(2,1)S(1)} %collective-permute-done.13.refs_4_) | copy-start | bytes 172036
  70.1 10.8 %collective-permute-start.25 = (bf16[112,256]{1,0:T(8,128)(2,1)}, bf16[112,256]{1,0:T(8,128)(2,1)S(1)}, u32[]{:S(2)}, u32[]{:S(2)}) collective-permute-start(bf16[112,256]{1,0:T(8,128)(2,1)} %get-tuple-element.64), channel_id=1, source_target_pairs={{0,20},{4,16},{8,28},{12,24},{16,4},{20,0},{24,12},{28,8},{1,21},{... | collective-permute-start | bytes 172040 | tf_op jit(solution)/shard_map/ppermute | solution.py:47
  72.4 11.1 %copy-start.5 = (bf16[112,256]{1,0:T(8,128)(2,1)}, bf16[112,256]{1,0:T(8,128)(2,1)S(1)}, u32[]{:S(2)}) copy-start(bf16[112,256]{1,0:T(8,128)(2,1)S(1)} %collective-permute-done.14.refs_5_) | copy-start | bytes 172036
  72.4 8.7 %collective-permute-start.26 = (bf16[112,256]{1,0:T(8,128)(2,1)}, bf16[112,256]{1,0:T(8,128)(2,1)S(1)}, u32[]{:S(2)}, u32[]{:S(2)}) collective-permute-start(bf16[112,256]{1,0:T(8,128)(2,1)} %get-tuple-element.65), channel_id=1, source_target_pairs={{0,8},{4,12},{8,16},{12,20},{16,24},{20,28},{24,0},{28,4},{1,9},{5... | collective-permute-start | bytes 172040 | tf_op jit(solution)/shard_map/ppermute | solution.py:47
  72.8 10.7 %copy-start.6 = (bf16[112,256]{1,0:T(8,128)(2,1)}, bf16[112,256]{1,0:T(8,128)(2,1)S(1)}, u32[]{:S(2)}) copy-start(bf16[112,256]{1,0:T(8,128)(2,1)S(1)} %collective-permute-done.15.refs_6_) | copy-start | bytes 172036
  72.8 8.4 %collective-permute-start.27 = (bf16[112,256]{1,0:T(8,128)(2,1)}, bf16[112,256]{1,0:T(8,128)(2,1)S(1)}, u32[]{:S(2)}, u32[]{:S(2)}) collective-permute-start(bf16[112,256]{1,0:T(8,128)(2,1)} %get-tuple-element.66), channel_id=1, source_target_pairs={{0,12},{4,8},{8,20},{12,16},{16,28},{20,24},{24,4},{28,0},{1,13},{... | collective-permute-start | bytes 172040 | tf_op jit(solution)/shard_map/ppermute | solution.py:47
  73.1 10.4 %copy-start.7 = (bf16[112,256]{1,0:T(8,128)(2,1)}, bf16[112,256]{1,0:T(8,128)(2,1)S(1)}, u32[]{:S(2)}) copy-start(bf16[112,256]{1,0:T(8,128)(2,1)S(1)} %collective-permute-done.16.refs_7_) | copy-start | bytes 172036
  73.1 9.1 %collective-permute-start.28 = (bf16[112,256]{1,0:T(8,128)(2,1)}, bf16[112,256]{1,0:T(8,128)(2,1)S(1)}, u32[]{:S(2)}, u32[]{:S(2)}) collective-permute-start(bf16[112,256]{1,0:T(8,128)(2,1)} %get-tuple-element.67), channel_id=1, source_target_pairs={{0,24},{4,28},{8,0},{12,4},{16,8},{20,12},{24,16},{28,20},{1,25},{... | collective-permute-start | bytes 172040 | tf_op jit(solution)/shard_map/ppermute | solution.py:47
  77.7 5.8 %copy-start.8 = (bf16[112,256]{1,0:T(8,128)(2,1)}, bf16[112,256]{1,0:T(8,128)(2,1)S(1)}, u32[]{:S(2)}) copy-start(bf16[112,256]{1,0:T(8,128)(2,1)S(1)} %collective-permute-done.24.refs_9_) | copy-start | bytes 172036
  77.7 5.8 %collective-permute-start.29 = (bf16[112,256]{1,0:T(8,128)(2,1)}, bf16[112,256]{1,0:T(8,128)(2,1)S(1)}, u32[]{:S(2)}, u32[]{:S(2)}) collective-permute-start(bf16[112,256]{1,0:T(8,128)(2,1)} %get-tuple-element.68), channel_id=1, source_target_pairs={{0,28},{4,24},{8,4},{12,0},{16,12},{20,8},{24,20},{28,16},{1,29},{... | collective-permute-start | bytes 172040 | tf_op jit(solution)/shard_map/ppermute | solution.py:47
  80.8 2.6 %collective-permute-start.30 = (bf16[112,256]{1,0:T(8,128)(2,1)}, bf16[112,256]{1,0:T(8,128)(2,1)S(1)}, u32[]{:S(2)}, u32[]{:S(2)}) collective-permute-start(bf16[112,256]{1,0:T(8,128)(2,1)} %get-tuple-element.69), channel_id=1, source_target_pairs={{0,4},{4,0},{8,12},{12,8},{16,20},{20,16},{24,28},{28,24},{1,5},{5... | collective-permute-start | bytes 172040 | tf_op jit(solution)/shard_map/ppermute | solution.py:47
  85.7 6.6 %collective-permute-start.33 = (f32[4,4,1024]{2,1,0:T(4,128)}, f32[4,4,1024]{2,1,0:T(4,128)S(1)}, u32[]{:S(2)}, u32[]{:S(2)}) collective-permute-start(f32[4,4,1024]{2,1,0:T(4,128)} %get-tuple-element.73), channel_id=1, source_target_pairs={{0,3},{1,0},{2,1},{3,2},{4,7},{5,4},{6,5},{7,6},{8,11},{9,8},{10,9... | collective-permute-start | bytes 196616 | tf_op jit(solution)/shard_map/ppermute | solution.py:268
  86.3 6.1 %collective-permute-start.32 = (f32[4,4,1024]{2,1,0:T(4,128)}, f32[4,4,1024]{2,1,0:T(4,128)S(1)}, u32[]{:S(2)}, u32[]{:S(2)}) collective-permute-start(f32[4,4,1024]{2,1,0:T(4,128)} %get-tuple-element.72), channel_id=1, source_target_pairs={{0,2},{1,3},{2,0},{3,1},{4,6},{5,7},{6,4},{7,5},{8,10},{9,11},{10,... | collective-permute-start | bytes 196616 | tf_op jit(solution)/shard_map/ppermute | solution.py:268
  87.8 5.4 %copy-start.29 = (f32[4,4,1024]{2,1,0:T(4,128)S(1)}, f32[4,4,1024]{2,1,0:T(4,128)}, u32[]{:S(2)}) copy-start(f32[4,4,1024]{2,1,0:T(4,128)} %get-tuple-element.70) | copy-start | bytes 196612
  87.8 5.4 %collective-permute-start.31 = (f32[4,4,1024]{2,1,0:T(4,128)}, f32[4,4,1024]{2,1,0:T(4,128)S(1)}, u32[]{:S(2)}, u32[]{:S(2)}) collective-permute-start(f32[4,4,1024]{2,1,0:T(4,128)} %get-tuple-element.71), channel_id=1, source_target_pairs={{0,1},{1,2},{2,3},{3,0},{4,5},{5,6},{6,7},{7,4},{8,9},{9,10},{10,1... | collective-permute-start | bytes 196616 | tf_op jit(solution)/shard_map/ppermute | solution.py:268
  (6 other events, 10.0 us)
where the time goes:
time: 94.2 us; the launch traced here: 93.8 us
  starting transfers between devices  45.2 us (48%)
  waiting for transfers between devices  26.5 us (28%)
  Pallas kernels  18.2 us (19%)
  local copies, waits for them, and re-layouts  1.56 us (2%)
  other arithmetic  1.37 us (1%)
  between operations  1 us (1%)
    ppermute x28, starting transfers between devices, send(): return lax.ppermute(block, 'seq', pairs)  36.5 us
    ppermute x28, waiting for transfers between devices, send(): return lax.ppermute(block, 'seq', pairs)  23.5 us
    pallas_call x2, Pallas kernels, per_device(): pl.pallas_call(functools.partial(block_kernel, n, nd, rc, wide, c * cw),...  8.79 us
    ppermute x3, starting transfers between devices, per_device(): lax.ppermute(own, 'dp', [(d, (d + k) % nd) for d in range(nd)])  5.07 us
    pallas_call x2, Pallas kernels, per_device(): pl.pallas_call(functools.partial(cut_kernel, n, wide, c * cw), out_shape=...  4.74 us
    ppermute x3, starting transfers between devices, per_device(): lax.ppermute(shares[k], 'dp', [(d, (d + k) % nd) for d in range(nd)])  3.56 us
    pallas_call x1, Pallas kernels, per_device(): pl.pallas_call(functools.partial(spread_kernel, n, nd, wide), out_shape=s...  3.04 us
    ppermute x3, waiting for transfers between devices, per_device(): lax.ppermute(own, 'dp', [(d, (d + k) % nd) for d in range(nd)])  2.17 us
  transfers between devices with their start and end apart: 34, of which 10 were waited for; matrix products, arithmetic and copies ran while one was open for 1% of the time, Pallas kernels for 18%

commit v1 on v0

--- a/solution.py
+++ b/solution.py
@@ -11,7 +11,6 @@
 HEAD_DIM = 128
 POOL = 4
 KINDS = 4
-CHUNKS = 2
 BF16 = jnp.bfloat16
 F32 = jnp.float32
 
@@ -170,43 +169,58 @@
         outs[i][3 * rc :, :] = low
 
 
-def collect_kernel(n, nd, wide, *refs):
-    blocks, outs, held = refs[: -nd - 1], refs[-nd - 1 : -1], refs[-1]
+def collect_kernel(n, nd, *refs):
+    blocks, outs, held = refs[:n], refs[n : n + nd], refs[n + nd]
     place, col, share = places(n, -1), lax.axis_index("dp"), n // nd
     cw = blocks[0].shape[1]
-    for c in range(len(blocks) // n):
-        for i in range(n):
-            part = blocks[c * n + i][...].astype(F32)
-            cols = pl.ds(pl.multiple_of(lax.rem(place[i], share) * wide + c * cw, HEAD_DIM), cw)
-            for t in range(KINDS):
-                held[lax.div(place[i], share), t, :, cols] = part[t * POOL : (t + 1) * POOL]
+    for i in range(n):
+        part = blocks[i][...].astype(F32)
+        cols = aligned(lax.rem(place[i], share), cw)
+        for t in range(KINDS):
+            held[lax.div(place[i], share), t, :, cols] = part[t * POOL : (t + 1) * POOL]
     for k in range(nd):
         outs[k][...] = held[lax.rem(col + k, nd)]
 
 
-def spread_kernel(n, nd, wide, weight, *refs):
-    blocks, out = refs[:-1], refs[-1]
+def total_kernel(wide, spans, *refs):
+    parts, out = refs[:-1], refs[-1]
+    nd = len(parts) // len(spans)
+    for c, (first, cw) in enumerate(spans):
+        total = parts[c * nd][...]
+        for k in range(1, nd):
+            total = total + parts[c * nd + k][...]
+        for b in range(total.shape[2] // cw):
+            out[:, :, b * wide + first : b * wide + first + cw] = total[:, :, b * cw : (b + 1) * cw]
+
+
+def spread_kernel(n, nd, wide, first, weight, *refs):
+    blocks, (out, made_ref, sem) = refs[:n], refs[-3:]
     place, col, share = places(n, -1), lax.axis_index("dp"), n // nd
-    rc = out.shape[0] // POOL
-    cw = blocks[0].shape[1]
-    sel = interleave_matrix(rc * POOL)
-    for c in range(len(blocks) // n):
-        for i in range(n):
-            ref = blocks[c * n + i]
-            cols = pl.ds(pl.multiple_of(place[i] * wide + c * cw, HEAD_DIM), cw)
-            w = weight[
-                lax.rem(col - lax.div(place[i], share) + nd, nd),
-                :,
-                pl.ds(pl.multiple_of(lax.rem(place[i], share) * wide + c * cw, HEAD_DIM), cw),
-            ]
-            parts = [ref[t * rc : (t + 1) * rc, :].astype(F32) for t in range(3)]
-            made = []
-            for j in range(POOL):
-                total = parts[0] * w[j][None, :]
-                for t in range(1, 3):
-                    total = total + parts[t] * w[t * POOL + j][None, :]
-                made.append(total.astype(BF16))
-            out[:, cols] = dot(sel, jnp.concatenate(made, 0), 0, 0).astype(BF16)
+    rows, cw = made_ref.shape[1:]
+    rc = rows // POOL
+    sel = interleave_matrix(rows)
+    copies = []
+    for i in range(n):
+        ref = blocks[i]
+        w = weight[
+            lax.rem(col - lax.div(place[i], share) + nd, nd),
+            :,
+            pl.ds(pl.multiple_of(lax.rem(place[i], share) * wide + first, HEAD_DIM), cw),
+        ]
+        parts = [ref[t * rc : (t + 1) * rc, :].astype(F32) for t in range(3)]
+        made = []
+        for j in range(POOL):
+            total = parts[0] * w[j][None, :]
+            for t in range(1, 3):
+                total = total + parts[t] * w[t * POOL + j][None, :]
+            made.append(total.astype(BF16))
+        made_ref[i] = dot(sel, jnp.concatenate(made, 0), 0, 0).astype(BF16)
+        cols = pl.ds(pl.multiple_of(place[i] * wide + first, HEAD_DIM), cw)
+        copy = pltpu.make_async_copy(made_ref.at[i], out.at[:, cols], sem.at[i])
+        copy.start()
+        copies.append(copy)
+    for copy in copies:
+        copy.wait()
 
 
 def per_device(n, nd, block_input, cotangent, pool_weight):
@@ -217,15 +231,17 @@
     rc = rows // POOL
     length = rc * n
     heads = wide // HEAD_DIM
-    chunks = CHUNKS if heads % CHUNKS == 0 else 1
-    cw = wide // chunks
+    share = n // nd
+    small = heads // 4
+    split = [heads - small, small] if small else [heads]
+    spans = [(sum(split[:c]) * HEAD_DIM, h * HEAD_DIM) for c, h in enumerate(split)]
     todo = messages(n)
     shape = jax.ShapeDtypeStruct
 
     arrived = []
-    for c in range(chunks):
+    for first, cw in spans:
         cut = pl.pallas_call(
-            functools.partial(cut_kernel, n, wide, c * cw),
+            functools.partial(cut_kernel, n, wide, first),
             out_shape=[shape((2 * rows, cw), BF16)] * n,
             in_specs=[ANY, ANY],
             out_specs=[VMEM] * n,
@@ -237,10 +253,10 @@
     weights = jnp.stack(pieces)
 
     back = []
-    for c in range(chunks):
+    for c, (first, cw) in enumerate(spans):
         full = lambda kind: pltpu.VMEM((length, cw), kind)
         made = pl.pallas_call(
-            functools.partial(block_kernel, n, nd, rc, wide, c * cw),
+            functools.partial(block_kernel, n, nd, rc, wide, first),
             out_shape=[shape((3 * rc + KINDS * POOL, cw), BF16)] * n,
             in_specs=[VMEM] * (1 + n),
             out_specs=[VMEM] * n,
@@ -250,29 +266,40 @@
             + [full(F32)] * 3
             + [pltpu.VMEM((KINDS * POOL, cw), F32)],
         )(weights, *arrived[c])
-        back += [made[0]] + [send(b, n, m) for b, m in zip(made[1:], todo)]
-
-    tail = pl.BlockSpec((KINDS * POOL, cw), lambda i: (3 * rc // (KINDS * POOL), 0))
-    owned = (KINDS, POOL, width // nd)
-    part = pl.BlockSpec(owned, lambda i: (0, 0, 0))
-    shares = pl.pallas_call(
-        functools.partial(collect_kernel, n, nd, wide),
-        out_shape=[shape(owned, F32)] * nd,
-        grid=(1,),
-        in_specs=[tail] * len(back),
-        out_specs=[part] * nd,
-        scratch_shapes=[pltpu.VMEM((nd,) + owned, F32)],
-    )(*back)
-    weight_grad = shares[0]
-    for k in range(1, nd):
-        weight_grad = weight_grad + lax.ppermute(shares[k], "dp", [(d, (d + k) % nd) for d in range(nd)])
-    input_grad = pl.pallas_call(
-        functools.partial(spread_kernel, n, nd, wide),
-        out_shape=shape((rows, width), BF16),
-        in_specs=[VMEM] * (1 + len(back)),
+        back.append([made[0]] + [send(b, n, m) for b, m in zip(made[1:], todo)])
+
+    parts = []
+    input_grad = ()
+    for c, (first, cw) in enumerate(spans):
+        owned = (KINDS, POOL, share * cw)
+        shares = pl.pallas_call(
+            functools.partial(collect_kernel, n, nd),
+            out_shape=[shape(owned, F32)] * nd,
+            grid=(1,),
+            in_specs=[pl.BlockSpec((KINDS * POOL, cw), lambda i: (3 * rc // (KINDS * POOL), 0))] * n,
+            out_specs=[pl.BlockSpec(owned, lambda i: (0, 0, 0))] * nd,
+            scratch_shapes=[pltpu.VMEM((nd,) + owned, F32)],
+        )(*back[c])
+        parts.append(shares[0])
+        for k in range(1, nd):
+            parts.append(lax.ppermute(shares[k], "dp", [(d, (d + k) % nd) for d in range(nd)]))
+        input_grad = (
+            pl.pallas_call(
+                functools.partial(spread_kernel, n, nd, wide, first),
+                out_shape=shape((rows, width), BF16),
+                in_specs=[VMEM] * (1 + n) + [ANY] * len(input_grad),
+                out_specs=ANY,
+                input_output_aliases={1 + n: 0} if input_grad else {},
+                scratch_shapes=[pltpu.VMEM((n, rows, cw), BF16), pltpu.SemaphoreType.DMA((n,))],
+            )(weights, *back[c], *input_grad),
+        )
+    weight_grad = pl.pallas_call(
+        functools.partial(total_kernel, wide, spans),
+        out_shape=shape((KINDS, POOL, width // nd), F32),
+        in_specs=[VMEM] * len(parts),
         out_specs=VMEM,
-    )(weights, *back)
-    return input_grad[None], weight_grad
+    )(*parts)
+    return input_grad[0][None], weight_grad
 
 
 def solution(mesh):

time: 94.2 us -> 104 us (1.10)
  waiting for transfers between devices: 26.5 us -> 31.2 us
  Pallas kernels: 18.2 us -> 22.5 us
    pallas_call x6 -> x9, Pallas kernels: 18.2 us -> 22.5 us  [the longest x2 8.85 us: per_device(): pl.pallas_call(functools.partial(block_kernel, n, nd, rc, wide, first), o...]
    ppermute x28, waiting for transfers between devices: 23.5 us -> 27.4 us  [send(): return lax.ppermute(block, 'seq', pairs)]
    ppermute x3 -> x6, waiting for transfers between devices: 0.85 us -> 3.76 us  [per_device(): lax.ppermute(shares[k], 'dp', [(d, (d + k) % nd) for d in range(nd)])]
    ppermute x3, waiting for transfers between devices: 2.17 us -> 0.01 us  [per_device(): lax.ppermute(own, 'dp', [(d, (d + k) % nd) for d in range(nd)])]
    ppermute x3 -> x6, starting transfers between devices: 3.56 us -> 5.7 us  [per_device(): lax.ppermute(shares[k], 'dp', [(d, (d + k) % nd) for d in range(nd)])]
    ppermute x3, starting transfers between devices: 5.07 us -> 3.6 us  [per_device(): lax.ppermute(own, 'dp', [(d, (d + k) % nd) for d in range(nd)])]
    unnamed x72 -> x94, local copies, waits for them, and re-layouts: 0.67 us -> 1.95 us
  transfers between devices with their start and end apart: 34 -> 37, of which waited for: 10 -> 6; matrix products, arithmetic and copies ran while one was open for 1% -> 1% of each run, Pallas kernels for 18% -> 18%
where the time goes in v1:
time: 104 us; the launch traced here: 103 us
  starting transfers between devices  45.6 us (44%)
  waiting for transfers between devices  31.2 us (30%)
  Pallas kernels  22.5 us (22%)
  local copies, waits for them, and re-layouts  2 us (2%)
  between operations  1.15 us (1%)
    ppermute x28, starting transfers between devices, send(): return lax.ppermute(block, 'seq', pairs)  36.3 us
    ppermute x28, waiting for transfers between devices, send(): return lax.ppermute(block, 'seq', pairs)  27.4 us
    pallas_call x2, Pallas kernels, per_device(): pl.pallas_call(functools.partial(block_kernel, n, nd, rc, wide, first), o...  8.85 us
    ppermute x6, starting transfers between devices, per_device(): lax.ppermute(shares[k], 'dp', [(d, (d + k) % nd) for d in range(nd)])  5.7 us
    pallas_call x2, Pallas kernels, per_device(): pl.pallas_call(functools.partial(cut_kernel, n, wide, first), out_shape=[...  4.69 us
    pallas_call x2, Pallas kernels, per_device(): pl.pallas_call(functools.partial(spread_kernel, n, nd, wide, first), out_...  4.53 us
    ppermute x6, waiting for transfers between devices, per_device(): lax.ppermute(shares[k], 'dp', [(d, (d + k) % nd) for d in range(nd)])  3.76 us
    ppermute x3, starting transfers between devices, per_device(): lax.ppermute(own, 'dp', [(d, (d + k) % nd) for d in range(nd)])  3.6 us
  transfers between devices with their start and end apart: 37, of which 6 were waited for; matrix products, arithmetic and copies ran while one was open for 1% of the time, Pallas kernels for 18%

profile of v1, /device:TPU:0, one launch (start us, length us, event | category | flops | bytes accessed | tf_op | source)
XLA Modules:
  0.0 103.1 jit_solution(7026568426128819379)
XLA Ops:
  0.6 2.8 %shard_map.52 = (bf16[256,384]{1,0:T(8,128)(2,1)}, bf16[256,384]{1,0:T(8,128)(2,1)}, bf16[256,384]{1,0:T(8,128)(2,1)}, bf16[256,384]{1,0:T(8,128)(2,1)}, bf16[25...) custom-call(bf16[128,4096]{1,0:T(8,128)(2,1)} %bitcast.6, ...), custom_call_target="tpu_custom_call" | custom-call | tf_op jit(solution)/shard_map/pallas_call | solution.py:243
  3.4 4.1 %collective-permute-start.17 = (bf16[256,384]{1,0:T(8,128)(2,1)}, bf16[256,384]{1,0:T(8,128)(2,1)S(1)}, u32[]{:S(2)}, u32[]{:S(2)}) collective-permute-start(bf16[256,384]{1,0:T(8,128)(2,1)} %get-tuple-element.59), channel_id=1, source_target_pairs={{0,16},{4,20},{8,24},{12,28},{16,0},{20,4},{24,8},{28,12},{1,17},{... | collective-permute-start | bytes 589832 | tf_op jit(solution)/shard_map/ppermute | solution.py:46
  7.5 0.0 collective-permute-start.18
  7.6 2.5 %collective-permute-start.2 = (f32[16,1024]{1,0:T(8,128)S(1)}, f32[16,1024]{1,0:T(8,128)S(1)}, u32[]{:S(2)}, u32[]{:S(2)}) collective-permute-start(f32[16,1024]{1,0:T(8,128)S(1)} %reshape.7), channel_id=1, source_target_pairs={{0,3},{1,0},{2,1},{3,2},{4,7},{5,4},{6,5},{7,6},{8,11},{9,8},{10,9... | collective-permute-start | bytes 196616 | tf_op jit(solution)/shard_map/ppermute | solution.py:252
  10.1 0.5 collective-permute-start.1
  10.6 0.6 collective-permute-start
  11.2 1.9 %shard_map.50 = (bf16[256,128]{1,0:T(8,128)(2,1)}, bf16[256,128]{1,0:T(8,128)(2,1)}, bf16[256,128]{1,0:T(8,128)(2,1)}, bf16[256,128]{1,0:T(8,128)(2,1)}, bf16[25...) custom-call(bf16[128,4096]{1,0:T(8,128)(2,1)} %bitcast.7, ...), custom_call_target="tpu_custom_call" | custom-call | tf_op jit(solution)/shard_map/pallas_call | solution.py:243
  13.2 2.1 %collective-permute-start.3 = (bf16[256,128]{1,0:T(8,128)(2,1)}, bf16[256,128]{1,0:T(8,128)(2,1)S(1)}, u32[]{:S(2)}, u32[]{:S(2)}) collective-permute-start(bf16[256,128]{1,0:T(8,128)(2,1)} %get-tuple-element.43), channel_id=1, source_target_pairs={{0,16},{4,20},{8,24},{12,28},{16,0},{20,4},{24,8},{28,12},{1,17},{... | collective-permute-start | bytes 196616 | tf_op jit(solution)/shard_map/ppermute | solution.py:46
  15.3 0.0 collective-permute-done.1
  15.3 1.0 collective-permute-start.4
  16.3 1.6 %collective-permute-start.19 = (bf16[256,384]{1,0:T(8,128)(2,1)S(1)}, bf16[256,384]{1,0:T(8,128)(2,1)S(1)}, u32[]{:S(2)}, u32[]{:S(2)}) collective-permute-start(bf16[256,384]{1,0:T(8,128)(2,1)S(1)} %copy-done.39), channel_id=1, source_target_pairs={{0,8},{4,12},{8,16},{12,20},{16,24},{20,28},{24,0},{28,4},{1,9},{5... | collective-permute-start | bytes 589832 | tf_op jit(solution)/shard_map/ppermute | solution.py:46
  17.9 16.5 %collective-permute-done.3.refs_1_ = bf16[256,128]{1,0:T(8,128)(2,1)S(1)} collective-permute-done((bf16[256,128]{1,0:T(8,128)(2,1)}, bf16[256,128]{1,0:T(8,128)(2,1)S(1)}, u32[]{:S(2)}, u32[]{:S(2)}) %collective-permute-start.3) | collective-permute-done | bytes 65568 | tf_op jit(solution)/shard_map/ppermute | solution.py:46
  34.4 0.0 collective-permute-start.20
  34.5 1.7 %collective-permute-start.21 = (bf16[256,384]{1,0:T(8,128)(2,1)S(1)}, bf16[256,384]{1,0:T(8,128)(2,1)S(1)}, u32[]{:S(2)}, u32[]{:S(2)}) collective-permute-start(bf16[256,384]{1,0:T(8,128)(2,1)S(1)} %copy-done.37), channel_id=1, source_target_pairs={{0,24},{4,28},{8,0},{12,4},{16,8},{20,12},{24,16},{28,20},{1,25},{... | collective-permute-start | bytes 589832 | tf_op jit(solution)/shard_map/ppermute | solution.py:46
  36.2 0.0 collective-permute-done.17.refs_1_
  36.2 1.9 %collective-permute-start.22 = (bf16[256,384]{1,0:T(8,128)(2,1)S(1)}, bf16[256,384]{1,0:T(8,128)(2,1)S(1)}, u32[]{:S(2)}, u32[]{:S(2)}) collective-permute-start(bf16[256,384]{1,0:T(8,128)(2,1)S(1)} %copy-done.36), channel_id=1, source_target_pairs={{0,28},{4,24},{8,4},{12,0},{16,12},{20,8},{24,20},{28,16},{1,29},{... | collective-permute-start | bytes 589832 | tf_op jit(solution)/shard_map/ppermute | solution.py:46
  38.2 0.2 collective-permute-start.23
  38.4 0.0 collective-permute-done.19.refs_3_
  38.4 1.7 %collective-permute-start.5 = (bf16[256,128]{1,0:T(8,128)(2,1)}, bf16[256,128]{1,0:T(8,128)(2,1)S(1)}, u32[]{:S(2)}, u32[]{:S(2)}) collective-permute-start(bf16[256,128]{1,0:T(8,128)(2,1)} %get-tuple-element.45), channel_id=1, source_target_pairs={{0,8},{4,12},{8,16},{12,20},{16,24},{20,28},{24,0},{28,4},{1,9},{5... | collective-permute-start | bytes 196616 | tf_op jit(solution)/shard_map/ppermute | solution.py:46
  40.1 3.4 %collective-permute-done.20.refs_4_ = bf16[256,384]{1,0:T(8,128)(2,1)S(1)} collective-permute-done((bf16[256,384]{1,0:T(8,128)(2,1)S(1)}, bf16[256,384]{1,0:T(8,128)(2,1)S(1)}, u32[]{:S(2)}, u32[]{:S(2)}) %collective-permute-start.20) | collective-permute-done | bytes 196640 | tf_op jit(solution)/shard_map/ppermute | solution.py:46
  43.4 4.1 %collective-permute-start.6 = (bf16[256,128]{1,0:T(8,128)(2,1)}, bf16[256,128]{1,0:T(8,128)(2,1)S(1)}, u32[]{:S(2)}, u32[]{:S(2)}) collective-permute-start(bf16[256,128]{1,0:T(8,128)(2,1)} %get-tuple-element.46), channel_id=1, source_target_pairs={{0,12},{4,8},{8,20},{12,16},{16,28},{20,24},{24,4},{28,0},{1,13},{... | collective-permute-start | bytes 196616 | tf_op jit(solution)/shard_map/ppermute | solution.py:46
  47.5 0.0 collective-permute-done.21.refs_5_
  47.5 0.0 collective-permute-start.7
  47.6 3.6 %collective-permute-done.22.refs_6_ = bf16[256,384]{1,0:T(8,128)(2,1)S(1)} collective-permute-done((bf16[256,384]{1,0:T(8,128)(2,1)S(1)}, bf16[256,384]{1,0:T(8,128)(2,1)S(1)}, u32[]{:S(2)}, u32[]{:S(2)}) %collective-permute-start.22) | collective-permute-done | bytes 196640 | tf_op jit(solution)/shard_map/ppermute | solution.py:46
  51.1 0.4 collective-permute-start.8
  51.5 0.5 collective-permute-start.9
  52.1 0.7 pad_maximum_fusion.weight
  52.9 5.7 %shard_map.53 = (bf16[112,384]{1,0:T(8,128)(2,1)}, bf16[112,384]{1,0:T(8,128)(2,1)}, bf16[112,384]{1,0:T(8,128)(2,1)}, bf16[112,384]{1,0:T(8,128)(2,1)}, bf16[11...) custom-call(f32[4,16,1024]{2,1,0:T(8,128)} %pad_maximum_fusion.weight, ...), custom_call_target="tpu_custom_call" | custom-call | tf_op jit(solution)/shard_map/pallas_call | solution.py:258
  58.5 0.6 collective-permute-start.24
  59.1 1.8 %collective-permute-start.25 = (bf16[112,384]{1,0:T(8,128)(2,1)}, bf16[112,384]{1,0:T(8,128)(2,1)S(1)}, u32[]{:S(2)}, u32[]{:S(2)}) collective-permute-start(bf16[112,384]{1,0:T(8,128)(2,1)} %get-tuple-element.68), channel_id=1, source_target_pairs={{0,20},{4,16},{8,28},{12,24},{16,4},{20,0},{24,12},{28,8},{1,21},{... | collective-permute-start | bytes 258056 | tf_op jit(solution)/shard_map/ppermute | solution.py:46
  61.0 0.6 copy-done.26
  61.5 0.0 copy-done.27
  61.5 0.0 copy-done.28
  61.6 3.2 %shard_map.51 = (bf16[112,128]{1,0:T(8,128)(2,1)}, bf16[112,128]{1,0:T(8,128)(2,1)}, bf16[112,128]{1,0:T(8,128)(2,1)}, bf16[112,128]{1,0:T(8,128)(2,1)}, bf16[11...) custom-call(f32[4,16,1024]{2,1,0:T(8,128)} %pad_maximum_fusion.weight, ...), custom_call_target="tpu_custom_call" | custom-call | tf_op jit(solution)/shard_map/pallas_call | solution.py:258
  64.8 0.9 collective-permute-start.10
  65.6 2.2 %collective-permute-start.11 = (bf16[112,128]{1,0:T(8,128)(2,1)}, bf16[112,128]{1,0:T(8,128)(2,1)S(1)}, u32[]{:S(2)}, u32[]{:S(2)}) collective-permute-start(bf16[112,128]{1,0:T(8,128)(2,1)} %get-tuple-element.52), channel_id=1, source_target_pairs={{0,20},{4,16},{8,28},{12,24},{16,4},{20,0},{24,12},{28,8},{1,21},{... | collective-permute-start | bytes 86024 | tf_op jit(solution)/shard_map/ppermute | solution.py:46
  67.8 1.2 %collective-permute-start.26 = (bf16[112,384]{1,0:T(8,128)(2,1)S(1)}, bf16[112,384]{1,0:T(8,128)(2,1)S(1)}, u32[]{:S(2)}, u32[]{:S(2)}) collective-permute-start(bf16[112,384]{1,0:T(8,128)(2,1)S(1)} %copy-done.44), channel_id=1, source_target_pairs={{0,8},{4,12},{8,16},{12,20},{16,24},{20,28},{24,0},{28,4},{1,9},{5... | collective-permute-start | bytes 258056 | tf_op jit(solution)/shard_map/ppermute | solution.py:46
  69.1 2.8 %collective-permute-done.10.refs_1_ = bf16[112,128]{1,0:T(8,128)(2,1)S(1)} collective-permute-done((bf16[112,128]{1,0:T(8,128)(2,1)}, bf16[112,128]{1,0:T(8,128)(2,1)S(1)}, u32[]{:S(2)}, u32[]{:S(2)}) %collective-permute-start.10) | collective-permute-done | bytes 28704 | tf_op jit(solution)/shard_map/ppermute | solution.py:46
  71.9 1.9 %collective-permute-start.28 = (bf16[112,384]{1,0:T(8,128)(2,1)S(1)}, bf16[112,384]{1,0:T(8,128)(2,1)S(1)}, u32[]{:S(2)}, u32[]{:S(2)}) collective-permute-start(bf16[112,384]{1,0:T(8,128)(2,1)S(1)} %copy-done.42), channel_id=1, source_target_pairs={{0,24},{4,28},{8,0},{12,4},{16,8},{20,12},{24,16},{28,20},{1,25},{... | collective-permute-start | bytes 258056 | tf_op jit(solution)/shard_map/ppermute | solution.py:46
  73.8 1.7 %collective-permute-start.29 = (bf16[112,384]{1,0:T(8,128)(2,1)S(1)}, bf16[112,384]{1,0:T(8,128)(2,1)S(1)}, u32[]{:S(2)}, u32[]{:S(2)}) collective-permute-start(bf16[112,384]{1,0:T(8,128)(2,1)S(1)} %copy-done.41), channel_id=1, source_target_pairs={{0,28},{4,24},{8,4},{12,0},{16,12},{20,8},{24,20},{28,16},{1,29},{... | collective-permute-start | bytes 258056 | tf_op jit(solution)/shard_map/ppermute | solution.py:46
  75.6 0.2 collective-permute-start.30
  75.8 1.7 %collective-permute-start.12 = (bf16[112,128]{1,0:T(8,128)(2,1)}, bf16[112,128]{1,0:T(8,128)(2,1)S(1)}, u32[]{:S(2)}, u32[]{:S(2)}) collective-permute-start(bf16[112,128]{1,0:T(8,128)(2,1)} %get-tuple-element.53), channel_id=1, source_target_pairs={{0,8},{4,12},{8,16},{12,20},{16,24},{20,28},{24,0},{28,4},{1,9},{5... | collective-permute-start | bytes 86024 | tf_op jit(solution)/shard_map/ppermute | solution.py:46
  77.4 1.1 %collective-permute-done.27.refs_4_ = bf16[112,384]{1,0:T(8,128)(2,1)S(1)} collective-permute-done((bf16[112,384]{1,0:T(8,128)(2,1)S(1)}, bf16[112,384]{1,0:T(8,128)(2,1)S(1)}, u32[]{:S(2)}, u32[]{:S(2)}) %collective-permute-start.27) | collective-permute-done | bytes 86048 | tf_op jit(solution)/shard_map/ppermute | solution.py:46
  78.5 2.5 %collective-permute-start.14 = (bf16[112,128]{1,0:T(8,128)(2,1)}, bf16[112,128]{1,0:T(8,128)(2,1)S(1)}, u32[]{:S(2)}, u32[]{:S(2)}) collective-permute-start(bf16[112,128]{1,0:T(8,128)(2,1)} %get-tuple-element.55), channel_id=1, source_target_pairs={{0,24},{4,28},{8,0},{12,4},{16,8},{20,12},{24,16},{28,20},{1,25},{... | collective-permute-start | bytes 86024 | tf_op jit(solution)/shard_map/ppermute | solution.py:46
  81.0 1.5 %collective-permute-start.15 = (bf16[112,128]{1,0:T(8,128)(2,1)}, bf16[112,128]{1,0:T(8,128)(2,1)S(1)}, u32[]{:S(2)}, u32[]{:S(2)}) collective-permute-start(bf16[112,128]{1,0:T(8,128)(2,1)} %get-tuple-element.56), channel_id=1, source_target_pairs={{0,28},{4,24},{8,4},{12,0},{16,12},{20,8},{24,20},{28,16},{1,29},{... | collective-permute-start | bytes 86024 | tf_op jit(solution)/shard_map/ppermute | solution.py:46
  82.5 0.7 collective-permute-start.16
  83.3 1.5 %shard_map.56 = (f32[4,4,768]{2,1,0:T(4,128)}, f32[4,4,768]{2,1,0:T(4,128)}, f32[4,4,768]{2,1,0:T(4,128)}, f32[4,4,768]{2,1,0:T(4,128)}) custom-call(bf16[112,384]{1,0:T(8,128)(2,1)} %get-tuple-element.66.refs_0_, bf16[112,384]{1,0:T(8,128)(2,1)} %copy-done, bf16[112,384]{1,0:T(8,128)(2,1)} %copy-done.1, bf16[112,384]{1,0:T(8,128)(2,1)} %copy-done.2, ...), custom_call_target="tpu_custom_call" | custom-call | tf_op jit(solution)/shard_map/pallas_call | solution.py:275
  84.8 1.6 %collective-permute-start.31 = (f32[4,4,768]{2,1,0:T(4,128)}, f32[4,4,768]{2,1,0:T(4,128)S(1)}, u32[]{:S(2)}, u32[]{:S(2)}) collective-permute-start(f32[4,4,768]{2,1,0:T(4,128)} %get-tuple-element.75), channel_id=1, source_target_pairs={{0,1},{1,2},{2,3},{3,0},{4,5},{5,6},{6,7},{7,4},{8,9},{9,10},{10,1... | collective-permute-start | bytes 147464 | tf_op jit(solution)/shard_map/ppermute | solution.py:285
  86.5 1.5 %collective-permute-start.32 = (f32[4,4,768]{2,1,0:T(4,128)}, f32[4,4,768]{2,1,0:T(4,128)S(1)}, u32[]{:S(2)}, u32[]{:S(2)}) collective-permute-start(f32[4,4,768]{2,1,0:T(4,128)} %get-tuple-element.76), channel_id=1, source_target_pairs={{0,2},{1,3},{2,0},{3,1},{4,6},{5,7},{6,4},{7,5},{8,10},{9,11},{10,... | collective-permute-start | bytes 147464 | tf_op jit(solution)/shard_map/ppermute | solution.py:285
  88.0 1.4 %collective-permute-start.33 = (f32[4,4,768]{2,1,0:T(4,128)}, f32[4,4,768]{2,1,0:T(4,128)S(1)}, u32[]{:S(2)}, u32[]{:S(2)}) collective-permute-start(f32[4,4,768]{2,1,0:T(4,128)} %get-tuple-element.77), channel_id=1, source_target_pairs={{0,3},{1,0},{2,1},{3,2},{4,7},{5,4},{6,5},{7,6},{8,11},{9,8},{10,9... | collective-permute-start | bytes 147464 | tf_op jit(solution)/shard_map/ppermute | solution.py:285
  89.5 0.6 copy-done.20
  90.1 0.0 copy-done.21
  90.1 1.4 %shard_map.57 = (f32[4,4,256]{2,1,0:T(4,128)}, f32[4,4,256]{2,1,0:T(4,128)}, f32[4,4,256]{2,1,0:T(4,128)}, f32[4,4,256]{2,1,0:T(4,128)}) custom-call(bf16[112,128]{1,0:T(8,128)(2,1)} %get-tuple-element.50.refs_0_, bf16[112,128]{1,0:T(8,128)(2,1)} %copy-done.15, bf16[112,128]{1,0:T(8,128)(2,1)} %copy-done.16, bf16[112,128]{1,0:T(8,128)(2,1)} %copy-done.17, ...), custom_call_target="tpu_custom_call" | custom-call | tf_op jit(solution)/shard_map/pallas_call | solution.py:275
  91.4 0.6 collective-permute-start.34
  92.0 0.5 collective-permute-start.35
  92.6 3.7 %collective-permute-done.34.refs_5_ = f32[4,4,256]{2,1,0:T(4,128)S(1)} collective-permute-done((f32[4,4,256]{2,1,0:T(4,128)}, f32[4,4,256]{2,1,0:T(4,128)S(1)}, u32[]{:S(2)}, u32[]{:S(2)}) %collective-permute-start.34) | collective-permute-done | bytes 16416 | tf_op jit(solution)/shard_map/ppermute | solution.py:285
  96.3 2.5 %shard_map.54.refs_8_ = bf16[128,4096]{1,0:T(8,128)(2,1)} custom-call(f32[4,16,1024]{2,1,0:T(8,128)} %pad_maximum_fusion.weight, bf16[112,384]{1,0:T(8,128)(2,1)} %get-tuple-element.66.refs_0_, bf16[112,384]{1,0:T(8,128)(2,1)} %copy-done, bf16[112,384]{1,0:T(8,128)(2,1)} %copy-done.1, bf16[112,384]{1,0:T(8,128)(2,1)} %copy-done.2, ...), custom_call_target="tpu_custom_call" | custom-call | tf_op jit(solution)/shard_map/pallas_call | solution.py:287
  98.8 2.0 %shard_map.55 = bf16[128,4096]{1,0:T(8,128)(2,1)} custom-call(f32[4,16,1024]{2,1,0:T(8,128)} %pad_maximum_fusion.weight, bf16[112,128]{1,0:T(8,128)(2,1)} %get-tuple-element.50.refs_0_, bf16[112,128]{1,0:T(8,128)(2,1)} %copy-done.15, bf16[112,128]{1,0:T(8,128)(2,1)} %copy-done.16, bf16[112,128]{1,0:T(8,128)(2,1)} %copy-done.17, ...), custom_call_target="tpu_custom_call", output_to_operand_aliasing={{}: (9, {})} | custom-call | tf_op jit(solution)/shard_map/pallas_call | solution.py:287
  101.0 0.5 copy-done.33
  101.5 0.0 copy-done.34
  101.5 0.0 copy-done.29
  101.5 0.0 copy-done.30
  101.5 0.0 copy-done.31
  101.6 1.5 %shard_map.58 = f32[4,4,1024]{2,1,0:T(4,128)} custom-call(f32[4,4,768]{2,1,0:T(4,128)} %get-tuple-element.74.refs_0_, f32[4,4,768]{2,1,0:T(4,128)} %copy-done.29, f32[4,4,768]{2,1,0:T(4,128)} %copy-done.30, f32[4,4,768]{2,1,0:T(4,128)} %copy-done.31, f32[4,4,256]{2,1,0:T(4,128)} %get-tuple-element.78.refs_4_, f32[4,4,256]{2,1,0:T(4,128)} %copy-done.32, ...), custom_call_target="tpu_custom_call" | custom-call | tf_op jit(solution)/shard_map/pallas_call | solution.py:296
  (116 shorter events, 0.3 us)
Async XLA Ops:
  0.6 6.9 %copy-start.7 = (f32[4,4,1024]{2,1,0:T(4,128)S(1)}, f32[4,4,1024]{2,1,0:T(4,128)}, u32[]{:S(2)}) copy-start(f32[4,4,1024]{2,1,0:T(4,128)} %param.5) | copy-start | bytes 196612
  3.4 32.8 %collective-permute-start.17 = (bf16[256,384]{1,0:T(8,128)(2,1)}, bf16[256,384]{1,0:T(8,128)(2,1)S(1)}, u32[]{:S(2)}, u32[]{:S(2)}) collective-permute-start(bf16[256,384]{1,0:T(8,128)(2,1)} %get-tuple-element.59), channel_id=1, source_target_pairs={{0,16},{4,20},{8,24},{12,28},{16,0},{20,4},{24,8},{28,12},{1,17},{... | collective-permute-start | bytes 589832 | tf_op jit(solution)/shard_map/ppermute | solution.py:46
  7.5 30.6 %collective-permute-start.18 = (bf16[256,384]{1,0:T(8,128)(2,1)}, bf16[256,384]{1,0:T(8,128)(2,1)S(1)}, u32[]{:S(2)}, u32[]{:S(2)}) collective-permute-start(bf16[256,384]{1,0:T(8,128)(2,1)} %get-tuple-element.60), channel_id=1, source_target_pairs={{0,20},{4,16},{8,28},{12,24},{16,4},{20,0},{24,12},{28,8},{1,21},{... | collective-permute-start | bytes 589832 | tf_op jit(solution)/shard_map/ppermute | solution.py:46
  7.6 8.7 %copy-start.39 = (bf16[256,384]{1,0:T(8,128)(2,1)S(1)}, bf16[256,384]{1,0:T(8,128)(2,1)}, u32[]{:S(2)}) copy-start(bf16[256,384]{1,0:T(8,128)(2,1)} %get-tuple-element.61) | copy-start | bytes 589828
  7.6 26.8 %copy-start.38 = (bf16[256,384]{1,0:T(8,128)(2,1)S(1)}, bf16[256,384]{1,0:T(8,128)(2,1)}, u32[]{:S(2)}) copy-start(bf16[256,384]{1,0:T(8,128)(2,1)} %get-tuple-element.62) | copy-start | bytes 589828
  7.6 26.9 %copy-start.37 = (bf16[256,384]{1,0:T(8,128)(2,1)S(1)}, bf16[256,384]{1,0:T(8,128)(2,1)}, u32[]{:S(2)}) copy-start(bf16[256,384]{1,0:T(8,128)(2,1)} %get-tuple-element.63) | copy-start | bytes 589828
  7.6 28.6 %copy-start.36 = (bf16[256,384]{1,0:T(8,128)(2,1)S(1)}, bf16[256,384]{1,0:T(8,128)(2,1)}, u32[]{:S(2)}) copy-start(bf16[256,384]{1,0:T(8,128)(2,1)} %get-tuple-element.64) | copy-start | bytes 589828
  7.6 30.5 %copy-start.35 = (bf16[256,384]{1,0:T(8,128)(2,1)S(1)}, bf16[256,384]{1,0:T(8,128)(2,1)}, u32[]{:S(2)}) copy-start(bf16[256,384]{1,0:T(8,128)(2,1)} %get-tuple-element.65) | copy-start | bytes 589828
  7.6 5.5 %collective-permute-start.2 = (f32[16,1024]{1,0:T(8,128)S(1)}, f32[16,1024]{1,0:T(8,128)S(1)}, u32[]{:S(2)}, u32[]{:S(2)}) collective-permute-start(f32[16,1024]{1,0:T(8,128)S(1)} %reshape.7), channel_id=1, source_target_pairs={{0,3},{1,0},{2,1},{3,2},{4,7},{5,4},{6,5},{7,6},{8,11},{9,8},{10,9... | collective-permute-start | bytes 196616 | tf_op jit(solution)/shard_map/ppermute | solution.py:252
  10.1 5.2 %collective-permute-start.1 = (f32[16,1024]{1,0:T(8,128)S(1)}, f32[16,1024]{1,0:T(8,128)S(1)}, u32[]{:S(2)}, u32[]{:S(2)}) collective-permute-start(f32[16,1024]{1,0:T(8,128)S(1)} %reshape.7), channel_id=1, source_target_pairs={{0,2},{1,3},{2,0},{3,1},{4,6},{5,7},{6,4},{7,5},{8,10},{9,11},{10,... | collective-permute-start | bytes 196616 | tf_op jit(solution)/shard_map/ppermute | solution.py:252
  10.6 5.7 %collective-permute-start = (f32[16,1024]{1,0:T(8,128)S(1)}, f32[16,1024]{1,0:T(8,128)S(1)}, u32[]{:S(2)}, u32[]{:S(2)}) collective-permute-start(f32[16,1024]{1,0:T(8,128)S(1)} %reshape.7), channel_id=1, source_target_pairs={{0,1},{1,2},{2,3},{3,0},{4,5},{5,6},{6,7},{7,4},{8,9},{9,10},{10,1... | collective-permute-start | bytes 196616 | tf_op jit(solution)/shard_map/ppermute | solution.py:252
  13.2 21.3 %collective-permute-start.3 = (bf16[256,128]{1,0:T(8,128)(2,1)}, bf16[256,128]{1,0:T(8,128)(2,1)S(1)}, u32[]{:S(2)}, u32[]{:S(2)}) collective-permute-start(bf16[256,128]{1,0:T(8,128)(2,1)} %get-tuple-element.43), channel_id=1, source_target_pairs={{0,16},{4,20},{8,24},{12,28},{16,0},{20,4},{24,8},{28,12},{1,17},{... | collective-permute-start | bytes 196616 | tf_op jit(solution)/shard_map/ppermute | solution.py:46
  15.3 19.1 %collective-permute-start.4 = (bf16[256,128]{1,0:T(8,128)(2,1)}, bf16[256,128]{1,0:T(8,128)(2,1)S(1)}, u32[]{:S(2)}, u32[]{:S(2)}) collective-permute-start(bf16[256,128]{1,0:T(8,128)(2,1)} %get-tuple-element.44), channel_id=1, source_target_pairs={{0,20},{4,16},{8,28},{12,24},{16,4},{20,0},{24,12},{28,8},{1,21},{... | collective-permute-start | bytes 196616 | tf_op jit(solution)/shard_map/ppermute | solution.py:46
  16.3 22.1 %collective-permute-start.19 = (bf16[256,384]{1,0:T(8,128)(2,1)S(1)}, bf16[256,384]{1,0:T(8,128)(2,1)S(1)}, u32[]{:S(2)}, u32[]{:S(2)}) collective-permute-start(bf16[256,384]{1,0:T(8,128)(2,1)S(1)} %copy-done.39), channel_id=1, source_target_pairs={{0,8},{4,12},{8,16},{12,20},{16,24},{20,28},{24,0},{28,4},{1,9},{5... | collective-permute-start | bytes 589832 | tf_op jit(solution)/shard_map/ppermute | solution.py:46
  34.4 9.0 %collective-permute-start.20 = (bf16[256,384]{1,0:T(8,128)(2,1)S(1)}, bf16[256,384]{1,0:T(8,128)(2,1)S(1)}, u32[]{:S(2)}, u32[]{:S(2)}) collective-permute-start(bf16[256,384]{1,0:T(8,128)(2,1)S(1)} %copy-done.38), channel_id=1, source_target_pairs={{0,12},{4,8},{8,20},{12,16},{16,28},{20,24},{24,4},{28,0},{1,13},{... | collective-permute-start | bytes 589832 | tf_op jit(solution)/shard_map/ppermute | solution.py:46
  34.4 18.4 %copy-start.23 = (bf16[256,128]{1,0:T(8,128)(2,1)}, bf16[256,128]{1,0:T(8,128)(2,1)S(1)}, u32[]{:S(2)}) copy-start(bf16[256,128]{1,0:T(8,128)(2,1)S(1)} %collective-permute-done.4.refs_2_) | copy-start | bytes 196612
  34.5 13.1 %collective-permute-start.21 = (bf16[256,384]{1,0:T(8,128)(2,1)S(1)}, bf16[256,384]{1,0:T(8,128)(2,1)S(1)}, u32[]{:S(2)}, u32[]{:S(2)}) collective-permute-start(bf16[256,384]{1,0:T(8,128)(2,1)S(1)} %copy-done.37), channel_id=1, source_target_pairs={{0,24},{4,28},{8,0},{12,4},{16,8},{20,12},{24,16},{28,20},{1,25},{... | collective-permute-start | bytes 589832 | tf_op jit(solution)/shard_map/ppermute | solution.py:46
  36.2 16.6 %copy-start.8 = (bf16[256,384]{1,0:T(8,128)(2,1)}, bf16[256,384]{1,0:T(8,128)(2,1)S(1)}, u32[]{:S(2)}) copy-start(bf16[256,384]{1,0:T(8,128)(2,1)S(1)} %collective-permute-done.17.refs_1_) | copy-start | bytes 589828
  36.2 14.9 %collective-permute-start.22 = (bf16[256,384]{1,0:T(8,128)(2,1)S(1)}, bf16[256,384]{1,0:T(8,128)(2,1)S(1)}, u32[]{:S(2)}, u32[]{:S(2)}) collective-permute-start(bf16[256,384]{1,0:T(8,128)(2,1)S(1)} %copy-done.36), channel_id=1, source_target_pairs={{0,28},{4,24},{8,4},{12,0},{16,12},{20,8},{24,20},{28,16},{1,29},{... | collective-permute-start | bytes 589832 | tf_op jit(solution)/shard_map/ppermute | solution.py:46
  38.1 14.7 %copy-start.9 = (bf16[256,384]{1,0:T(8,128)(2,1)}, bf16[256,384]{1,0:T(8,128)(2,1)S(1)}, u32[]{:S(2)}) copy-start(bf16[256,384]{1,0:T(8,128)(2,1)S(1)} %collective-permute-done.18.refs_2_) | copy-start | bytes 589828
  38.1 13.0 %copy-start.46 = (bf16[256,128]{1,0:T(8,128)(2,1)S(1)}, bf16[256,128]{1,0:T(8,128)(2,1)}, u32[]{:S(2)}) copy-start(bf16[256,128]{1,0:T(8,128)(2,1)} %get-tuple-element.48) | copy-start | bytes 196612
  38.1 13.4 %copy-start.45 = (bf16[256,128]{1,0:T(8,128)(2,1)S(1)}, bf16[256,128]{1,0:T(8,128)(2,1)}, u32[]{:S(2)}) copy-start(bf16[256,128]{1,0:T(8,128)(2,1)} %get-tuple-element.49) | copy-start | bytes 196612
  38.2 13.4 %collective-permute-start.23 = (bf16[256,384]{1,0:T(8,128)(2,1)S(1)}, bf16[256,384]{1,0:T(8,128)(2,1)S(1)}, u32[]{:S(2)}, u32[]{:S(2)}) collective-permute-start(bf16[256,384]{1,0:T(8,128)(2,1)S(1)} %copy-done.35), channel_id=1, source_target_pairs={{0,4},{4,0},{8,12},{12,8},{16,20},{20,16},{24,28},{28,24},{1,5},{5... | collective-permute-start | bytes 589832 | tf_op jit(solution)/shard_map/ppermute | solution.py:46
  38.4 14.4 %copy-start.10 = (bf16[256,384]{1,0:T(8,128)(2,1)}, bf16[256,384]{1,0:T(8,128)(2,1)S(1)}, u32[]{:S(2)}) copy-start(bf16[256,384]{1,0:T(8,128)(2,1)S(1)} %collective-permute-done.19.refs_3_) | copy-start | bytes 589828
  38.4 20.1 %collective-permute-start.5 = (bf16[256,128]{1,0:T(8,128)(2,1)}, bf16[256,128]{1,0:T(8,128)(2,1)S(1)}, u32[]{:S(2)}, u32[]{:S(2)}) collective-permute-start(bf16[256,128]{1,0:T(8,128)(2,1)} %get-tuple-element.45), channel_id=1, source_target_pairs={{0,8},{4,12},{8,16},{12,20},{16,24},{20,28},{24,0},{28,4},{1,9},{5... | collective-permute-start | bytes 196616 | tf_op jit(solution)/shard_map/ppermute | solution.py:46
  43.4 9.4 %copy-start.11 = (bf16[256,384]{1,0:T(8,128)(2,1)}, bf16[256,384]{1,0:T(8,128)(2,1)S(1)}, u32[]{:S(2)}) copy-start(bf16[256,384]{1,0:T(8,128)(2,1)S(1)} %collective-permute-done.20.refs_4_) | copy-start | bytes 589828
  43.4 15.7 %collective-permute-start.6 = (bf16[256,128]{1,0:T(8,128)(2,1)}, bf16[256,128]{1,0:T(8,128)(2,1)S(1)}, u32[]{:S(2)}, u32[]{:S(2)}) collective-permute-start(bf16[256,128]{1,0:T(8,128)(2,1)} %get-tuple-element.46), channel_id=1, source_target_pairs={{0,12},{4,8},{8,20},{12,16},{16,28},{20,24},{24,4},{28,0},{1,13},{... | collective-permute-start | bytes 196616 | tf_op jit(solution)/shard_map/ppermute | solution.py:46
  47.5 5.3 %copy-start.12 = (bf16[256,384]{1,0:T(8,128)(2,1)}, bf16[256,384]{1,0:T(8,128)(2,1)S(1)}, u32[]{:S(2)}) copy-start(bf16[256,384]{1,0:T(8,128)(2,1)S(1)} %collective-permute-done.21.refs_5_) | copy-start | bytes 589828
  47.5 13.3 %collective-permute-start.7 = (bf16[256,128]{1,0:T(8,128)(2,1)}, bf16[256,128]{1,0:T(8,128)(2,1)S(1)}, u32[]{:S(2)}, u32[]{:S(2)}) collective-permute-start(bf16[256,128]{1,0:T(8,128)(2,1)} %get-tuple-element.47), channel_id=1, source_target_pairs={{0,24},{4,28},{8,0},{12,4},{16,8},{20,12},{24,16},{28,20},{1,25},{... | collective-permute-start | bytes 196616 | tf_op jit(solution)/shard_map/ppermute | solution.py:46
  51.1 9.8 %collective-permute-start.8 = (bf16[256,128]{1,0:T(8,128)(2,1)S(1)}, bf16[256,128]{1,0:T(8,128)(2,1)S(1)}, u32[]{:S(2)}, u32[]{:S(2)}) collective-permute-start(bf16[256,128]{1,0:T(8,128)(2,1)S(1)} %copy-done.46), channel_id=1, source_target_pairs={{0,28},{4,24},{8,4},{12,0},{16,12},{20,8},{24,20},{28,16},{1,29},{... | collective-permute-start | bytes 196616 | tf_op jit(solution)/shard_map/ppermute | solution.py:46
  51.5 9.4 %collective-permute-start.9 = (bf16[256,128]{1,0:T(8,128)(2,1)S(1)}, bf16[256,128]{1,0:T(8,128)(2,1)S(1)}, u32[]{:S(2)}, u32[]{:S(2)}) collective-permute-start(bf16[256,128]{1,0:T(8,128)(2,1)S(1)} %copy-done.45), channel_id=1, source_target_pairs={{0,4},{4,0},{8,12},{12,8},{16,20},{20,16},{24,28},{28,24},{1,5},{5... | collective-permute-start | bytes 196616 | tf_op jit(solution)/shard_map/ppermute | solution.py:46
  58.5 15.3 %collective-permute-start.24 = (bf16[112,384]{1,0:T(8,128)(2,1)}, bf16[112,384]{1,0:T(8,128)(2,1)S(1)}, u32[]{:S(2)}, u32[]{:S(2)}) collective-permute-start(bf16[112,384]{1,0:T(8,128)(2,1)} %get-tuple-element.67), channel_id=1, source_target_pairs={{0,16},{4,20},{8,24},{12,28},{16,0},{20,4},{24,8},{28,12},{1,17},{... | collective-permute-start | bytes 258056 | tf_op jit(solution)/shard_map/ppermute | solution.py:46
  59.1 16.5 %collective-permute-start.25 = (bf16[112,384]{1,0:T(8,128)(2,1)}, bf16[112,384]{1,0:T(8,128)(2,1)S(1)}, u32[]{:S(2)}, u32[]{:S(2)}) collective-permute-start(bf16[112,384]{1,0:T(8,128)(2,1)} %get-tuple-element.68), channel_id=1, source_target_pairs={{0,20},{4,16},{8,28},{12,24},{16,4},{20,0},{24,12},{28,8},{1,21},{... | collective-permute-start | bytes 258056 | tf_op jit(solution)/shard_map/ppermute | solution.py:46
  61.6 6.2 %copy-start.44 = (bf16[112,384]{1,0:T(8,128)(2,1)S(1)}, bf16[112,384]{1,0:T(8,128)(2,1)}, u32[]{:S(2)}) copy-start(bf16[112,384]{1,0:T(8,128)(2,1)} %get-tuple-element.69) | copy-start | bytes 258052
  61.6 10.3 %copy-start.43 = (bf16[112,384]{1,0:T(8,128)(2,1)S(1)}, bf16[112,384]{1,0:T(8,128)(2,1)}, u32[]{:S(2)}) copy-start(bf16[112,384]{1,0:T(8,128)(2,1)} %get-tuple-element.70) | copy-start | bytes 258052
  61.6 10.3 %copy-start.42 = (bf16[112,384]{1,0:T(8,128)(2,1)S(1)}, bf16[112,384]{1,0:T(8,128)(2,1)}, u32[]{:S(2)}) copy-start(bf16[112,384]{1,0:T(8,128)(2,1)} %get-tuple-element.71) | copy-start | bytes 258052
  61.6 12.2 %copy-start.41 = (bf16[112,384]{1,0:T(8,128)(2,1)S(1)}, bf16[112,384]{1,0:T(8,128)(2,1)}, u32[]{:S(2)}) copy-start(bf16[112,384]{1,0:T(8,128)(2,1)} %get-tuple-element.72) | copy-start | bytes 258052
  61.6 14.0 %copy-start.40 = (bf16[112,384]{1,0:T(8,128)(2,1)S(1)}, bf16[112,384]{1,0:T(8,128)(2,1)}, u32[]{:S(2)}) copy-start(bf16[112,384]{1,0:T(8,128)(2,1)} %get-tuple-element.73) | copy-start | bytes 258052
  64.8 7.1 %collective-permute-start.10 = (bf16[112,128]{1,0:T(8,128)(2,1)}, bf16[112,128]{1,0:T(8,128)(2,1)S(1)}, u32[]{:S(2)}, u32[]{:S(2)}) collective-permute-start(bf16[112,128]{1,0:T(8,128)(2,1)} %get-tuple-element.51), channel_id=1, source_target_pairs={{0,16},{4,20},{8,24},{12,28},{16,0},{20,4},{24,8},{28,12},{1,17},{... | collective-permute-start | bytes 86024 | tf_op jit(solution)/shard_map/ppermute | solution.py:46
  65.6 6.3 %collective-permute-start.11 = (bf16[112,128]{1,0:T(8,128)(2,1)}, bf16[112,128]{1,0:T(8,128)(2,1)S(1)}, u32[]{:S(2)}, u32[]{:S(2)}) collective-permute-start(bf16[112,128]{1,0:T(8,128)(2,1)} %get-tuple-element.52), channel_id=1, source_target_pairs={{0,20},{4,16},{8,28},{12,24},{16,4},{20,0},{24,12},{28,8},{1,21},{... | collective-permute-start | bytes 86024 | tf_op jit(solution)/shard_map/ppermute | solution.py:46
  67.8 7.9 %collective-permute-start.26 = (bf16[112,384]{1,0:T(8,128)(2,1)S(1)}, bf16[112,384]{1,0:T(8,128)(2,1)S(1)}, u32[]{:S(2)}, u32[]{:S(2)}) collective-permute-start(bf16[112,384]{1,0:T(8,128)(2,1)S(1)} %copy-done.44), channel_id=1, source_target_pairs={{0,8},{4,12},{8,16},{12,20},{16,24},{20,28},{24,0},{28,4},{1,9},{5... | collective-permute-start | bytes 258056 | tf_op jit(solution)/shard_map/ppermute | solution.py:46
  71.9 13.0 %copy-start.15 = (bf16[112,128]{1,0:T(8,128)(2,1)}, bf16[112,128]{1,0:T(8,128)(2,1)S(1)}, u32[]{:S(2)}) copy-start(bf16[112,128]{1,0:T(8,128)(2,1)S(1)} %collective-permute-done.10.refs_1_) | copy-start | bytes 86020
  71.9 6.6 %collective-permute-start.27 = (bf16[112,384]{1,0:T(8,128)(2,1)S(1)}, bf16[112,384]{1,0:T(8,128)(2,1)S(1)}, u32[]{:S(2)}, u32[]{:S(2)}) collective-permute-start(bf16[112,384]{1,0:T(8,128)(2,1)S(1)} %copy-done.43), channel_id=1, source_target_pairs={{0,12},{4,8},{8,20},{12,16},{16,28},{20,24},{24,4},{28,0},{1,13},{... | collective-permute-start | bytes 258056 | tf_op jit(solution)/shard_map/ppermute | solution.py:46
  71.9 12.9 %copy-start.16 = (bf16[112,128]{1,0:T(8,128)(2,1)}, bf16[112,128]{1,0:T(8,128)(2,1)S(1)}, u32[]{:S(2)}) copy-start(bf16[112,128]{1,0:T(8,128)(2,1)S(1)} %collective-permute-done.11.refs_2_) | copy-start | bytes 86020
  71.9 6.6 %collective-permute-start.28 = (bf16[112,384]{1,0:T(8,128)(2,1)S(1)}, bf16[112,384]{1,0:T(8,128)(2,1)S(1)}, u32[]{:S(2)}, u32[]{:S(2)}) collective-permute-start(bf16[112,384]{1,0:T(8,128)(2,1)S(1)} %copy-done.42), channel_id=1, source_target_pairs={{0,24},{4,28},{8,0},{12,4},{16,8},{20,12},{24,16},{28,20},{1,25},{... | collective-permute-start | bytes 258056 | tf_op jit(solution)/shard_map/ppermute | solution.py:46
  73.8 9.4 %copy-start = (bf16[112,384]{1,0:T(8,128)(2,1)}, bf16[112,384]{1,0:T(8,128)(2,1)S(1)}, u32[]{:S(2)}) copy-start(bf16[112,384]{1,0:T(8,128)(2,1)S(1)} %collective-permute-done.24.refs_1_) | copy-start | bytes 258052
  73.8 7.2 %collective-permute-start.29 = (bf16[112,384]{1,0:T(8,128)(2,1)S(1)}, bf16[112,384]{1,0:T(8,128)(2,1)S(1)}, u32[]{:S(2)}, u32[]{:S(2)}) collective-permute-start(bf16[112,384]{1,0:T(8,128)(2,1)S(1)} %copy-done.41), channel_id=1, source_target_pairs={{0,28},{4,24},{8,4},{12,0},{16,12},{20,8},{24,20},{28,16},{1,29},{... | collective-permute-start | bytes 258056 | tf_op jit(solution)/shard_map/ppermute | solution.py:46
  75.6 7.7 %copy-start.1 = (bf16[112,384]{1,0:T(8,128)(2,1)}, bf16[112,384]{1,0:T(8,128)(2,1)S(1)}, u32[]{:S(2)}) copy-start(bf16[112,384]{1,0:T(8,128)(2,1)S(1)} %collective-permute-done.25.refs_2_) | copy-start | bytes 258052
  75.6 6.9 %collective-permute-start.30 = (bf16[112,384]{1,0:T(8,128)(2,1)S(1)}, bf16[112,384]{1,0:T(8,128)(2,1)S(1)}, u32[]{:S(2)}, u32[]{:S(2)}) collective-permute-start(bf16[112,384]{1,0:T(8,128)(2,1)S(1)} %copy-done.40), channel_id=1, source_target_pairs={{0,4},{4,0},{8,12},{12,8},{16,20},{20,16},{24,28},{28,24},{1,5},{5... | collective-permute-start | bytes 258056 | tf_op jit(solution)/shard_map/ppermute | solution.py:46
  75.8 7.5 %copy-start.2 = (bf16[112,384]{1,0:T(8,128)(2,1)}, bf16[112,384]{1,0:T(8,128)(2,1)S(1)}, u32[]{:S(2)}) copy-start(bf16[112,384]{1,0:T(8,128)(2,1)S(1)} %collective-permute-done.26.refs_3_) | copy-start | bytes 258052
  75.8 9.1 %collective-permute-start.12 = (bf16[112,128]{1,0:T(8,128)(2,1)}, bf16[112,128]{1,0:T(8,128)(2,1)S(1)}, u32[]{:S(2)}, u32[]{:S(2)}) collective-permute-start(bf16[112,128]{1,0:T(8,128)(2,1)} %get-tuple-element.53), channel_id=1, source_target_pairs={{0,8},{4,12},{8,16},{12,20},{16,24},{20,28},{24,0},{28,4},{1,9},{5... | collective-permute-start | bytes 86024 | tf_op jit(solution)/shard_map/ppermute | solution.py:46
  78.5 4.8 %copy-start.3 = (bf16[112,384]{1,0:T(8,128)(2,1)}, bf16[112,384]{1,0:T(8,128)(2,1)S(1)}, u32[]{:S(2)}) copy-start(bf16[112,384]{1,0:T(8,128)(2,1)S(1)} %collective-permute-done.27.refs_4_) | copy-start | bytes 258052
  78.5 8.0 %collective-permute-start.13 = (bf16[112,128]{1,0:T(8,128)(2,1)}, bf16[112,128]{1,0:T(8,128)(2,1)S(1)}, u32[]{:S(2)}, u32[]{:S(2)}) collective-permute-start(bf16[112,128]{1,0:T(8,128)(2,1)} %get-tuple-element.54), channel_id=1, source_target_pairs={{0,12},{4,8},{8,20},{12,16},{16,28},{20,24},{24,4},{28,0},{1,13},{... | collective-permute-start | bytes 86024 | tf_op jit(solution)/shard_map/ppermute | solution.py:46
  78.5 4.7 %copy-start.4 = (bf16[112,384]{1,0:T(8,128)(2,1)}, bf16[112,384]{1,0:T(8,128)(2,1)S(1)}, u32[]{:S(2)}) copy-start(bf16[112,384]{1,0:T(8,128)(2,1)S(1)} %collective-permute-done.28.refs_5_) | copy-start | bytes 258052
  78.5 9.5 %collective-permute-start.14 = (bf16[112,128]{1,0:T(8,128)(2,1)}, bf16[112,128]{1,0:T(8,128)(2,1)S(1)}, u32[]{:S(2)}, u32[]{:S(2)}) collective-permute-start(bf16[112,128]{1,0:T(8,128)(2,1)} %get-tuple-element.55), channel_id=1, source_target_pairs={{0,24},{4,28},{8,0},{12,4},{16,8},{20,12},{24,16},{28,20},{1,25},{... | collective-permute-start | bytes 86024 | tf_op jit(solution)/shard_map/ppermute | solution.py:46
  81.0 8.4 %collective-permute-start.15 = (bf16[112,128]{1,0:T(8,128)(2,1)}, bf16[112,128]{1,0:T(8,128)(2,1)S(1)}, u32[]{:S(2)}, u32[]{:S(2)}) collective-permute-start(bf16[112,128]{1,0:T(8,128)(2,1)} %get-tuple-element.56), channel_id=1, source_target_pairs={{0,28},{4,24},{8,4},{12,0},{16,12},{20,8},{24,20},{28,16},{1,29},{... | collective-permute-start | bytes 86024 | tf_op jit(solution)/shard_map/ppermute | solution.py:46
  82.5 7.0 %collective-permute-start.16 = (bf16[112,128]{1,0:T(8,128)(2,1)}, bf16[112,128]{1,0:T(8,128)(2,1)S(1)}, u32[]{:S(2)}, u32[]{:S(2)}) collective-permute-start(bf16[112,128]{1,0:T(8,128)(2,1)} %get-tuple-element.57), channel_id=1, source_target_pairs={{0,4},{4,0},{8,12},{12,8},{16,20},{20,16},{24,28},{28,24},{1,5},{5... | collective-permute-start | bytes 86024 | tf_op jit(solution)/shard_map/ppermute | solution.py:46
  84.8 4.6 %copy-start.17 = (bf16[112,128]{1,0:T(8,128)(2,1)}, bf16[112,128]{1,0:T(8,128)(2,1)S(1)}, u32[]{:S(2)}) copy-start(bf16[112,128]{1,0:T(8,128)(2,1)S(1)} %collective-permute-done.12.refs_3_) | copy-start | bytes 86020
  84.8 16.1 %collective-permute-start.31 = (f32[4,4,768]{2,1,0:T(4,128)}, f32[4,4,768]{2,1,0:T(4,128)S(1)}, u32[]{:S(2)}, u32[]{:S(2)}) collective-permute-start(f32[4,4,768]{2,1,0:T(4,128)} %get-tuple-element.75), channel_id=1, source_target_pairs={{0,1},{1,2},{2,3},{3,0},{4,5},{5,6},{6,7},{7,4},{8,9},{9,10},{10,1... | collective-permute-start | bytes 147464 | tf_op jit(solution)/shard_map/ppermute | solution.py:285
  86.5 14.4 %collective-permute-start.32 = (f32[4,4,768]{2,1,0:T(4,128)}, f32[4,4,768]{2,1,0:T(4,128)S(1)}, u32[]{:S(2)}, u32[]{:S(2)}) collective-permute-start(f32[4,4,768]{2,1,0:T(4,128)} %get-tuple-element.76), channel_id=1, source_target_pairs={{0,2},{1,3},{2,0},{3,1},{4,6},{5,7},{6,4},{7,5},{8,10},{9,11},{10,... | collective-permute-start | bytes 147464 | tf_op jit(solution)/shard_map/ppermute | solution.py:285
  88.0 12.9 %collective-permute-start.33 = (f32[4,4,768]{2,1,0:T(4,128)}, f32[4,4,768]{2,1,0:T(4,128)S(1)}, u32[]{:S(2)}, u32[]{:S(2)}) collective-permute-start(f32[4,4,768]{2,1,0:T(4,128)} %get-tuple-element.77), channel_id=1, source_target_pairs={{0,3},{1,0},{2,1},{3,2},{4,7},{5,4},{6,5},{7,6},{8,11},{9,8},{10,9... | collective-permute-start | bytes 147464 | tf_op jit(solution)/shard_map/ppermute | solution.py:285
  91.4 4.8 %collective-permute-start.34 = (f32[4,4,256]{2,1,0:T(4,128)}, f32[4,4,256]{2,1,0:T(4,128)S(1)}, u32[]{:S(2)}, u32[]{:S(2)}) collective-permute-start(f32[4,4,256]{2,1,0:T(4,128)} %get-tuple-element.79), channel_id=1, source_target_pairs={{0,1},{1,2},{2,3},{3,0},{4,5},{5,6},{6,7},{7,4},{8,9},{9,10},{10,1... | collective-permute-start | bytes 49160 | tf_op jit(solution)/shard_map/ppermute | solution.py:285
  92.0 8.8 %collective-permute-start.35 = (f32[4,4,256]{2,1,0:T(4,128)}, f32[4,4,256]{2,1,0:T(4,128)S(1)}, u32[]{:S(2)}, u32[]{:S(2)}) collective-permute-start(f32[4,4,256]{2,1,0:T(4,128)} %get-tuple-element.80), channel_id=1, source_target_pairs={{0,2},{1,3},{2,0},{3,1},{4,6},{5,7},{6,4},{7,5},{8,10},{9,11},{10,... | collective-permute-start | bytes 49160 | tf_op jit(solution)/shard_map/ppermute | solution.py:285
  96.3 4.6 %collective-permute-start.36 = (f32[4,4,256]{2,1,0:T(4,128)}, f32[4,4,256]{2,1,0:T(4,128)S(1)}, u32[]{:S(2)}, u32[]{:S(2)}) collective-permute-start(f32[4,4,256]{2,1,0:T(4,128)} %get-tuple-element.81), channel_id=1, source_target_pairs={{0,3},{1,0},{2,1},{3,2},{4,7},{5,4},{6,5},{7,6},{8,11},{9,8},{10,9... | collective-permute-start | bytes 49160 | tf_op jit(solution)/shard_map/ppermute | solution.py:285
  (20 other events, 27.4 us)

commit v2 on v0

--- a/solution.py
+++ b/solution.py
@@ -25,31 +25,16 @@
 
 
 def messages(n):
-    nz = n // 2
-    steps = sorted(range(nz), key=lambda d: (-min(d, nz - d), d))
-    return [(d, c) for d in steps for c in range(2) if (d, c) != (0, 0)]
-
-
-def target(s, n, message, sign=1):
-    nz = n // 2
-    step, flip = message
-    if isinstance(s, int):
-        half, core = divmod(s, 2)
-        chip = (half + (step if sign > 0 else nz - step)) % nz
-    else:
-        half, core = lax.div(s, 2), lax.rem(s, 2)
-        chip = lax.rem(half + (step if sign > 0 else nz - step), nz)
-    return 2 * chip + (1 - core if flip else core)
-
-
-def send(block, n, message):
-    pairs = [(s, target(s, n, message)) for s in range(n)]
-    return lax.ppermute(block, "seq", pairs)
-
-
-def places(n, sign=1):
+    return [*range(n // 2, n), *range(2, n // 2), 1]
+
+
+def send(block, axis, n, message):
+    return lax.ppermute(block, axis, [(s, s ^ message) for s in range(n)])
+
+
+def places(n):
     me = lax.axis_index("seq")
-    return [me] + [target(me, n, m, sign) for m in messages(n)]
+    return [me] + [lax.bitwise_xor(me, jnp.int32(m)) for m in messages(n)]
 
 
 def interleave_matrix(rows):
@@ -87,10 +72,11 @@
     q_ref, k_ref, v_ref, x_ref, y_ref, g_ref, a_ref, qg, kg, vg, wg_ref = refs[2 * n :]
     length, width = q_ref.shape
     rows = rc * POOL
-    place, goal = places(n, -1), places(n)
+    place = places(n)
+    goal = place
     me, col, share = lax.axis_index("seq"), lax.axis_index("dp"), n // nd
     w = weight[
-        lax.rem(col - lax.div(me, share) + nd, nd),
+        lax.bitwise_xor(col, lax.div(me, share)),
         :,
         pl.ds(pl.multiple_of(lax.rem(me, share) * wide + first, HEAD_DIM), width),
     ]
@@ -172,7 +158,7 @@
 
 def collect_kernel(n, nd, wide, *refs):
     blocks, outs, held = refs[: -nd - 1], refs[-nd - 1 : -1], refs[-1]
-    place, col, share = places(n, -1), lax.axis_index("dp"), n // nd
+    place, col, share = places(n), lax.axis_index("dp"), n // nd
     cw = blocks[0].shape[1]
     for c in range(len(blocks) // n):
         for i in range(n):
@@ -181,12 +167,12 @@
             for t in range(KINDS):
                 held[lax.div(place[i], share), t, :, cols] = part[t * POOL : (t + 1) * POOL]
     for k in range(nd):
-        outs[k][...] = held[lax.rem(col + k, nd)]
+        outs[k][...] = held[lax.bitwise_xor(col, jnp.int32(k))]
 
 
 def spread_kernel(n, nd, wide, weight, *refs):
     blocks, out = refs[:-1], refs[-1]
-    place, col, share = places(n, -1), lax.axis_index("dp"), n // nd
+    place, col, share = places(n), lax.axis_index("dp"), n // nd
     rc = out.shape[0] // POOL
     cw = blocks[0].shape[1]
     sel = interleave_matrix(rc * POOL)
@@ -195,7 +181,7 @@
             ref = blocks[c * n + i]
             cols = pl.ds(pl.multiple_of(place[i] * wide + c * cw, HEAD_DIM), cw)
             w = weight[
-                lax.rem(col - lax.div(place[i], share) + nd, nd),
+                lax.bitwise_xor(col, lax.div(place[i], share)),
                 :,
                 pl.ds(pl.multiple_of(lax.rem(place[i], share) * wide + c * cw, HEAD_DIM), cw),
             ]
@@ -231,9 +217,9 @@
             out_specs=[VMEM] * n,
             scratch_shapes=[pltpu.SemaphoreType.DMA((2 * n,))],
         )(inputs, upstream)
-        arrived.append([cut[0]] + [send(b, n, m) for b, m in zip(cut[1:], todo)])
+        arrived.append([cut[0]] + [send(b, "seq", n, m) for b, m in zip(cut[1:], todo)])
     own = pool_weight.reshape(KINDS * POOL, -1)
-    pieces = [own] + [lax.ppermute(own, "dp", [(d, (d + k) % nd) for d in range(nd)]) for k in range(1, nd)]
+    pieces = [own] + [send(own, "dp", nd, k) for k in range(1, nd)]
     weights = jnp.stack(pieces)
 
     back = []
@@ -250,7 +236,7 @@
             + [full(F32)] * 3
             + [pltpu.VMEM((KINDS * POOL, cw), F32)],
         )(weights, *arrived[c])
-        back += [made[0]] + [send(b, n, m) for b, m in zip(made[1:], todo)]
+        back += [made[0]] + [send(b, "seq", n, m) for b, m in zip(made[1:], todo)]
 
     tail = pl.BlockSpec((KINDS * POOL, cw), lambda i: (3 * rc // (KINDS * POOL), 0))
     owned = (KINDS, POOL, width // nd)
@@ -265,7 +251,7 @@
     )(*back)
     weight_grad = shares[0]
     for k in range(1, nd):
-        weight_grad = weight_grad + lax.ppermute(shares[k], "dp", [(d, (d + k) % nd) for d in range(nd)])
+        weight_grad = weight_grad + send(shares[k], "dp", nd, k)
     input_grad = pl.pallas_call(
         functools.partial(spread_kernel, n, nd, wide),
         out_shape=shape((rows, width), BF16),
@@ -277,7 +263,7 @@
 
 def solution(mesh):
     n, nd = mesh.shape["seq"], mesh.shape["dp"]
-    if n % 2 or n % nd:
+    if n < 4 or n & (n - 1) or n % nd:
         raise ValueError("unsupported mesh")
     placed = (P("dp", "seq", None), P("dp", "seq", None), P(None, None, "dp"))
 

time: 94.2 us -> 93.7 us (level)
  starting transfers between devices: 45.2 us -> 43.9 us
    ppermute x34, starting transfers between devices: 45.2 us -> 43.9 us  [send(): return lax.ppermute(block, axis, [(s, s ^ message) for s in range(n)])]
where the time goes in v2:
time: 93.7 us; the launch traced here: 93.3 us
  starting transfers between devices  43.9 us (47%)
  waiting for transfers between devices  26.8 us (29%)
  Pallas kernels  18.1 us (19%)
  local copies, waits for them, and re-layouts  2.15 us (2%)
  other arithmetic  1.37 us (1%)
  between operations  0.94 us (1%)
    ppermute x34, starting transfers between devices, send(): return lax.ppermute(block, axis, [(s, s ^ message) for s in range(n)])  43.9 us
    ppermute x34, waiting for transfers between devices, send(): return lax.ppermute(block, axis, [(s, s ^ message) for s in range(n)])  26.8 us
    pallas_call x2, Pallas kernels, per_device(): pl.pallas_call(functools.partial(block_kernel, n, nd, rc, wide, c * cw),...  8.76 us
    pallas_call x2, Pallas kernels, per_device(): pl.pallas_call(functools.partial(cut_kernel, n, wide, c * cw), out_shape=...  4.73 us
    pallas_call x1, Pallas kernels, per_device(): pl.pallas_call(functools.partial(spread_kernel, n, nd, wide), out_shape=s...  3.03 us
  transfers between devices with their start and end apart: 34, of which 10 were waited for; matrix products, arithmetic and copies ran while one was open for 1% of the time, Pallas kernels for 18%

profile of v2, /device:TPU:0, one launch (start us, length us, event | category | flops | bytes accessed | tf_op | source)
XLA Modules:
  0.0 93.3 jit_solution(13473787713442663632)
XLA Ops:
  0.6 0.9 reshape.7
  1.5 4.0 %collective-permute-start.2 = (f32[16,1024]{1,0:T(8,128)S(1)}, f32[16,1024]{1,0:T(8,128)S(1)}, u32[]{:S(2)}, u32[]{:S(2)}) collective-permute-start(f32[16,1024]{1,0:T(8,128)S(1)} %reshape.7), channel_id=1, source_target_pairs={{0,3},{1,2},{2,1},{3,0},{4,7},{5,6},{6,5},{7,4},{8,11},{9,10},{10,... | collective-permute-start | bytes 196616 | tf_op jit(solution)/shard_map/ppermute | solution.py:32
  5.5 0.5 collective-permute-start.1
  6.0 2.3 %shard_map.50 = (bf16[256,256]{1,0:T(8,128)(2,1)}, bf16[256,256]{1,0:T(8,128)(2,1)}, bf16[256,256]{1,0:T(8,128)(2,1)}, bf16[256,256]{1,0:T(8,128)(2,1)}, bf16[25...) custom-call(bf16[128,4096]{1,0:T(8,128)(2,1)} %bitcast.11, ...), custom_call_target="tpu_custom_call" | custom-call | tf_op jit(solution)/shard_map/pallas_call | solution.py:213
  8.3 2.7 %collective-permute-start.3 = (bf16[256,256]{1,0:T(8,128)(2,1)}, bf16[256,256]{1,0:T(8,128)(2,1)S(1)}, u32[]{:S(2)}, u32[]{:S(2)}) collective-permute-start(bf16[256,256]{1,0:T(8,128)(2,1)} %get-tuple-element.39), channel_id=1, source_target_pairs={{0,16},{4,20},{8,24},{12,28},{16,0},{20,4},{24,8},{28,12},{1,17},{... | collective-permute-start | bytes 393224 | tf_op jit(solution)/shard_map/ppermute | solution.py:32
  11.0 2.5 %collective-permute-start.5 = (bf16[256,256]{1,0:T(8,128)(2,1)}, bf16[256,256]{1,0:T(8,128)(2,1)S(1)}, u32[]{:S(2)}, u32[]{:S(2)}) collective-permute-start(bf16[256,256]{1,0:T(8,128)(2,1)} %get-tuple-element.41), channel_id=1, source_target_pairs={{0,24},{4,28},{8,16},{12,20},{16,8},{20,12},{24,0},{28,4},{1,25},{... | collective-permute-start | bytes 393224 | tf_op jit(solution)/shard_map/ppermute | solution.py:32
  13.5 0.0 collective-permute-done.2
  13.5 0.0 copy-start
  13.6 1.2 %collective-permute-start.6 = (bf16[256,256]{1,0:T(8,128)(2,1)}, bf16[256,256]{1,0:T(8,128)(2,1)S(1)}, u32[]{:S(2)}, u32[]{:S(2)}) collective-permute-start(bf16[256,256]{1,0:T(8,128)(2,1)} %get-tuple-element.42), channel_id=1, source_target_pairs={{0,28},{4,24},{8,20},{12,16},{16,12},{20,8},{24,4},{28,0},{1,29},{... | collective-permute-start | bytes 393224 | tf_op jit(solution)/shard_map/ppermute | solution.py:32
  14.8 0.5 collective-permute-start
  15.3 2.4 %shard_map.52 = (bf16[256,256]{1,0:T(8,128)(2,1)}, bf16[256,256]{1,0:T(8,128)(2,1)}, bf16[256,256]{1,0:T(8,128)(2,1)}, bf16[256,256]{1,0:T(8,128)(2,1)}, bf16[25...) custom-call(bf16[128,4096]{1,0:T(8,128)(2,1)} %bitcast.12, ...), custom_call_target="tpu_custom_call" | custom-call | tf_op jit(solution)/shard_map/pallas_call | solution.py:213
  17.7 1.3 %collective-permute-done = f32[16,1024]{1,0:T(8,128)S(1)} collective-permute-done((f32[16,1024]{1,0:T(8,128)S(1)}, f32[16,1024]{1,0:T(8,128)S(1)}, u32[]{:S(2)}, u32[]{:S(2)}) %collective-permute-start) | collective-permute-done | bytes 65568 | tf_op jit(solution)/shard_map/ppermute | solution.py:32
  19.0 0.0 collective-permute-start.7
  19.0 7.6 %collective-permute-done.3.refs_1_ = bf16[256,256]{1,0:T(8,128)(2,1)S(1)} collective-permute-done((bf16[256,256]{1,0:T(8,128)(2,1)}, bf16[256,256]{1,0:T(8,128)(2,1)S(1)}, u32[]{:S(2)}, u32[]{:S(2)}) %collective-permute-start.3) | collective-permute-done | bytes 131104 | tf_op jit(solution)/shard_map/ppermute | solution.py:32
  26.6 0.0 collective-permute-start.8
  26.6 0.6 collective-permute-done.4.refs_2_
  27.2 2.0 %collective-permute-start.9 = (bf16[256,256]{1,0:T(8,128)(2,1)S(1)}, bf16[256,256]{1,0:T(8,128)(2,1)S(1)}, u32[]{:S(2)}, u32[]{:S(2)}) collective-permute-start(bf16[256,256]{1,0:T(8,128)(2,1)S(1)} %copy-done.31), channel_id=1, source_target_pairs={{0,4},{4,0},{8,12},{12,8},{16,20},{20,16},{24,28},{28,24},{1,5},{5... | collective-permute-start | bytes 393224 | tf_op jit(solution)/shard_map/ppermute | solution.py:32
  29.2 4.6 %collective-permute-start.17 = (bf16[256,256]{1,0:T(8,128)(2,1)}, bf16[256,256]{1,0:T(8,128)(2,1)S(1)}, u32[]{:S(2)}, u32[]{:S(2)}) collective-permute-start(bf16[256,256]{1,0:T(8,128)(2,1)} %get-tuple-element.55), channel_id=1, source_target_pairs={{0,16},{4,20},{8,24},{12,28},{16,0},{20,4},{24,8},{28,12},{1,17},{... | collective-permute-start | bytes 393224 | tf_op jit(solution)/shard_map/ppermute | solution.py:32
  33.8 2.3 %collective-permute-start.18 = (bf16[256,256]{1,0:T(8,128)(2,1)}, bf16[256,256]{1,0:T(8,128)(2,1)S(1)}, u32[]{:S(2)}, u32[]{:S(2)}) collective-permute-start(bf16[256,256]{1,0:T(8,128)(2,1)} %get-tuple-element.56), channel_id=1, source_target_pairs={{0,20},{4,16},{8,28},{12,24},{16,4},{20,0},{24,12},{28,8},{1,21},{... | collective-permute-start | bytes 393224 | tf_op jit(solution)/shard_map/ppermute | solution.py:32
  36.1 0.6 collective-permute-start.19
  36.7 3.0 %collective-permute-start.20 = (bf16[256,256]{1,0:T(8,128)(2,1)}, bf16[256,256]{1,0:T(8,128)(2,1)S(1)}, u32[]{:S(2)}, u32[]{:S(2)}) collective-permute-start(bf16[256,256]{1,0:T(8,128)(2,1)} %get-tuple-element.58), channel_id=1, source_target_pairs={{0,28},{4,24},{8,20},{12,16},{16,12},{20,8},{24,4},{28,0},{1,29},{... | collective-permute-start | bytes 393224 | tf_op jit(solution)/shard_map/ppermute | solution.py:32
  39.7 9.6 %collective-permute-done.17.refs_1_ = bf16[256,256]{1,0:T(8,128)(2,1)S(1)} collective-permute-done((bf16[256,256]{1,0:T(8,128)(2,1)}, bf16[256,256]{1,0:T(8,128)(2,1)S(1)}, u32[]{:S(2)}, u32[]{:S(2)}) %collective-permute-start.17) | collective-permute-done | bytes 131104 | tf_op jit(solution)/shard_map/ppermute | solution.py:32
  49.3 2.0 %collective-permute-done.18.refs_2_ = bf16[256,256]{1,0:T(8,128)(2,1)S(1)} collective-permute-done((bf16[256,256]{1,0:T(8,128)(2,1)}, bf16[256,256]{1,0:T(8,128)(2,1)S(1)}, u32[]{:S(2)}, u32[]{:S(2)}) %collective-permute-start.18) | collective-permute-done | bytes 131104 | tf_op jit(solution)/shard_map/ppermute | solution.py:32
  51.3 0.5 collective-permute-start.23
  51.8 0.7 pad_maximum_fusion.weight
  52.6 4.4 %shard_map.51 = (bf16[112,256]{1,0:T(8,128)(2,1)}, bf16[112,256]{1,0:T(8,128)(2,1)}, bf16[112,256]{1,0:T(8,128)(2,1)}, bf16[112,256]{1,0:T(8,128)(2,1)}, bf16[11...) custom-call(f32[4,16,1024]{2,1,0:T(8,128)} %pad_maximum_fusion.weight, ...), custom_call_target="tpu_custom_call" | custom-call | tf_op jit(solution)/shard_map/pallas_call | solution.py:228
  57.0 0.0 collective-permute-done.19.refs_3_
  57.0 0.0 copy-start.21
  57.0 0.7 collective-permute-start.10
  57.6 0.0 collective-permute-done.20.refs_4_
  57.7 1.7 %collective-permute-start.11 = (bf16[112,256]{1,0:T(8,128)(2,1)}, bf16[112,256]{1,0:T(8,128)(2,1)S(1)}, u32[]{:S(2)}, u32[]{:S(2)}) collective-permute-start(bf16[112,256]{1,0:T(8,128)(2,1)} %get-tuple-element.48), channel_id=1, source_target_pairs={{0,20},{4,16},{8,28},{12,24},{16,4},{20,0},{24,12},{28,8},{1,21},{... | collective-permute-start | bytes 172040 | tf_op jit(solution)/shard_map/ppermute | solution.py:32
  59.4 0.0 collective-permute-done.21.refs_5_
  59.4 2.9 %collective-permute-start.12 = (bf16[112,256]{1,0:T(8,128)(2,1)}, bf16[112,256]{1,0:T(8,128)(2,1)S(1)}, u32[]{:S(2)}, u32[]{:S(2)}) collective-permute-start(bf16[112,256]{1,0:T(8,128)(2,1)} %get-tuple-element.49), channel_id=1, source_target_pairs={{0,24},{4,28},{8,16},{12,20},{16,8},{20,12},{24,0},{28,4},{1,25},{... | collective-permute-start | bytes 172040 | tf_op jit(solution)/shard_map/ppermute | solution.py:32
  62.2 0.0 collective-permute-done.22.refs_6_
  62.2 1.0 %collective-permute-start.13 = (bf16[112,256]{1,0:T(8,128)(2,1)}, bf16[112,256]{1,0:T(8,128)(2,1)S(1)}, u32[]{:S(2)}, u32[]{:S(2)}) collective-permute-start(bf16[112,256]{1,0:T(8,128)(2,1)} %get-tuple-element.50), channel_id=1, source_target_pairs={{0,28},{4,24},{8,20},{12,16},{16,12},{20,8},{24,4},{28,0},{1,29},{... | collective-permute-start | bytes 172040 | tf_op jit(solution)/shard_map/ppermute | solution.py:32
  63.3 0.0 collective-permute-start.14
  63.3 0.6 copy-done.27
  63.9 4.4 %shard_map.53 = (bf16[112,256]{1,0:T(8,128)(2,1)}, bf16[112,256]{1,0:T(8,128)(2,1)}, bf16[112,256]{1,0:T(8,128)(2,1)}, bf16[112,256]{1,0:T(8,128)(2,1)}, bf16[11...) custom-call(f32[4,16,1024]{2,1,0:T(8,128)} %pad_maximum_fusion.weight, ...), custom_call_target="tpu_custom_call" | custom-call | tf_op jit(solution)/shard_map/pallas_call | solution.py:228
  68.3 0.0 collective-permute-done.10.refs_1_
  68.3 0.9 collective-permute-start.15
  69.2 0.8 collective-permute-start.16
  70.0 1.6 %collective-permute-start.24 = (bf16[112,256]{1,0:T(8,128)(2,1)}, bf16[112,256]{1,0:T(8,128)(2,1)S(1)}, u32[]{:S(2)}, u32[]{:S(2)}) collective-permute-start(bf16[112,256]{1,0:T(8,128)(2,1)} %get-tuple-element.63), channel_id=1, source_target_pairs={{0,16},{4,20},{8,24},{12,28},{16,0},{20,4},{24,8},{28,12},{1,17},{... | collective-permute-start | bytes 172040 | tf_op jit(solution)/shard_map/ppermute | solution.py:32
  71.7 0.0 collective-permute-done.13.refs_4_
  71.7 0.7 collective-permute-start.25
  72.4 0.0 collective-permute-done.14.refs_5_
  72.4 2.5 %collective-permute-start.26 = (bf16[112,256]{1,0:T(8,128)(2,1)}, bf16[112,256]{1,0:T(8,128)(2,1)S(1)}, u32[]{:S(2)}, u32[]{:S(2)}) collective-permute-start(bf16[112,256]{1,0:T(8,128)(2,1)} %get-tuple-element.65), channel_id=1, source_target_pairs={{0,24},{4,28},{8,16},{12,20},{16,8},{20,12},{24,0},{28,4},{1,25},{... | collective-permute-start | bytes 172040 | tf_op jit(solution)/shard_map/ppermute | solution.py:32
  74.9 1.3 %collective-permute-start.27 = (bf16[112,256]{1,0:T(8,128)(2,1)}, bf16[112,256]{1,0:T(8,128)(2,1)S(1)}, u32[]{:S(2)}, u32[]{:S(2)}) collective-permute-start(bf16[112,256]{1,0:T(8,128)(2,1)} %get-tuple-element.66), channel_id=1, source_target_pairs={{0,28},{4,24},{8,20},{12,16},{16,12},{20,8},{24,4},{28,0},{1,29},{... | collective-permute-start | bytes 172040 | tf_op jit(solution)/shard_map/ppermute | solution.py:32
  76.3 0.0 collective-permute-done.16.refs_7_
  76.3 0.0 collective-permute-start.28
  76.3 3.0 %collective-permute-done.24.refs_9_ = bf16[112,256]{1,0:T(8,128)(2,1)S(1)} collective-permute-done((bf16[112,256]{1,0:T(8,128)(2,1)}, bf16[112,256]{1,0:T(8,128)(2,1)S(1)}, u32[]{:S(2)}, u32[]{:S(2)}) %collective-permute-start.24) | collective-permute-done | bytes 57376 | tf_op jit(solution)/shard_map/ppermute | solution.py:32
  79.2 0.3 collective-permute-done.25.refs_10_
  79.6 1.9 %collective-permute-start.30 = (bf16[112,256]{1,0:T(8,128)(2,1)}, bf16[112,256]{1,0:T(8,128)(2,1)S(1)}, u32[]{:S(2)}, u32[]{:S(2)}) collective-permute-start(bf16[112,256]{1,0:T(8,128)(2,1)} %get-tuple-element.69), channel_id=1, source_target_pairs={{0,4},{4,0},{8,12},{12,8},{16,20},{20,16},{24,28},{28,24},{1,5},{5... | collective-permute-start | bytes 172040 | tf_op jit(solution)/shard_map/ppermute | solution.py:32
  81.5 1.0 %collective-permute-done.28.refs_13_ = bf16[112,256]{1,0:T(8,128)(2,1)S(1)} collective-permute-done((bf16[112,256]{1,0:T(8,128)(2,1)}, bf16[112,256]{1,0:T(8,128)(2,1)S(1)}, u32[]{:S(2)}, u32[]{:S(2)}) %collective-permute-start.28) | collective-permute-done | bytes 57376 | tf_op jit(solution)/shard_map/ppermute | solution.py:32
  82.5 1.2 %collective-permute-done.29.refs_14_ = bf16[112,256]{1,0:T(8,128)(2,1)S(1)} collective-permute-done((bf16[112,256]{1,0:T(8,128)(2,1)}, bf16[112,256]{1,0:T(8,128)(2,1)S(1)}, u32[]{:S(2)}, u32[]{:S(2)}) %collective-permute-start.29) | collective-permute-done | bytes 57376 | tf_op jit(solution)/shard_map/ppermute | solution.py:32
  83.8 0.5 copy-done.13
  84.3 0.0 copy-done.14
  84.3 1.6 %shard_map.55 = (f32[4,4,1024]{2,1,0:T(4,128)}, f32[4,4,1024]{2,1,0:T(4,128)}, f32[4,4,1024]{2,1,0:T(4,128)}, f32[4,4,1024]{2,1,0:T(4,128)}) custom-call(bf16[112,256]{1,0:T(8,128)(2,1)} %get-tuple-element.46.refs_0_, bf16[112,256]{1,0:T(8,128)(2,1)} %copy-done.1, bf16[112,256]{1,0:T(8,128)(2,1)} %copy-done.2, bf16[112,256]{1,0:T(8,128)(2,1)} %copy-done.3, ...), custom_call_target="tpu_custom_call" | custom-call | tf_op jit(solution)/shard_map/pallas_call | solution.py:244
  85.9 1.5 %collective-permute-start.33 = (f32[4,4,1024]{2,1,0:T(4,128)}, f32[4,4,1024]{2,1,0:T(4,128)S(1)}, u32[]{:S(2)}, u32[]{:S(2)}) collective-permute-start(f32[4,4,1024]{2,1,0:T(4,128)} %get-tuple-element.73), channel_id=1, source_target_pairs={{0,3},{1,2},{2,1},{3,0},{4,7},{5,6},{6,5},{7,4},{8,11},{9,10},{10,... | collective-permute-start | bytes 196616 | tf_op jit(solution)/shard_map/ppermute | solution.py:32
  87.4 0.5 collective-permute-start.32
  88.0 1.5 %collective-permute-start.31 = (f32[4,4,1024]{2,1,0:T(4,128)}, f32[4,4,1024]{2,1,0:T(4,128)S(1)}, u32[]{:S(2)}, u32[]{:S(2)}) collective-permute-start(f32[4,4,1024]{2,1,0:T(4,128)} %get-tuple-element.71), channel_id=1, source_target_pairs={{0,1},{1,0},{2,3},{3,2},{4,5},{5,4},{6,7},{7,6},{8,9},{9,8},{10,11... | collective-permute-start | bytes 196616 | tf_op jit(solution)/shard_map/ppermute | solution.py:32
  89.4 3.0 %shard_map.54 = bf16[128,4096]{1,0:T(8,128)(2,1)} custom-call(f32[4,16,1024]{2,1,0:T(8,128)} %pad_maximum_fusion.weight, bf16[112,256]{1,0:T(8,128)(2,1)} %get-tuple-element.46.refs_0_, bf16[112,256]{1,0:T(8,128)(2,1)} %copy-done.1, bf16[112,256]{1,0:T(8,128)(2,1)} %copy-done.2, bf16[112,256]{1,0:T(8,128)(2,1)} %copy-done.3, bf16[112,256]{1,0:T(8,128)(2,1)} %copy-done.4, ...), custom_call_target="tpu_custom_call" | custom-call | tf_op jit(solution)/shard_map/pallas_call | solution.py:255
  92.5 0.1 collective-permute-done.32
  92.6 0.0 collective-permute-done.31
  92.6 0.6 add_add_fusion
  (86 shorter events, 0.2 us)
Async XLA Ops:
  1.5 12.0 %collective-permute-start.2 = (f32[16,1024]{1,0:T(8,128)S(1)}, f32[16,1024]{1,0:T(8,128)S(1)}, u32[]{:S(2)}, u32[]{:S(2)}) collective-permute-start(f32[16,1024]{1,0:T(8,128)S(1)} %reshape.7), channel_id=1, source_target_pairs={{0,3},{1,2},{2,1},{3,0},{4,7},{5,6},{6,5},{7,4},{8,11},{9,10},{10,... | collective-permute-start | bytes 196616 | tf_op jit(solution)/shard_map/ppermute | solution.py:32
  5.5 9.3 %collective-permute-start.1 = (f32[16,1024]{1,0:T(8,128)S(1)}, f32[16,1024]{1,0:T(8,128)S(1)}, u32[]{:S(2)}, u32[]{:S(2)}) collective-permute-start(f32[16,1024]{1,0:T(8,128)S(1)} %reshape.7), channel_id=1, source_target_pairs={{0,2},{1,3},{2,0},{3,1},{4,6},{5,7},{6,4},{7,5},{8,10},{9,11},{10,... | collective-permute-start | bytes 196616 | tf_op jit(solution)/shard_map/ppermute | solution.py:32
  8.3 18.3 %collective-permute-start.3 = (bf16[256,256]{1,0:T(8,128)(2,1)}, bf16[256,256]{1,0:T(8,128)(2,1)S(1)}, u32[]{:S(2)}, u32[]{:S(2)}) collective-permute-start(bf16[256,256]{1,0:T(8,128)(2,1)} %get-tuple-element.39), channel_id=1, source_target_pairs={{0,16},{4,20},{8,24},{12,28},{16,0},{20,4},{24,8},{28,12},{1,17},{... | collective-permute-start | bytes 393224 | tf_op jit(solution)/shard_map/ppermute | solution.py:32
  11.0 16.2 %collective-permute-start.4 = (bf16[256,256]{1,0:T(8,128)(2,1)}, bf16[256,256]{1,0:T(8,128)(2,1)S(1)}, u32[]{:S(2)}, u32[]{:S(2)}) collective-permute-start(bf16[256,256]{1,0:T(8,128)(2,1)} %get-tuple-element.40), channel_id=1, source_target_pairs={{0,20},{4,16},{8,28},{12,24},{16,4},{20,0},{24,12},{28,8},{1,21},{... | collective-permute-start | bytes 393224 | tf_op jit(solution)/shard_map/ppermute | solution.py:32
  11.0 18.2 %collective-permute-start.5 = (bf16[256,256]{1,0:T(8,128)(2,1)}, bf16[256,256]{1,0:T(8,128)(2,1)S(1)}, u32[]{:S(2)}, u32[]{:S(2)}) collective-permute-start(bf16[256,256]{1,0:T(8,128)(2,1)} %get-tuple-element.41), channel_id=1, source_target_pairs={{0,24},{4,28},{8,16},{12,20},{16,8},{20,12},{24,0},{28,4},{1,25},{... | collective-permute-start | bytes 393224 | tf_op jit(solution)/shard_map/ppermute | solution.py:32
  13.5 5.5 %copy-start.33 = (bf16[256,256]{1,0:T(8,128)(2,1)S(1)}, bf16[256,256]{1,0:T(8,128)(2,1)}, u32[]{:S(2)}) copy-start(bf16[256,256]{1,0:T(8,128)(2,1)} %get-tuple-element.43) | copy-start | bytes 393220
  13.5 13.1 %copy-start.32 = (bf16[256,256]{1,0:T(8,128)(2,1)S(1)}, bf16[256,256]{1,0:T(8,128)(2,1)}, u32[]{:S(2)}) copy-start(bf16[256,256]{1,0:T(8,128)(2,1)} %get-tuple-element.44) | copy-start | bytes 393220
  13.5 13.7 %copy-start.31 = (bf16[256,256]{1,0:T(8,128)(2,1)S(1)}, bf16[256,256]{1,0:T(8,128)(2,1)}, u32[]{:S(2)}) copy-start(bf16[256,256]{1,0:T(8,128)(2,1)} %get-tuple-element.45) | copy-start | bytes 393220
  13.5 35.7 %copy-start = (f32[4,4,1024]{2,1,0:T(4,128)S(1)}, f32[4,4,1024]{2,1,0:T(4,128)}, u32[]{:S(2)}) copy-start(f32[4,4,1024]{2,1,0:T(4,128)} %param.5) | copy-start | bytes 196612
  13.6 20.2 %collective-permute-start.6 = (bf16[256,256]{1,0:T(8,128)(2,1)}, bf16[256,256]{1,0:T(8,128)(2,1)S(1)}, u32[]{:S(2)}, u32[]{:S(2)}) collective-permute-start(bf16[256,256]{1,0:T(8,128)(2,1)} %get-tuple-element.42), channel_id=1, source_target_pairs={{0,28},{4,24},{8,20},{12,16},{16,12},{20,8},{24,4},{28,0},{1,29},{... | collective-permute-start | bytes 393224 | tf_op jit(solution)/shard_map/ppermute | solution.py:32
  14.8 4.3 %collective-permute-start = (f32[16,1024]{1,0:T(8,128)S(1)}, f32[16,1024]{1,0:T(8,128)S(1)}, u32[]{:S(2)}, u32[]{:S(2)}) collective-permute-start(f32[16,1024]{1,0:T(8,128)S(1)} %reshape.7), channel_id=1, source_target_pairs={{0,1},{1,0},{2,3},{3,2},{4,5},{5,4},{6,7},{7,6},{8,9},{9,8},{10,11... | collective-permute-start | bytes 196616 | tf_op jit(solution)/shard_map/ppermute | solution.py:32
  17.7 33.6 %copy-start.30 = (bf16[256,256]{1,0:T(8,128)(2,1)S(1)}, bf16[256,256]{1,0:T(8,128)(2,1)}, u32[]{:S(2)}) copy-start(bf16[256,256]{1,0:T(8,128)(2,1)} %get-tuple-element.61) | copy-start | bytes 393220
  19.0 17.1 %collective-permute-start.7 = (bf16[256,256]{1,0:T(8,128)(2,1)S(1)}, bf16[256,256]{1,0:T(8,128)(2,1)S(1)}, u32[]{:S(2)}, u32[]{:S(2)}) collective-permute-start(bf16[256,256]{1,0:T(8,128)(2,1)S(1)} %copy-done.33), channel_id=1, source_target_pairs={{0,8},{4,12},{8,0},{12,4},{16,24},{20,28},{24,16},{28,20},{1,9},{5... | collective-permute-start | bytes 393224 | tf_op jit(solution)/shard_map/ppermute | solution.py:32
  26.6 25.9 %copy-start.15 = (bf16[256,256]{1,0:T(8,128)(2,1)}, bf16[256,256]{1,0:T(8,128)(2,1)S(1)}, u32[]{:S(2)}) copy-start(bf16[256,256]{1,0:T(8,128)(2,1)S(1)} %collective-permute-done.3.refs_1_) | copy-start | bytes 393220
  26.6 10.0 %collective-permute-start.8 = (bf16[256,256]{1,0:T(8,128)(2,1)S(1)}, bf16[256,256]{1,0:T(8,128)(2,1)S(1)}, u32[]{:S(2)}, u32[]{:S(2)}) collective-permute-start(bf16[256,256]{1,0:T(8,128)(2,1)S(1)} %copy-done.32), channel_id=1, source_target_pairs={{0,12},{4,8},{8,4},{12,0},{16,28},{20,24},{24,20},{28,16},{1,13},{... | collective-permute-start | bytes 393224 | tf_op jit(solution)/shard_map/ppermute | solution.py:32
  27.2 25.4 %copy-start.16 = (bf16[256,256]{1,0:T(8,128)(2,1)}, bf16[256,256]{1,0:T(8,128)(2,1)S(1)}, u32[]{:S(2)}) copy-start(bf16[256,256]{1,0:T(8,128)(2,1)S(1)} %collective-permute-done.4.refs_2_) | copy-start | bytes 393220
  27.2 12.4 %collective-permute-start.9 = (bf16[256,256]{1,0:T(8,128)(2,1)S(1)}, bf16[256,256]{1,0:T(8,128)(2,1)S(1)}, u32[]{:S(2)}, u32[]{:S(2)}) collective-permute-start(bf16[256,256]{1,0:T(8,128)(2,1)S(1)} %copy-done.31), channel_id=1, source_target_pairs={{0,4},{4,0},{8,12},{12,8},{16,20},{20,16},{24,28},{28,24},{1,5},{5... | collective-permute-start | bytes 393224 | tf_op jit(solution)/shard_map/ppermute | solution.py:32
  29.2 23.4 %copy-start.18 = (bf16[256,256]{1,0:T(8,128)(2,1)}, bf16[256,256]{1,0:T(8,128)(2,1)S(1)}, u32[]{:S(2)}) copy-start(bf16[256,256]{1,0:T(8,128)(2,1)S(1)} %collective-permute-done.5.refs_3_) | copy-start | bytes 393220
  29.2 20.0 %collective-permute-start.17 = (bf16[256,256]{1,0:T(8,128)(2,1)}, bf16[256,256]{1,0:T(8,128)(2,1)S(1)}, u32[]{:S(2)}, u32[]{:S(2)}) collective-permute-start(bf16[256,256]{1,0:T(8,128)(2,1)} %get-tuple-element.55), channel_id=1, source_target_pairs={{0,16},{4,20},{8,24},{12,28},{16,0},{20,4},{24,8},{28,12},{1,17},{... | collective-permute-start | bytes 393224 | tf_op jit(solution)/shard_map/ppermute | solution.py:32
  33.8 18.8 %copy-start.19 = (bf16[256,256]{1,0:T(8,128)(2,1)}, bf16[256,256]{1,0:T(8,128)(2,1)S(1)}, u32[]{:S(2)}) copy-start(bf16[256,256]{1,0:T(8,128)(2,1)S(1)} %collective-permute-done.6.refs_4_) | copy-start | bytes 393220
  33.8 17.6 %collective-permute-start.18 = (bf16[256,256]{1,0:T(8,128)(2,1)}, bf16[256,256]{1,0:T(8,128)(2,1)S(1)}, u32[]{:S(2)}, u32[]{:S(2)}) collective-permute-start(bf16[256,256]{1,0:T(8,128)(2,1)} %get-tuple-element.56), channel_id=1, source_target_pairs={{0,20},{4,16},{8,28},{12,24},{16,4},{20,0},{24,12},{28,8},{1,21},{... | collective-permute-start | bytes 393224 | tf_op jit(solution)/shard_map/ppermute | solution.py:32
  36.1 16.5 %copy-start.24 = (bf16[256,256]{1,0:T(8,128)(2,1)}, bf16[256,256]{1,0:T(8,128)(2,1)S(1)}, u32[]{:S(2)}) copy-start(bf16[256,256]{1,0:T(8,128)(2,1)S(1)} %collective-permute-done.7.refs_5_) | copy-start | bytes 393220
  36.1 20.9 %collective-permute-start.19 = (bf16[256,256]{1,0:T(8,128)(2,1)}, bf16[256,256]{1,0:T(8,128)(2,1)S(1)}, u32[]{:S(2)}, u32[]{:S(2)}) collective-permute-start(bf16[256,256]{1,0:T(8,128)(2,1)} %get-tuple-element.57), channel_id=1, source_target_pairs={{0,24},{4,28},{8,16},{12,20},{16,8},{20,12},{24,0},{28,4},{1,25},{... | collective-permute-start | bytes 393224 | tf_op jit(solution)/shard_map/ppermute | solution.py:32
  36.7 15.9 %copy-start.26 = (bf16[256,256]{1,0:T(8,128)(2,1)}, bf16[256,256]{1,0:T(8,128)(2,1)S(1)}, u32[]{:S(2)}) copy-start(bf16[256,256]{1,0:T(8,128)(2,1)S(1)} %collective-permute-done.8.refs_6_) | copy-start | bytes 393220
  36.7 21.0 %collective-permute-start.20 = (bf16[256,256]{1,0:T(8,128)(2,1)}, bf16[256,256]{1,0:T(8,128)(2,1)S(1)}, u32[]{:S(2)}, u32[]{:S(2)}) collective-permute-start(bf16[256,256]{1,0:T(8,128)(2,1)} %get-tuple-element.58), channel_id=1, source_target_pairs={{0,28},{4,24},{8,20},{12,16},{16,12},{20,8},{24,4},{28,0},{1,29},{... | collective-permute-start | bytes 393224 | tf_op jit(solution)/shard_map/ppermute | solution.py:32
  39.7 12.9 %copy-start.28 = (bf16[256,256]{1,0:T(8,128)(2,1)}, bf16[256,256]{1,0:T(8,128)(2,1)S(1)}, u32[]{:S(2)}) copy-start(bf16[256,256]{1,0:T(8,128)(2,1)S(1)} %collective-permute-done.9.refs_7_) | copy-start | bytes 393220
  39.7 19.7 %collective-permute-start.21 = (bf16[256,256]{1,0:T(8,128)(2,1)}, bf16[256,256]{1,0:T(8,128)(2,1)S(1)}, u32[]{:S(2)}, u32[]{:S(2)}) collective-permute-start(bf16[256,256]{1,0:T(8,128)(2,1)} %get-tuple-element.59), channel_id=1, source_target_pairs={{0,8},{4,12},{8,0},{12,4},{16,24},{20,28},{24,16},{28,20},{1,9},{5... | collective-permute-start | bytes 393224 | tf_op jit(solution)/shard_map/ppermute | solution.py:32
  49.3 3.3 %copy-start.17 = (bf16[256,256]{1,0:T(8,128)(2,1)}, bf16[256,256]{1,0:T(8,128)(2,1)S(1)}, u32[]{:S(2)}) copy-start(bf16[256,256]{1,0:T(8,128)(2,1)S(1)} %collective-permute-done.17.refs_1_) | copy-start | bytes 393220
  49.3 13.0 %collective-permute-start.22 = (bf16[256,256]{1,0:T(8,128)(2,1)}, bf16[256,256]{1,0:T(8,128)(2,1)S(1)}, u32[]{:S(2)}, u32[]{:S(2)}) collective-permute-start(bf16[256,256]{1,0:T(8,128)(2,1)} %get-tuple-element.60), channel_id=1, source_target_pairs={{0,12},{4,8},{8,4},{12,0},{16,28},{20,24},{24,20},{28,16},{1,13},{... | collective-permute-start | bytes 393224 | tf_op jit(solution)/shard_map/ppermute | solution.py:32
  51.3 5.6 %copy-start.20 = (bf16[256,256]{1,0:T(8,128)(2,1)}, bf16[256,256]{1,0:T(8,128)(2,1)S(1)}, u32[]{:S(2)}) copy-start(bf16[256,256]{1,0:T(8,128)(2,1)S(1)} %collective-permute-done.18.refs_2_) | copy-start | bytes 393220
  51.3 11.9 %collective-permute-start.23 = (bf16[256,256]{1,0:T(8,128)(2,1)S(1)}, bf16[256,256]{1,0:T(8,128)(2,1)S(1)}, u32[]{:S(2)}, u32[]{:S(2)}) collective-permute-start(bf16[256,256]{1,0:T(8,128)(2,1)S(1)} %copy-done.30), channel_id=1, source_target_pairs={{0,4},{4,0},{8,12},{12,8},{16,20},{20,16},{24,28},{28,24},{1,5},{5... | collective-permute-start | bytes 393224 | tf_op jit(solution)/shard_map/ppermute | solution.py:32
  57.0 6.3 %copy-start.21 = (bf16[256,256]{1,0:T(8,128)(2,1)}, bf16[256,256]{1,0:T(8,128)(2,1)S(1)}, u32[]{:S(2)}) copy-start(bf16[256,256]{1,0:T(8,128)(2,1)S(1)} %collective-permute-done.19.refs_3_) | copy-start | bytes 393220
  57.0 11.3 %collective-permute-start.10 = (bf16[112,256]{1,0:T(8,128)(2,1)}, bf16[112,256]{1,0:T(8,128)(2,1)S(1)}, u32[]{:S(2)}, u32[]{:S(2)}) collective-permute-start(bf16[112,256]{1,0:T(8,128)(2,1)} %get-tuple-element.47), channel_id=1, source_target_pairs={{0,16},{4,20},{8,24},{12,28},{16,0},{20,4},{24,8},{28,12},{1,17},{... | collective-permute-start | bytes 172040 | tf_op jit(solution)/shard_map/ppermute | solution.py:32
  57.7 5.6 %copy-start.22 = (bf16[256,256]{1,0:T(8,128)(2,1)}, bf16[256,256]{1,0:T(8,128)(2,1)S(1)}, u32[]{:S(2)}) copy-start(bf16[256,256]{1,0:T(8,128)(2,1)S(1)} %collective-permute-done.20.refs_4_) | copy-start | bytes 393220
  57.7 11.6 %collective-permute-start.11 = (bf16[112,256]{1,0:T(8,128)(2,1)}, bf16[112,256]{1,0:T(8,128)(2,1)S(1)}, u32[]{:S(2)}, u32[]{:S(2)}) collective-permute-start(bf16[112,256]{1,0:T(8,128)(2,1)} %get-tuple-element.48), channel_id=1, source_target_pairs={{0,20},{4,16},{8,28},{12,24},{16,4},{20,0},{24,12},{28,8},{1,21},{... | collective-permute-start | bytes 172040 | tf_op jit(solution)/shard_map/ppermute | solution.py:32
  59.4 3.9 %copy-start.23 = (bf16[256,256]{1,0:T(8,128)(2,1)}, bf16[256,256]{1,0:T(8,128)(2,1)S(1)}, u32[]{:S(2)}) copy-start(bf16[256,256]{1,0:T(8,128)(2,1)S(1)} %collective-permute-done.21.refs_5_) | copy-start | bytes 393220
  59.4 10.7 %collective-permute-start.12 = (bf16[112,256]{1,0:T(8,128)(2,1)}, bf16[112,256]{1,0:T(8,128)(2,1)S(1)}, u32[]{:S(2)}, u32[]{:S(2)}) collective-permute-start(bf16[112,256]{1,0:T(8,128)(2,1)} %get-tuple-element.49), channel_id=1, source_target_pairs={{0,24},{4,28},{8,16},{12,20},{16,8},{20,12},{24,0},{28,4},{1,25},{... | collective-permute-start | bytes 172040 | tf_op jit(solution)/shard_map/ppermute | solution.py:32
  62.2 9.4 %collective-permute-start.13 = (bf16[112,256]{1,0:T(8,128)(2,1)}, bf16[112,256]{1,0:T(8,128)(2,1)S(1)}, u32[]{:S(2)}, u32[]{:S(2)}) collective-permute-start(bf16[112,256]{1,0:T(8,128)(2,1)} %get-tuple-element.50), channel_id=1, source_target_pairs={{0,28},{4,24},{8,20},{12,16},{16,12},{20,8},{24,4},{28,0},{1,29},{... | collective-permute-start | bytes 172040 | tf_op jit(solution)/shard_map/ppermute | solution.py:32
  63.3 9.1 %collective-permute-start.14 = (bf16[112,256]{1,0:T(8,128)(2,1)}, bf16[112,256]{1,0:T(8,128)(2,1)S(1)}, u32[]{:S(2)}, u32[]{:S(2)}) collective-permute-start(bf16[112,256]{1,0:T(8,128)(2,1)} %get-tuple-element.51), channel_id=1, source_target_pairs={{0,8},{4,12},{8,0},{12,4},{16,24},{20,28},{24,16},{28,20},{1,9},{5... | collective-permute-start | bytes 172040 | tf_op jit(solution)/shard_map/ppermute | solution.py:32
  63.9 4.4 %copy-start.35 = (bf16[112,256]{1,0:T(8,128)(2,1)S(1)}, bf16[112,256]{1,0:T(8,128)(2,1)}, u32[]{:S(2)}) copy-start(bf16[112,256]{1,0:T(8,128)(2,1)} %get-tuple-element.52) | copy-start | bytes 172036
  63.9 5.3 %copy-start.34 = (bf16[112,256]{1,0:T(8,128)(2,1)S(1)}, bf16[112,256]{1,0:T(8,128)(2,1)}, u32[]{:S(2)}) copy-start(bf16[112,256]{1,0:T(8,128)(2,1)} %get-tuple-element.53) | copy-start | bytes 172036
  68.3 15.3 %copy-start.1 = (bf16[112,256]{1,0:T(8,128)(2,1)}, bf16[112,256]{1,0:T(8,128)(2,1)S(1)}, u32[]{:S(2)}) copy-start(bf16[112,256]{1,0:T(8,128)(2,1)S(1)} %collective-permute-done.10.refs_1_) | copy-start | bytes 172036
  68.3 6.6 %collective-permute-start.15 = (bf16[112,256]{1,0:T(8,128)(2,1)S(1)}, bf16[112,256]{1,0:T(8,128)(2,1)S(1)}, u32[]{:S(2)}, u32[]{:S(2)}) collective-permute-start(bf16[112,256]{1,0:T(8,128)(2,1)S(1)} %copy-done.35), channel_id=1, source_target_pairs={{0,12},{4,8},{8,4},{12,0},{16,28},{20,24},{24,20},{28,16},{1,13},{... | collective-permute-start | bytes 172040 | tf_op jit(solution)/shard_map/ppermute | solution.py:32
  69.2 14.5 %copy-start.2 = (bf16[112,256]{1,0:T(8,128)(2,1)}, bf16[112,256]{1,0:T(8,128)(2,1)S(1)}, u32[]{:S(2)}) copy-start(bf16[112,256]{1,0:T(8,128)(2,1)S(1)} %collective-permute-done.11.refs_2_) | copy-start | bytes 172036
  69.2 7.0 %collective-permute-start.16 = (bf16[112,256]{1,0:T(8,128)(2,1)S(1)}, bf16[112,256]{1,0:T(8,128)(2,1)S(1)}, u32[]{:S(2)}, u32[]{:S(2)}) collective-permute-start(bf16[112,256]{1,0:T(8,128)(2,1)S(1)} %copy-done.34), channel_id=1, source_target_pairs={{0,4},{4,0},{8,12},{12,8},{16,20},{20,16},{24,28},{28,24},{1,5},{5... | collective-permute-start | bytes 172040 | tf_op jit(solution)/shard_map/ppermute | solution.py:32
  70.0 13.6 %copy-start.3 = (bf16[112,256]{1,0:T(8,128)(2,1)}, bf16[112,256]{1,0:T(8,128)(2,1)S(1)}, u32[]{:S(2)}) copy-start(bf16[112,256]{1,0:T(8,128)(2,1)S(1)} %collective-permute-done.12.refs_3_) | copy-start | bytes 172036
  70.0 9.2 %collective-permute-start.24 = (bf16[112,256]{1,0:T(8,128)(2,1)}, bf16[112,256]{1,0:T(8,128)(2,1)S(1)}, u32[]{:S(2)}, u32[]{:S(2)}) collective-permute-start(bf16[112,256]{1,0:T(8,128)(2,1)} %get-tuple-element.63), channel_id=1, source_target_pairs={{0,16},{4,20},{8,24},{12,28},{16,0},{20,4},{24,8},{28,12},{1,17},{... | collective-permute-start | bytes 172040 | tf_op jit(solution)/shard_map/ppermute | solution.py:32
  71.7 12.0 %copy-start.4 = (bf16[112,256]{1,0:T(8,128)(2,1)}, bf16[112,256]{1,0:T(8,128)(2,1)S(1)}, u32[]{:S(2)}) copy-start(bf16[112,256]{1,0:T(8,128)(2,1)S(1)} %collective-permute-done.13.refs_4_) | copy-start | bytes 172036
  71.7 7.9 %collective-permute-start.25 = (bf16[112,256]{1,0:T(8,128)(2,1)}, bf16[112,256]{1,0:T(8,128)(2,1)S(1)}, u32[]{:S(2)}, u32[]{:S(2)}) collective-permute-start(bf16[112,256]{1,0:T(8,128)(2,1)} %get-tuple-element.64), channel_id=1, source_target_pairs={{0,20},{4,16},{8,28},{12,24},{16,4},{20,0},{24,12},{28,8},{1,21},{... | collective-permute-start | bytes 172040 | tf_op jit(solution)/shard_map/ppermute | solution.py:32
  72.4 11.3 %copy-start.5 = (bf16[112,256]{1,0:T(8,128)(2,1)}, bf16[112,256]{1,0:T(8,128)(2,1)S(1)}, u32[]{:S(2)}) copy-start(bf16[112,256]{1,0:T(8,128)(2,1)S(1)} %collective-permute-done.14.refs_5_) | copy-start | bytes 172036
  72.4 9.1 %collective-permute-start.26 = (bf16[112,256]{1,0:T(8,128)(2,1)}, bf16[112,256]{1,0:T(8,128)(2,1)S(1)}, u32[]{:S(2)}, u32[]{:S(2)}) collective-permute-start(bf16[112,256]{1,0:T(8,128)(2,1)} %get-tuple-element.65), channel_id=1, source_target_pairs={{0,24},{4,28},{8,16},{12,20},{16,8},{20,12},{24,0},{28,4},{1,25},{... | collective-permute-start | bytes 172040 | tf_op jit(solution)/shard_map/ppermute | solution.py:32
  74.9 8.8 %copy-start.6 = (bf16[112,256]{1,0:T(8,128)(2,1)}, bf16[112,256]{1,0:T(8,128)(2,1)S(1)}, u32[]{:S(2)}) copy-start(bf16[112,256]{1,0:T(8,128)(2,1)S(1)} %collective-permute-done.15.refs_6_) | copy-start | bytes 172036
  74.9 6.5 %collective-permute-start.27 = (bf16[112,256]{1,0:T(8,128)(2,1)}, bf16[112,256]{1,0:T(8,128)(2,1)S(1)}, u32[]{:S(2)}, u32[]{:S(2)}) collective-permute-start(bf16[112,256]{1,0:T(8,128)(2,1)} %get-tuple-element.66), channel_id=1, source_target_pairs={{0,28},{4,24},{8,20},{12,16},{16,12},{20,8},{24,4},{28,0},{1,29},{... | collective-permute-start | bytes 172040 | tf_op jit(solution)/shard_map/ppermute | solution.py:32
  76.3 7.5 %copy-start.7 = (bf16[112,256]{1,0:T(8,128)(2,1)}, bf16[112,256]{1,0:T(8,128)(2,1)S(1)}, u32[]{:S(2)}) copy-start(bf16[112,256]{1,0:T(8,128)(2,1)S(1)} %collective-permute-done.16.refs_7_) | copy-start | bytes 172036
  76.3 6.2 %collective-permute-start.28 = (bf16[112,256]{1,0:T(8,128)(2,1)}, bf16[112,256]{1,0:T(8,128)(2,1)S(1)}, u32[]{:S(2)}, u32[]{:S(2)}) collective-permute-start(bf16[112,256]{1,0:T(8,128)(2,1)} %get-tuple-element.67), channel_id=1, source_target_pairs={{0,8},{4,12},{8,0},{12,4},{16,24},{20,28},{24,16},{28,20},{1,9},{5... | collective-permute-start | bytes 172040 | tf_op jit(solution)/shard_map/ppermute | solution.py:32
  79.2 4.5 %copy-start.8 = (bf16[112,256]{1,0:T(8,128)(2,1)}, bf16[112,256]{1,0:T(8,128)(2,1)S(1)}, u32[]{:S(2)}) copy-start(bf16[112,256]{1,0:T(8,128)(2,1)S(1)} %collective-permute-done.24.refs_9_) | copy-start | bytes 172036
  79.2 4.4 %collective-permute-start.29 = (bf16[112,256]{1,0:T(8,128)(2,1)}, bf16[112,256]{1,0:T(8,128)(2,1)S(1)}, u32[]{:S(2)}, u32[]{:S(2)}) collective-permute-start(bf16[112,256]{1,0:T(8,128)(2,1)} %get-tuple-element.68), channel_id=1, source_target_pairs={{0,12},{4,8},{8,4},{12,0},{16,28},{20,24},{24,20},{28,16},{1,13},{... | collective-permute-start | bytes 172040 | tf_op jit(solution)/shard_map/ppermute | solution.py:32
  79.6 4.2 %copy-start.9 = (bf16[112,256]{1,0:T(8,128)(2,1)}, bf16[112,256]{1,0:T(8,128)(2,1)S(1)}, u32[]{:S(2)}) copy-start(bf16[112,256]{1,0:T(8,128)(2,1)S(1)} %collective-permute-done.25.refs_10_) | copy-start | bytes 172036
  79.6 4.1 %collective-permute-start.30 = (bf16[112,256]{1,0:T(8,128)(2,1)}, bf16[112,256]{1,0:T(8,128)(2,1)S(1)}, u32[]{:S(2)}, u32[]{:S(2)}) collective-permute-start(bf16[112,256]{1,0:T(8,128)(2,1)} %get-tuple-element.69), channel_id=1, source_target_pairs={{0,4},{4,0},{8,12},{12,8},{16,20},{20,16},{24,28},{28,24},{1,5},{5... | collective-permute-start | bytes 172040 | tf_op jit(solution)/shard_map/ppermute | solution.py:32
  81.5 2.3 %copy-start.11 = (bf16[112,256]{1,0:T(8,128)(2,1)}, bf16[112,256]{1,0:T(8,128)(2,1)S(1)}, u32[]{:S(2)}) copy-start(bf16[112,256]{1,0:T(8,128)(2,1)S(1)} %collective-permute-done.27.refs_12_) | copy-start | bytes 172036
  85.9 6.6 %collective-permute-start.33 = (f32[4,4,1024]{2,1,0:T(4,128)}, f32[4,4,1024]{2,1,0:T(4,128)S(1)}, u32[]{:S(2)}, u32[]{:S(2)}) collective-permute-start(f32[4,4,1024]{2,1,0:T(4,128)} %get-tuple-element.73), channel_id=1, source_target_pairs={{0,3},{1,2},{2,1},{3,0},{4,7},{5,6},{6,5},{7,4},{8,11},{9,10},{10,... | collective-permute-start | bytes 196616 | tf_op jit(solution)/shard_map/ppermute | solution.py:32
  87.4 5.1 %collective-permute-start.32 = (f32[4,4,1024]{2,1,0:T(4,128)}, f32[4,4,1024]{2,1,0:T(4,128)S(1)}, u32[]{:S(2)}, u32[]{:S(2)}) collective-permute-start(f32[4,4,1024]{2,1,0:T(4,128)} %get-tuple-element.72), channel_id=1, source_target_pairs={{0,2},{1,3},{2,0},{3,1},{4,6},{5,7},{6,4},{7,5},{8,10},{9,11},{10,... | collective-permute-start | bytes 196616 | tf_op jit(solution)/shard_map/ppermute | solution.py:32
  88.0 4.7 %copy-start.29 = (f32[4,4,1024]{2,1,0:T(4,128)S(1)}, f32[4,4,1024]{2,1,0:T(4,128)}, u32[]{:S(2)}) copy-start(f32[4,4,1024]{2,1,0:T(4,128)} %get-tuple-element.70) | copy-start | bytes 196612
  88.0 4.7 %collective-permute-start.31 = (f32[4,4,1024]{2,1,0:T(4,128)}, f32[4,4,1024]{2,1,0:T(4,128)S(1)}, u32[]{:S(2)}, u32[]{:S(2)}) collective-permute-start(f32[4,4,1024]{2,1,0:T(4,128)} %get-tuple-element.71), channel_id=1, source_target_pairs={{0,1},{1,0},{2,3},{3,2},{4,5},{5,4},{6,7},{7,6},{8,9},{9,8},{10,11... | collective-permute-start | bytes 196616 | tf_op jit(solution)/shard_map/ppermute | solution.py:32
  (6 other events, 6.6 us)

commit v3 on v2

--- a/solution.py
+++ b/solution.py
@@ -217,7 +217,10 @@
             out_specs=[VMEM] * n,
             scratch_shapes=[pltpu.SemaphoreType.DMA((2 * n,))],
         )(inputs, upstream)
-        arrived.append([cut[0]] + [send(b, "seq", n, m) for b, m in zip(cut[1:], todo)])
+        got = [cut[0]]
+        for b, m in zip(cut[1:], todo):
+            got.append(send(b, "seq", n, m))
+        arrived.append(got)
     own = pool_weight.reshape(KINDS * POOL, -1)
     pieces = [own] + [send(own, "dp", nd, k) for k in range(1, nd)]
     weights = jnp.stack(pieces)

time: 93.7 us -> 93.7 us (level)
  no operation moved by 1% of the time
where the time goes in v3:
time: 93.7 us; the launch traced here: 93.3 us
  starting transfers between devices  43.9 us (47%)
  waiting for transfers between devices  26.8 us (29%)
  Pallas kernels  18.1 us (19%)
  local copies, waits for them, and re-layouts  2.15 us (2%)
  other arithmetic  1.37 us (1%)
  between operations  0.94 us (1%)
    ppermute x34, starting transfers between devices, send(): return lax.ppermute(block, axis, [(s, s ^ message) for s in range(n)])  43.9 us
    ppermute x34, waiting for transfers between devices, send(): return lax.ppermute(block, axis, [(s, s ^ message) for s in range(n)])  26.8 us
    pallas_call x2, Pallas kernels, per_device(): pl.pallas_call(functools.partial(block_kernel, n, nd, rc, wide, c * cw),...  8.76 us
    pallas_call x2, Pallas kernels, per_device(): pl.pallas_call(functools.partial(cut_kernel, n, wide, c * cw), out_shape=...  4.73 us
    pallas_call x1, Pallas kernels, per_device(): pl.pallas_call(functools.partial(spread_kernel, n, nd, wide), out_shape=s...  3.03 us
  transfers between devices with their start and end apart: 34, of which 10 were waited for; matrix products, arithmetic and copies ran while one was open for 1% of the time, Pallas kernels for 18%

profile of v3, /device:TPU:0, one launch (start us, length us, event | category | flops | bytes accessed | tf_op | source)
XLA Modules:
  0.0 93.3 jit_solution(13473787713442663632)
XLA Ops:
  0.6 0.9 reshape.7
  1.5 4.0 %collective-permute-start.2 = (f32[16,1024]{1,0:T(8,128)S(1)}, f32[16,1024]{1,0:T(8,128)S(1)}, u32[]{:S(2)}, u32[]{:S(2)}) collective-permute-start(f32[16,1024]{1,0:T(8,128)S(1)} %reshape.7), channel_id=1, source_target_pairs={{0,3},{1,2},{2,1},{3,0},{4,7},{5,6},{6,5},{7,4},{8,11},{9,10},{10,... | collective-permute-start | bytes 196616 | tf_op jit(solution)/shard_map/ppermute | solution.py:32
  5.5 0.5 collective-permute-start.1
  6.0 2.3 %shard_map.50 = (bf16[256,256]{1,0:T(8,128)(2,1)}, bf16[256,256]{1,0:T(8,128)(2,1)}, bf16[256,256]{1,0:T(8,128)(2,1)}, bf16[256,256]{1,0:T(8,128)(2,1)}, bf16[25...) custom-call(bf16[128,4096]{1,0:T(8,128)(2,1)} %bitcast.11, ...), custom_call_target="tpu_custom_call" | custom-call | tf_op jit(solution)/shard_map/pallas_call | solution.py:213
  8.3 2.7 %collective-permute-start.3 = (bf16[256,256]{1,0:T(8,128)(2,1)}, bf16[256,256]{1,0:T(8,128)(2,1)S(1)}, u32[]{:S(2)}, u32[]{:S(2)}) collective-permute-start(bf16[256,256]{1,0:T(8,128)(2,1)} %get-tuple-element.39), channel_id=1, source_target_pairs={{0,16},{4,20},{8,24},{12,28},{16,0},{20,4},{24,8},{28,12},{1,17},{... | collective-permute-start | bytes 393224 | tf_op jit(solution)/shard_map/ppermute | solution.py:32
  11.0 2.5 %collective-permute-start.5 = (bf16[256,256]{1,0:T(8,128)(2,1)}, bf16[256,256]{1,0:T(8,128)(2,1)S(1)}, u32[]{:S(2)}, u32[]{:S(2)}) collective-permute-start(bf16[256,256]{1,0:T(8,128)(2,1)} %get-tuple-element.41), channel_id=1, source_target_pairs={{0,24},{4,28},{8,16},{12,20},{16,8},{20,12},{24,0},{28,4},{1,25},{... | collective-permute-start | bytes 393224 | tf_op jit(solution)/shard_map/ppermute | solution.py:32
  13.5 0.0 collective-permute-done.2
  13.5 0.0 copy-start
  13.6 1.2 %collective-permute-start.6 = (bf16[256,256]{1,0:T(8,128)(2,1)}, bf16[256,256]{1,0:T(8,128)(2,1)S(1)}, u32[]{:S(2)}, u32[]{:S(2)}) collective-permute-start(bf16[256,256]{1,0:T(8,128)(2,1)} %get-tuple-element.42), channel_id=1, source_target_pairs={{0,28},{4,24},{8,20},{12,16},{16,12},{20,8},{24,4},{28,0},{1,29},{... | collective-permute-start | bytes 393224 | tf_op jit(solution)/shard_map/ppermute | solution.py:32
  14.8 0.5 collective-permute-start
  15.3 2.4 %shard_map.52 = (bf16[256,256]{1,0:T(8,128)(2,1)}, bf16[256,256]{1,0:T(8,128)(2,1)}, bf16[256,256]{1,0:T(8,128)(2,1)}, bf16[256,256]{1,0:T(8,128)(2,1)}, bf16[25...) custom-call(bf16[128,4096]{1,0:T(8,128)(2,1)} %bitcast.12, ...), custom_call_target="tpu_custom_call" | custom-call | tf_op jit(solution)/shard_map/pallas_call | solution.py:213
  17.7 1.3 %collective-permute-done = f32[16,1024]{1,0:T(8,128)S(1)} collective-permute-done((f32[16,1024]{1,0:T(8,128)S(1)}, f32[16,1024]{1,0:T(8,128)S(1)}, u32[]{:S(2)}, u32[]{:S(2)}) %collective-permute-start) | collective-permute-done | bytes 65568 | tf_op jit(solution)/shard_map/ppermute | solution.py:32
  19.0 0.0 collective-permute-start.7
  19.0 7.6 %collective-permute-done.3.refs_1_ = bf16[256,256]{1,0:T(8,128)(2,1)S(1)} collective-permute-done((bf16[256,256]{1,0:T(8,128)(2,1)}, bf16[256,256]{1,0:T(8,128)(2,1)S(1)}, u32[]{:S(2)}, u32[]{:S(2)}) %collective-permute-start.3) | collective-permute-done | bytes 131104 | tf_op jit(solution)/shard_map/ppermute | solution.py:32
  26.6 0.0 collective-permute-start.8
  26.6 0.6 collective-permute-done.4.refs_2_
  27.2 2.0 %collective-permute-start.9 = (bf16[256,256]{1,0:T(8,128)(2,1)S(1)}, bf16[256,256]{1,0:T(8,128)(2,1)S(1)}, u32[]{:S(2)}, u32[]{:S(2)}) collective-permute-start(bf16[256,256]{1,0:T(8,128)(2,1)S(1)} %copy-done.31), channel_id=1, source_target_pairs={{0,4},{4,0},{8,12},{12,8},{16,20},{20,16},{24,28},{28,24},{1,5},{5... | collective-permute-start | bytes 393224 | tf_op jit(solution)/shard_map/ppermute | solution.py:32
  29.2 4.6 %collective-permute-start.17 = (bf16[256,256]{1,0:T(8,128)(2,1)}, bf16[256,256]{1,0:T(8,128)(2,1)S(1)}, u32[]{:S(2)}, u32[]{:S(2)}) collective-permute-start(bf16[256,256]{1,0:T(8,128)(2,1)} %get-tuple-element.55), channel_id=1, source_target_pairs={{0,16},{4,20},{8,24},{12,28},{16,0},{20,4},{24,8},{28,12},{1,17},{... | collective-permute-start | bytes 393224 | tf_op jit(solution)/shard_map/ppermute | solution.py:32
  33.8 2.3 %collective-permute-start.18 = (bf16[256,256]{1,0:T(8,128)(2,1)}, bf16[256,256]{1,0:T(8,128)(2,1)S(1)}, u32[]{:S(2)}, u32[]{:S(2)}) collective-permute-start(bf16[256,256]{1,0:T(8,128)(2,1)} %get-tuple-element.56), channel_id=1, source_target_pairs={{0,20},{4,16},{8,28},{12,24},{16,4},{20,0},{24,12},{28,8},{1,21},{... | collective-permute-start | bytes 393224 | tf_op jit(solution)/shard_map/ppermute | solution.py:32
  36.1 0.6 collective-permute-start.19
  36.7 3.0 %collective-permute-start.20 = (bf16[256,256]{1,0:T(8,128)(2,1)}, bf16[256,256]{1,0:T(8,128)(2,1)S(1)}, u32[]{:S(2)}, u32[]{:S(2)}) collective-permute-start(bf16[256,256]{1,0:T(8,128)(2,1)} %get-tuple-element.58), channel_id=1, source_target_pairs={{0,28},{4,24},{8,20},{12,16},{16,12},{20,8},{24,4},{28,0},{1,29},{... | collective-permute-start | bytes 393224 | tf_op jit(solution)/shard_map/ppermute | solution.py:32
  39.7 9.6 %collective-permute-done.17.refs_1_ = bf16[256,256]{1,0:T(8,128)(2,1)S(1)} collective-permute-done((bf16[256,256]{1,0:T(8,128)(2,1)}, bf16[256,256]{1,0:T(8,128)(2,1)S(1)}, u32[]{:S(2)}, u32[]{:S(2)}) %collective-permute-start.17) | collective-permute-done | bytes 131104 | tf_op jit(solution)/shard_map/ppermute | solution.py:32
  49.3 2.0 %collective-permute-done.18.refs_2_ = bf16[256,256]{1,0:T(8,128)(2,1)S(1)} collective-permute-done((bf16[256,256]{1,0:T(8,128)(2,1)}, bf16[256,256]{1,0:T(8,128)(2,1)S(1)}, u32[]{:S(2)}, u32[]{:S(2)}) %collective-permute-start.18) | collective-permute-done | bytes 131104 | tf_op jit(solution)/shard_map/ppermute | solution.py:32
  51.3 0.5 collective-permute-start.23
  51.8 0.7 pad_maximum_fusion.weight
  52.6 4.4 %shard_map.51 = (bf16[112,256]{1,0:T(8,128)(2,1)}, bf16[112,256]{1,0:T(8,128)(2,1)}, bf16[112,256]{1,0:T(8,128)(2,1)}, bf16[112,256]{1,0:T(8,128)(2,1)}, bf16[11...) custom-call(f32[4,16,1024]{2,1,0:T(8,128)} %pad_maximum_fusion.weight, ...), custom_call_target="tpu_custom_call" | custom-call | tf_op jit(solution)/shard_map/pallas_call | solution.py:231
  57.0 0.0 collective-permute-done.19.refs_3_
  57.0 0.0 copy-start.21
  57.0 0.7 collective-permute-start.10
  57.6 0.0 collective-permute-done.20.refs_4_
  57.7 1.7 %collective-permute-start.11 = (bf16[112,256]{1,0:T(8,128)(2,1)}, bf16[112,256]{1,0:T(8,128)(2,1)S(1)}, u32[]{:S(2)}, u32[]{:S(2)}) collective-permute-start(bf16[112,256]{1,0:T(8,128)(2,1)} %get-tuple-element.48), channel_id=1, source_target_pairs={{0,20},{4,16},{8,28},{12,24},{16,4},{20,0},{24,12},{28,8},{1,21},{... | collective-permute-start | bytes 172040 | tf_op jit(solution)/shard_map/ppermute | solution.py:32
  59.4 0.0 collective-permute-done.21.refs_5_
  59.4 2.9 %collective-permute-start.12 = (bf16[112,256]{1,0:T(8,128)(2,1)}, bf16[112,256]{1,0:T(8,128)(2,1)S(1)}, u32[]{:S(2)}, u32[]{:S(2)}) collective-permute-start(bf16[112,256]{1,0:T(8,128)(2,1)} %get-tuple-element.49), channel_id=1, source_target_pairs={{0,24},{4,28},{8,16},{12,20},{16,8},{20,12},{24,0},{28,4},{1,25},{... | collective-permute-start | bytes 172040 | tf_op jit(solution)/shard_map/ppermute | solution.py:32
  62.2 0.0 collective-permute-done.22.refs_6_
  62.2 1.0 %collective-permute-start.13 = (bf16[112,256]{1,0:T(8,128)(2,1)}, bf16[112,256]{1,0:T(8,128)(2,1)S(1)}, u32[]{:S(2)}, u32[]{:S(2)}) collective-permute-start(bf16[112,256]{1,0:T(8,128)(2,1)} %get-tuple-element.50), channel_id=1, source_target_pairs={{0,28},{4,24},{8,20},{12,16},{16,12},{20,8},{24,4},{28,0},{1,29},{... | collective-permute-start | bytes 172040 | tf_op jit(solution)/shard_map/ppermute | solution.py:32
  63.3 0.0 collective-permute-start.14
  63.3 0.6 copy-done.27
  63.9 4.4 %shard_map.53 = (bf16[112,256]{1,0:T(8,128)(2,1)}, bf16[112,256]{1,0:T(8,128)(2,1)}, bf16[112,256]{1,0:T(8,128)(2,1)}, bf16[112,256]{1,0:T(8,128)(2,1)}, bf16[11...) custom-call(f32[4,16,1024]{2,1,0:T(8,128)} %pad_maximum_fusion.weight, ...), custom_call_target="tpu_custom_call" | custom-call | tf_op jit(solution)/shard_map/pallas_call | solution.py:231
  68.3 0.0 collective-permute-done.10.refs_1_
  68.3 0.9 collective-permute-start.15
  69.2 0.8 collective-permute-start.16
  70.0 1.6 %collective-permute-start.24 = (bf16[112,256]{1,0:T(8,128)(2,1)}, bf16[112,256]{1,0:T(8,128)(2,1)S(1)}, u32[]{:S(2)}, u32[]{:S(2)}) collective-permute-start(bf16[112,256]{1,0:T(8,128)(2,1)} %get-tuple-element.63), channel_id=1, source_target_pairs={{0,16},{4,20},{8,24},{12,28},{16,0},{20,4},{24,8},{28,12},{1,17},{... | collective-permute-start | bytes 172040 | tf_op jit(solution)/shard_map/ppermute | solution.py:32
  71.7 0.0 collective-permute-done.13.refs_4_
  71.7 0.7 collective-permute-start.25
  72.4 0.0 collective-permute-done.14.refs_5_
  72.4 2.5 %collective-permute-start.26 = (bf16[112,256]{1,0:T(8,128)(2,1)}, bf16[112,256]{1,0:T(8,128)(2,1)S(1)}, u32[]{:S(2)}, u32[]{:S(2)}) collective-permute-start(bf16[112,256]{1,0:T(8,128)(2,1)} %get-tuple-element.65), channel_id=1, source_target_pairs={{0,24},{4,28},{8,16},{12,20},{16,8},{20,12},{24,0},{28,4},{1,25},{... | collective-permute-start | bytes 172040 | tf_op jit(solution)/shard_map/ppermute | solution.py:32
  74.9 1.3 %collective-permute-start.27 = (bf16[112,256]{1,0:T(8,128)(2,1)}, bf16[112,256]{1,0:T(8,128)(2,1)S(1)}, u32[]{:S(2)}, u32[]{:S(2)}) collective-permute-start(bf16[112,256]{1,0:T(8,128)(2,1)} %get-tuple-element.66), channel_id=1, source_target_pairs={{0,28},{4,24},{8,20},{12,16},{16,12},{20,8},{24,4},{28,0},{1,29},{... | collective-permute-start | bytes 172040 | tf_op jit(solution)/shard_map/ppermute | solution.py:32
  76.3 0.0 collective-permute-done.16.refs_7_
  76.3 0.0 collective-permute-start.28
  76.3 3.0 %collective-permute-done.24.refs_9_ = bf16[112,256]{1,0:T(8,128)(2,1)S(1)} collective-permute-done((bf16[112,256]{1,0:T(8,128)(2,1)}, bf16[112,256]{1,0:T(8,128)(2,1)S(1)}, u32[]{:S(2)}, u32[]{:S(2)}) %collective-permute-start.24) | collective-permute-done | bytes 57376 | tf_op jit(solution)/shard_map/ppermute | solution.py:32
  79.2 0.3 collective-permute-done.25.refs_10_
  79.6 1.9 %collective-permute-start.30 = (bf16[112,256]{1,0:T(8,128)(2,1)}, bf16[112,256]{1,0:T(8,128)(2,1)S(1)}, u32[]{:S(2)}, u32[]{:S(2)}) collective-permute-start(bf16[112,256]{1,0:T(8,128)(2,1)} %get-tuple-element.69), channel_id=1, source_target_pairs={{0,4},{4,0},{8,12},{12,8},{16,20},{20,16},{24,28},{28,24},{1,5},{5... | collective-permute-start | bytes 172040 | tf_op jit(solution)/shard_map/ppermute | solution.py:32
  81.5 1.0 %collective-permute-done.28.refs_13_ = bf16[112,256]{1,0:T(8,128)(2,1)S(1)} collective-permute-done((bf16[112,256]{1,0:T(8,128)(2,1)}, bf16[112,256]{1,0:T(8,128)(2,1)S(1)}, u32[]{:S(2)}, u32[]{:S(2)}) %collective-permute-start.28) | collective-permute-done | bytes 57376 | tf_op jit(solution)/shard_map/ppermute | solution.py:32
  82.5 1.2 %collective-permute-done.29.refs_14_ = bf16[112,256]{1,0:T(8,128)(2,1)S(1)} collective-permute-done((bf16[112,256]{1,0:T(8,128)(2,1)}, bf16[112,256]{1,0:T(8,128)(2,1)S(1)}, u32[]{:S(2)}, u32[]{:S(2)}) %collective-permute-start.29) | collective-permute-done | bytes 57376 | tf_op jit(solution)/shard_map/ppermute | solution.py:32
  83.8 0.5 copy-done.13
  84.3 0.0 copy-done.14
  84.3 1.6 %shard_map.55 = (f32[4,4,1024]{2,1,0:T(4,128)}, f32[4,4,1024]{2,1,0:T(4,128)}, f32[4,4,1024]{2,1,0:T(4,128)}, f32[4,4,1024]{2,1,0:T(4,128)}) custom-call(bf16[112,256]{1,0:T(8,128)(2,1)} %get-tuple-element.46.refs_0_, bf16[112,256]{1,0:T(8,128)(2,1)} %copy-done.1, bf16[112,256]{1,0:T(8,128)(2,1)} %copy-done.2, bf16[112,256]{1,0:T(8,128)(2,1)} %copy-done.3, ...), custom_call_target="tpu_custom_call" | custom-call | tf_op jit(solution)/shard_map/pallas_call | solution.py:247
  85.9 1.5 %collective-permute-start.33 = (f32[4,4,1024]{2,1,0:T(4,128)}, f32[4,4,1024]{2,1,0:T(4,128)S(1)}, u32[]{:S(2)}, u32[]{:S(2)}) collective-permute-start(f32[4,4,1024]{2,1,0:T(4,128)} %get-tuple-element.73), channel_id=1, source_target_pairs={{0,3},{1,2},{2,1},{3,0},{4,7},{5,6},{6,5},{7,4},{8,11},{9,10},{10,... | collective-permute-start | bytes 196616 | tf_op jit(solution)/shard_map/ppermute | solution.py:32
  87.4 0.5 collective-permute-start.32
  88.0 1.5 %collective-permute-start.31 = (f32[4,4,1024]{2,1,0:T(4,128)}, f32[4,4,1024]{2,1,0:T(4,128)S(1)}, u32[]{:S(2)}, u32[]{:S(2)}) collective-permute-start(f32[4,4,1024]{2,1,0:T(4,128)} %get-tuple-element.71), channel_id=1, source_target_pairs={{0,1},{1,0},{2,3},{3,2},{4,5},{5,4},{6,7},{7,6},{8,9},{9,8},{10,11... | collective-permute-start | bytes 196616 | tf_op jit(solution)/shard_map/ppermute | solution.py:32
  89.4 3.0 %shard_map.54 = bf16[128,4096]{1,0:T(8,128)(2,1)} custom-call(f32[4,16,1024]{2,1,0:T(8,128)} %pad_maximum_fusion.weight, bf16[112,256]{1,0:T(8,128)(2,1)} %get-tuple-element.46.refs_0_, bf16[112,256]{1,0:T(8,128)(2,1)} %copy-done.1, bf16[112,256]{1,0:T(8,128)(2,1)} %copy-done.2, bf16[112,256]{1,0:T(8,128)(2,1)} %copy-done.3, bf16[112,256]{1,0:T(8,128)(2,1)} %copy-done.4, ...), custom_call_target="tpu_custom_call" | custom-call | tf_op jit(solution)/shard_map/pallas_call | solution.py:258
  92.5 0.1 collective-permute-done.32
  92.6 0.0 collective-permute-done.31
  92.6 0.6 add_add_fusion
  (86 shorter events, 0.2 us)
Async XLA Ops:
  1.5 12.0 %collective-permute-start.2 = (f32[16,1024]{1,0:T(8,128)S(1)}, f32[16,1024]{1,0:T(8,128)S(1)}, u32[]{:S(2)}, u32[]{:S(2)}) collective-permute-start(f32[16,1024]{1,0:T(8,128)S(1)} %reshape.7), channel_id=1, source_target_pairs={{0,3},{1,2},{2,1},{3,0},{4,7},{5,6},{6,5},{7,4},{8,11},{9,10},{10,... | collective-permute-start | bytes 196616 | tf_op jit(solution)/shard_map/ppermute | solution.py:32
  5.5 9.3 %collective-permute-start.1 = (f32[16,1024]{1,0:T(8,128)S(1)}, f32[16,1024]{1,0:T(8,128)S(1)}, u32[]{:S(2)}, u32[]{:S(2)}) collective-permute-start(f32[16,1024]{1,0:T(8,128)S(1)} %reshape.7), channel_id=1, source_target_pairs={{0,2},{1,3},{2,0},{3,1},{4,6},{5,7},{6,4},{7,5},{8,10},{9,11},{10,... | collective-permute-start | bytes 196616 | tf_op jit(solution)/shard_map/ppermute | solution.py:32
  8.3 18.3 %collective-permute-start.3 = (bf16[256,256]{1,0:T(8,128)(2,1)}, bf16[256,256]{1,0:T(8,128)(2,1)S(1)}, u32[]{:S(2)}, u32[]{:S(2)}) collective-permute-start(bf16[256,256]{1,0:T(8,128)(2,1)} %get-tuple-element.39), channel_id=1, source_target_pairs={{0,16},{4,20},{8,24},{12,28},{16,0},{20,4},{24,8},{28,12},{1,17},{... | collective-permute-start | bytes 393224 | tf_op jit(solution)/shard_map/ppermute | solution.py:32
  11.0 16.2 %collective-permute-start.4 = (bf16[256,256]{1,0:T(8,128)(2,1)}, bf16[256,256]{1,0:T(8,128)(2,1)S(1)}, u32[]{:S(2)}, u32[]{:S(2)}) collective-permute-start(bf16[256,256]{1,0:T(8,128)(2,1)} %get-tuple-element.40), channel_id=1, source_target_pairs={{0,20},{4,16},{8,28},{12,24},{16,4},{20,0},{24,12},{28,8},{1,21},{... | collective-permute-start | bytes 393224 | tf_op jit(solution)/shard_map/ppermute | solution.py:32
  11.0 18.2 %collective-permute-start.5 = (bf16[256,256]{1,0:T(8,128)(2,1)}, bf16[256,256]{1,0:T(8,128)(2,1)S(1)}, u32[]{:S(2)}, u32[]{:S(2)}) collective-permute-start(bf16[256,256]{1,0:T(8,128)(2,1)} %get-tuple-element.41), channel_id=1, source_target_pairs={{0,24},{4,28},{8,16},{12,20},{16,8},{20,12},{24,0},{28,4},{1,25},{... | collective-permute-start | bytes 393224 | tf_op jit(solution)/shard_map/ppermute | solution.py:32
  13.5 5.5 %copy-start.33 = (bf16[256,256]{1,0:T(8,128)(2,1)S(1)}, bf16[256,256]{1,0:T(8,128)(2,1)}, u32[]{:S(2)}) copy-start(bf16[256,256]{1,0:T(8,128)(2,1)} %get-tuple-element.43) | copy-start | bytes 393220
  13.5 13.1 %copy-start.32 = (bf16[256,256]{1,0:T(8,128)(2,1)S(1)}, bf16[256,256]{1,0:T(8,128)(2,1)}, u32[]{:S(2)}) copy-start(bf16[256,256]{1,0:T(8,128)(2,1)} %get-tuple-element.44) | copy-start | bytes 393220
  13.5 13.7 %copy-start.31 = (bf16[256,256]{1,0:T(8,128)(2,1)S(1)}, bf16[256,256]{1,0:T(8,128)(2,1)}, u32[]{:S(2)}) copy-start(bf16[256,256]{1,0:T(8,128)(2,1)} %get-tuple-element.45) | copy-start | bytes 393220
  13.5 35.7 %copy-start = (f32[4,4,1024]{2,1,0:T(4,128)S(1)}, f32[4,4,1024]{2,1,0:T(4,128)}, u32[]{:S(2)}) copy-start(f32[4,4,1024]{2,1,0:T(4,128)} %param.5) | copy-start | bytes 196612
  13.6 20.2 %collective-permute-start.6 = (bf16[256,256]{1,0:T(8,128)(2,1)}, bf16[256,256]{1,0:T(8,128)(2,1)S(1)}, u32[]{:S(2)}, u32[]{:S(2)}) collective-permute-start(bf16[256,256]{1,0:T(8,128)(2,1)} %get-tuple-element.42), channel_id=1, source_target_pairs={{0,28},{4,24},{8,20},{12,16},{16,12},{20,8},{24,4},{28,0},{1,29},{... | collective-permute-start | bytes 393224 | tf_op jit(solution)/shard_map/ppermute | solution.py:32
  14.8 4.3 %collective-permute-start = (f32[16,1024]{1,0:T(8,128)S(1)}, f32[16,1024]{1,0:T(8,128)S(1)}, u32[]{:S(2)}, u32[]{:S(2)}) collective-permute-start(f32[16,1024]{1,0:T(8,128)S(1)} %reshape.7), channel_id=1, source_target_pairs={{0,1},{1,0},{2,3},{3,2},{4,5},{5,4},{6,7},{7,6},{8,9},{9,8},{10,11... | collective-permute-start | bytes 196616 | tf_op jit(solution)/shard_map/ppermute | solution.py:32
  17.7 33.6 %copy-start.30 = (bf16[256,256]{1,0:T(8,128)(2,1)S(1)}, bf16[256,256]{1,0:T(8,128)(2,1)}, u32[]{:S(2)}) copy-start(bf16[256,256]{1,0:T(8,128)(2,1)} %get-tuple-element.61) | copy-start | bytes 393220
  19.0 17.1 %collective-permute-start.7 = (bf16[256,256]{1,0:T(8,128)(2,1)S(1)}, bf16[256,256]{1,0:T(8,128)(2,1)S(1)}, u32[]{:S(2)}, u32[]{:S(2)}) collective-permute-start(bf16[256,256]{1,0:T(8,128)(2,1)S(1)} %copy-done.33), channel_id=1, source_target_pairs={{0,8},{4,12},{8,0},{12,4},{16,24},{20,28},{24,16},{28,20},{1,9},{5... | collective-permute-start | bytes 393224 | tf_op jit(solution)/shard_map/ppermute | solution.py:32
  26.6 25.9 %copy-start.15 = (bf16[256,256]{1,0:T(8,128)(2,1)}, bf16[256,256]{1,0:T(8,128)(2,1)S(1)}, u32[]{:S(2)}) copy-start(bf16[256,256]{1,0:T(8,128)(2,1)S(1)} %collective-permute-done.3.refs_1_) | copy-start | bytes 393220
  26.6 10.0 %collective-permute-start.8 = (bf16[256,256]{1,0:T(8,128)(2,1)S(1)}, bf16[256,256]{1,0:T(8,128)(2,1)S(1)}, u32[]{:S(2)}, u32[]{:S(2)}) collective-permute-start(bf16[256,256]{1,0:T(8,128)(2,1)S(1)} %copy-done.32), channel_id=1, source_target_pairs={{0,12},{4,8},{8,4},{12,0},{16,28},{20,24},{24,20},{28,16},{1,13},{... | collective-permute-start | bytes 393224 | tf_op jit(solution)/shard_map/ppermute | solution.py:32
  27.2 25.4 %copy-start.16 = (bf16[256,256]{1,0:T(8,128)(2,1)}, bf16[256,256]{1,0:T(8,128)(2,1)S(1)}, u32[]{:S(2)}) copy-start(bf16[256,256]{1,0:T(8,128)(2,1)S(1)} %collective-permute-done.4.refs_2_) | copy-start | bytes 393220
  27.2 12.4 %collective-permute-start.9 = (bf16[256,256]{1,0:T(8,128)(2,1)S(1)}, bf16[256,256]{1,0:T(8,128)(2,1)S(1)}, u32[]{:S(2)}, u32[]{:S(2)}) collective-permute-start(bf16[256,256]{1,0:T(8,128)(2,1)S(1)} %copy-done.31), channel_id=1, source_target_pairs={{0,4},{4,0},{8,12},{12,8},{16,20},{20,16},{24,28},{28,24},{1,5},{5... | collective-permute-start | bytes 393224 | tf_op jit(solution)/shard_map/ppermute | solution.py:32
  29.2 23.4 %copy-start.18 = (bf16[256,256]{1,0:T(8,128)(2,1)}, bf16[256,256]{1,0:T(8,128)(2,1)S(1)}, u32[]{:S(2)}) copy-start(bf16[256,256]{1,0:T(8,128)(2,1)S(1)} %collective-permute-done.5.refs_3_) | copy-start | bytes 393220
  29.2 20.0 %collective-permute-start.17 = (bf16[256,256]{1,0:T(8,128)(2,1)}, bf16[256,256]{1,0:T(8,128)(2,1)S(1)}, u32[]{:S(2)}, u32[]{:S(2)}) collective-permute-start(bf16[256,256]{1,0:T(8,128)(2,1)} %get-tuple-element.55), channel_id=1, source_target_pairs={{0,16},{4,20},{8,24},{12,28},{16,0},{20,4},{24,8},{28,12},{1,17},{... | collective-permute-start | bytes 393224 | tf_op jit(solution)/shard_map/ppermute | solution.py:32
  33.8 18.8 %copy-start.19 = (bf16[256,256]{1,0:T(8,128)(2,1)}, bf16[256,256]{1,0:T(8,128)(2,1)S(1)}, u32[]{:S(2)}) copy-start(bf16[256,256]{1,0:T(8,128)(2,1)S(1)} %collective-permute-done.6.refs_4_) | copy-start | bytes 393220
  33.8 17.6 %collective-permute-start.18 = (bf16[256,256]{1,0:T(8,128)(2,1)}, bf16[256,256]{1,0:T(8,128)(2,1)S(1)}, u32[]{:S(2)}, u32[]{:S(2)}) collective-permute-start(bf16[256,256]{1,0:T(8,128)(2,1)} %get-tuple-element.56), channel_id=1, source_target_pairs={{0,20},{4,16},{8,28},{12,24},{16,4},{20,0},{24,12},{28,8},{1,21},{... | collective-permute-start | bytes 393224 | tf_op jit(solution)/shard_map/ppermute | solution.py:32
  36.1 16.5 %copy-start.24 = (bf16[256,256]{1,0:T(8,128)(2,1)}, bf16[256,256]{1,0:T(8,128)(2,1)S(1)}, u32[]{:S(2)}) copy-start(bf16[256,256]{1,0:T(8,128)(2,1)S(1)} %collective-permute-done.7.refs_5_) | copy-start | bytes 393220
  36.1 20.9 %collective-permute-start.19 = (bf16[256,256]{1,0:T(8,128)(2,1)}, bf16[256,256]{1,0:T(8,128)(2,1)S(1)}, u32[]{:S(2)}, u32[]{:S(2)}) collective-permute-start(bf16[256,256]{1,0:T(8,128)(2,1)} %get-tuple-element.57), channel_id=1, source_target_pairs={{0,24},{4,28},{8,16},{12,20},{16,8},{20,12},{24,0},{28,4},{1,25},{... | collective-permute-start | bytes 393224 | tf_op jit(solution)/shard_map/ppermute | solution.py:32
  36.7 15.9 %copy-start.26 = (bf16[256,256]{1,0:T(8,128)(2,1)}, bf16[256,256]{1,0:T(8,128)(2,1)S(1)}, u32[]{:S(2)}) copy-start(bf16[256,256]{1,0:T(8,128)(2,1)S(1)} %collective-permute-done.8.refs_6_) | copy-start | bytes 393220
  36.7 21.0 %collective-permute-start.20 = (bf16[256,256]{1,0:T(8,128)(2,1)}, bf16[256,256]{1,0:T(8,128)(2,1)S(1)}, u32[]{:S(2)}, u32[]{:S(2)}) collective-permute-start(bf16[256,256]{1,0:T(8,128)(2,1)} %get-tuple-element.58), channel_id=1, source_target_pairs={{0,28},{4,24},{8,20},{12,16},{16,12},{20,8},{24,4},{28,0},{1,29},{... | collective-permute-start | bytes 393224 | tf_op jit(solution)/shard_map/ppermute | solution.py:32
  39.7 12.9 %copy-start.28 = (bf16[256,256]{1,0:T(8,128)(2,1)}, bf16[256,256]{1,0:T(8,128)(2,1)S(1)}, u32[]{:S(2)}) copy-start(bf16[256,256]{1,0:T(8,128)(2,1)S(1)} %collective-permute-done.9.refs_7_) | copy-start | bytes 393220
  39.7 19.7 %collective-permute-start.21 = (bf16[256,256]{1,0:T(8,128)(2,1)}, bf16[256,256]{1,0:T(8,128)(2,1)S(1)}, u32[]{:S(2)}, u32[]{:S(2)}) collective-permute-start(bf16[256,256]{1,0:T(8,128)(2,1)} %get-tuple-element.59), channel_id=1, source_target_pairs={{0,8},{4,12},{8,0},{12,4},{16,24},{20,28},{24,16},{28,20},{1,9},{5... | collective-permute-start | bytes 393224 | tf_op jit(solution)/shard_map/ppermute | solution.py:32
  49.3 3.3 %copy-start.17 = (bf16[256,256]{1,0:T(8,128)(2,1)}, bf16[256,256]{1,0:T(8,128)(2,1)S(1)}, u32[]{:S(2)}) copy-start(bf16[256,256]{1,0:T(8,128)(2,1)S(1)} %collective-permute-done.17.refs_1_) | copy-start | bytes 393220
  49.3 13.0 %collective-permute-start.22 = (bf16[256,256]{1,0:T(8,128)(2,1)}, bf16[256,256]{1,0:T(8,128)(2,1)S(1)}, u32[]{:S(2)}, u32[]{:S(2)}) collective-permute-start(bf16[256,256]{1,0:T(8,128)(2,1)} %get-tuple-element.60), channel_id=1, source_target_pairs={{0,12},{4,8},{8,4},{12,0},{16,28},{20,24},{24,20},{28,16},{1,13},{... | collective-permute-start | bytes 393224 | tf_op jit(solution)/shard_map/ppermute | solution.py:32
  51.3 5.6 %copy-start.20 = (bf16[256,256]{1,0:T(8,128)(2,1)}, bf16[256,256]{1,0:T(8,128)(2,1)S(1)}, u32[]{:S(2)}) copy-start(bf16[256,256]{1,0:T(8,128)(2,1)S(1)} %collective-permute-done.18.refs_2_) | copy-start | bytes 393220
  51.3 11.9 %collective-permute-start.23 = (bf16[256,256]{1,0:T(8,128)(2,1)S(1)}, bf16[256,256]{1,0:T(8,128)(2,1)S(1)}, u32[]{:S(2)}, u32[]{:S(2)}) collective-permute-start(bf16[256,256]{1,0:T(8,128)(2,1)S(1)} %copy-done.30), channel_id=1, source_target_pairs={{0,4},{4,0},{8,12},{12,8},{16,20},{20,16},{24,28},{28,24},{1,5},{5... | collective-permute-start | bytes 393224 | tf_op jit(solution)/shard_map/ppermute | solution.py:32
  57.0 6.3 %copy-start.21 = (bf16[256,256]{1,0:T(8,128)(2,1)}, bf16[256,256]{1,0:T(8,128)(2,1)S(1)}, u32[]{:S(2)}) copy-start(bf16[256,256]{1,0:T(8,128)(2,1)S(1)} %collective-permute-done.19.refs_3_) | copy-start | bytes 393220
  57.0 11.3 %collective-permute-start.10 = (bf16[112,256]{1,0:T(8,128)(2,1)}, bf16[112,256]{1,0:T(8,128)(2,1)S(1)}, u32[]{:S(2)}, u32[]{:S(2)}) collective-permute-start(bf16[112,256]{1,0:T(8,128)(2,1)} %get-tuple-element.47), channel_id=1, source_target_pairs={{0,16},{4,20},{8,24},{12,28},{16,0},{20,4},{24,8},{28,12},{1,17},{... | collective-permute-start | bytes 172040 | tf_op jit(solution)/shard_map/ppermute | solution.py:32
  57.7 5.6 %copy-start.22 = (bf16[256,256]{1,0:T(8,128)(2,1)}, bf16[256,256]{1,0:T(8,128)(2,1)S(1)}, u32[]{:S(2)}) copy-start(bf16[256,256]{1,0:T(8,128)(2,1)S(1)} %collective-permute-done.20.refs_4_) | copy-start | bytes 393220
  57.7 11.6 %collective-permute-start.11 = (bf16[112,256]{1,0:T(8,128)(2,1)}, bf16[112,256]{1,0:T(8,128)(2,1)S(1)}, u32[]{:S(2)}, u32[]{:S(2)}) collective-permute-start(bf16[112,256]{1,0:T(8,128)(2,1)} %get-tuple-element.48), channel_id=1, source_target_pairs={{0,20},{4,16},{8,28},{12,24},{16,4},{20,0},{24,12},{28,8},{1,21},{... | collective-permute-start | bytes 172040 | tf_op jit(solution)/shard_map/ppermute | solution.py:32
  59.4 3.9 %copy-start.23 = (bf16[256,256]{1,0:T(8,128)(2,1)}, bf16[256,256]{1,0:T(8,128)(2,1)S(1)}, u32[]{:S(2)}) copy-start(bf16[256,256]{1,0:T(8,128)(2,1)S(1)} %collective-permute-done.21.refs_5_) | copy-start | bytes 393220
  59.4 10.7 %collective-permute-start.12 = (bf16[112,256]{1,0:T(8,128)(2,1)}, bf16[112,256]{1,0:T(8,128)(2,1)S(1)}, u32[]{:S(2)}, u32[]{:S(2)}) collective-permute-start(bf16[112,256]{1,0:T(8,128)(2,1)} %get-tuple-element.49), channel_id=1, source_target_pairs={{0,24},{4,28},{8,16},{12,20},{16,8},{20,12},{24,0},{28,4},{1,25},{... | collective-permute-start | bytes 172040 | tf_op jit(solution)/shard_map/ppermute | solution.py:32
  62.2 9.4 %collective-permute-start.13 = (bf16[112,256]{1,0:T(8,128)(2,1)}, bf16[112,256]{1,0:T(8,128)(2,1)S(1)}, u32[]{:S(2)}, u32[]{:S(2)}) collective-permute-start(bf16[112,256]{1,0:T(8,128)(2,1)} %get-tuple-element.50), channel_id=1, source_target_pairs={{0,28},{4,24},{8,20},{12,16},{16,12},{20,8},{24,4},{28,0},{1,29},{... | collective-permute-start | bytes 172040 | tf_op jit(solution)/shard_map/ppermute | solution.py:32
  63.3 9.1 %collective-permute-start.14 = (bf16[112,256]{1,0:T(8,128)(2,1)}, bf16[112,256]{1,0:T(8,128)(2,1)S(1)}, u32[]{:S(2)}, u32[]{:S(2)}) collective-permute-start(bf16[112,256]{1,0:T(8,128)(2,1)} %get-tuple-element.51), channel_id=1, source_target_pairs={{0,8},{4,12},{8,0},{12,4},{16,24},{20,28},{24,16},{28,20},{1,9},{5... | collective-permute-start | bytes 172040 | tf_op jit(solution)/shard_map/ppermute | solution.py:32
  63.9 4.4 %copy-start.35 = (bf16[112,256]{1,0:T(8,128)(2,1)S(1)}, bf16[112,256]{1,0:T(8,128)(2,1)}, u32[]{:S(2)}) copy-start(bf16[112,256]{1,0:T(8,128)(2,1)} %get-tuple-element.52) | copy-start | bytes 172036
  63.9 5.3 %copy-start.34 = (bf16[112,256]{1,0:T(8,128)(2,1)S(1)}, bf16[112,256]{1,0:T(8,128)(2,1)}, u32[]{:S(2)}) copy-start(bf16[112,256]{1,0:T(8,128)(2,1)} %get-tuple-element.53) | copy-start | bytes 172036
  68.3 15.3 %copy-start.1 = (bf16[112,256]{1,0:T(8,128)(2,1)}, bf16[112,256]{1,0:T(8,128)(2,1)S(1)}, u32[]{:S(2)}) copy-start(bf16[112,256]{1,0:T(8,128)(2,1)S(1)} %collective-permute-done.10.refs_1_) | copy-start | bytes 172036
  68.3 6.6 %collective-permute-start.15 = (bf16[112,256]{1,0:T(8,128)(2,1)S(1)}, bf16[112,256]{1,0:T(8,128)(2,1)S(1)}, u32[]{:S(2)}, u32[]{:S(2)}) collective-permute-start(bf16[112,256]{1,0:T(8,128)(2,1)S(1)} %copy-done.35), channel_id=1, source_target_pairs={{0,12},{4,8},{8,4},{12,0},{16,28},{20,24},{24,20},{28,16},{1,13},{... | collective-permute-start | bytes 172040 | tf_op jit(solution)/shard_map/ppermute | solution.py:32
  69.2 14.5 %copy-start.2 = (bf16[112,256]{1,0:T(8,128)(2,1)}, bf16[112,256]{1,0:T(8,128)(2,1)S(1)}, u32[]{:S(2)}) copy-start(bf16[112,256]{1,0:T(8,128)(2,1)S(1)} %collective-permute-done.11.refs_2_) | copy-start | bytes 172036
  69.2 7.0 %collective-permute-start.16 = (bf16[112,256]{1,0:T(8,128)(2,1)S(1)}, bf16[112,256]{1,0:T(8,128)(2,1)S(1)}, u32[]{:S(2)}, u32[]{:S(2)}) collective-permute-start(bf16[112,256]{1,0:T(8,128)(2,1)S(1)} %copy-done.34), channel_id=1, source_target_pairs={{0,4},{4,0},{8,12},{12,8},{16,20},{20,16},{24,28},{28,24},{1,5},{5... | collective-permute-start | bytes 172040 | tf_op jit(solution)/shard_map/ppermute | solution.py:32
  70.0 13.6 %copy-start.3 = (bf16[112,256]{1,0:T(8,128)(2,1)}, bf16[112,256]{1,0:T(8,128)(2,1)S(1)}, u32[]{:S(2)}) copy-start(bf16[112,256]{1,0:T(8,128)(2,1)S(1)} %collective-permute-done.12.refs_3_) | copy-start | bytes 172036
  70.0 9.2 %collective-permute-start.24 = (bf16[112,256]{1,0:T(8,128)(2,1)}, bf16[112,256]{1,0:T(8,128)(2,1)S(1)}, u32[]{:S(2)}, u32[]{:S(2)}) collective-permute-start(bf16[112,256]{1,0:T(8,128)(2,1)} %get-tuple-element.63), channel_id=1, source_target_pairs={{0,16},{4,20},{8,24},{12,28},{16,0},{20,4},{24,8},{28,12},{1,17},{... | collective-permute-start | bytes 172040 | tf_op jit(solution)/shard_map/ppermute | solution.py:32
  71.7 12.0 %copy-start.4 = (bf16[112,256]{1,0:T(8,128)(2,1)}, bf16[112,256]{1,0:T(8,128)(2,1)S(1)}, u32[]{:S(2)}) copy-start(bf16[112,256]{1,0:T(8,128)(2,1)S(1)} %collective-permute-done.13.refs_4_) | copy-start | bytes 172036
  71.7 7.9 %collective-permute-start.25 = (bf16[112,256]{1,0:T(8,128)(2,1)}, bf16[112,256]{1,0:T(8,128)(2,1)S(1)}, u32[]{:S(2)}, u32[]{:S(2)}) collective-permute-start(bf16[112,256]{1,0:T(8,128)(2,1)} %get-tuple-element.64), channel_id=1, source_target_pairs={{0,20},{4,16},{8,28},{12,24},{16,4},{20,0},{24,12},{28,8},{1,21},{... | collective-permute-start | bytes 172040 | tf_op jit(solution)/shard_map/ppermute | solution.py:32
  72.4 11.3 %copy-start.5 = (bf16[112,256]{1,0:T(8,128)(2,1)}, bf16[112,256]{1,0:T(8,128)(2,1)S(1)}, u32[]{:S(2)}) copy-start(bf16[112,256]{1,0:T(8,128)(2,1)S(1)} %collective-permute-done.14.refs_5_) | copy-start | bytes 172036
  72.4 9.1 %collective-permute-start.26 = (bf16[112,256]{1,0:T(8,128)(2,1)}, bf16[112,256]{1,0:T(8,128)(2,1)S(1)}, u32[]{:S(2)}, u32[]{:S(2)}) collective-permute-start(bf16[112,256]{1,0:T(8,128)(2,1)} %get-tuple-element.65), channel_id=1, source_target_pairs={{0,24},{4,28},{8,16},{12,20},{16,8},{20,12},{24,0},{28,4},{1,25},{... | collective-permute-start | bytes 172040 | tf_op jit(solution)/shard_map/ppermute | solution.py:32
  74.9 8.8 %copy-start.6 = (bf16[112,256]{1,0:T(8,128)(2,1)}, bf16[112,256]{1,0:T(8,128)(2,1)S(1)}, u32[]{:S(2)}) copy-start(bf16[112,256]{1,0:T(8,128)(2,1)S(1)} %collective-permute-done.15.refs_6_) | copy-start | bytes 172036
  74.9 6.5 %collective-permute-start.27 = (bf16[112,256]{1,0:T(8,128)(2,1)}, bf16[112,256]{1,0:T(8,128)(2,1)S(1)}, u32[]{:S(2)}, u32[]{:S(2)}) collective-permute-start(bf16[112,256]{1,0:T(8,128)(2,1)} %get-tuple-element.66), channel_id=1, source_target_pairs={{0,28},{4,24},{8,20},{12,16},{16,12},{20,8},{24,4},{28,0},{1,29},{... | collective-permute-start | bytes 172040 | tf_op jit(solution)/shard_map/ppermute | solution.py:32
  76.3 7.5 %copy-start.7 = (bf16[112,256]{1,0:T(8,128)(2,1)}, bf16[112,256]{1,0:T(8,128)(2,1)S(1)}, u32[]{:S(2)}) copy-start(bf16[112,256]{1,0:T(8,128)(2,1)S(1)} %collective-permute-done.16.refs_7_) | copy-start | bytes 172036
  76.3 6.2 %collective-permute-start.28 = (bf16[112,256]{1,0:T(8,128)(2,1)}, bf16[112,256]{1,0:T(8,128)(2,1)S(1)}, u32[]{:S(2)}, u32[]{:S(2)}) collective-permute-start(bf16[112,256]{1,0:T(8,128)(2,1)} %get-tuple-element.67), channel_id=1, source_target_pairs={{0,8},{4,12},{8,0},{12,4},{16,24},{20,28},{24,16},{28,20},{1,9},{5... | collective-permute-start | bytes 172040 | tf_op jit(solution)/shard_map/ppermute | solution.py:32
  79.2 4.5 %copy-start.8 = (bf16[112,256]{1,0:T(8,128)(2,1)}, bf16[112,256]{1,0:T(8,128)(2,1)S(1)}, u32[]{:S(2)}) copy-start(bf16[112,256]{1,0:T(8,128)(2,1)S(1)} %collective-permute-done.24.refs_9_) | copy-start | bytes 172036
  79.2 4.4 %collective-permute-start.29 = (bf16[112,256]{1,0:T(8,128)(2,1)}, bf16[112,256]{1,0:T(8,128)(2,1)S(1)}, u32[]{:S(2)}, u32[]{:S(2)}) collective-permute-start(bf16[112,256]{1,0:T(8,128)(2,1)} %get-tuple-element.68), channel_id=1, source_target_pairs={{0,12},{4,8},{8,4},{12,0},{16,28},{20,24},{24,20},{28,16},{1,13},{... | collective-permute-start | bytes 172040 | tf_op jit(solution)/shard_map/ppermute | solution.py:32
  79.6 4.2 %copy-start.9 = (bf16[112,256]{1,0:T(8,128)(2,1)}, bf16[112,256]{1,0:T(8,128)(2,1)S(1)}, u32[]{:S(2)}) copy-start(bf16[112,256]{1,0:T(8,128)(2,1)S(1)} %collective-permute-done.25.refs_10_) | copy-start | bytes 172036
  79.6 4.1 %collective-permute-start.30 = (bf16[112,256]{1,0:T(8,128)(2,1)}, bf16[112,256]{1,0:T(8,128)(2,1)S(1)}, u32[]{:S(2)}, u32[]{:S(2)}) collective-permute-start(bf16[112,256]{1,0:T(8,128)(2,1)} %get-tuple-element.69), channel_id=1, source_target_pairs={{0,4},{4,0},{8,12},{12,8},{16,20},{20,16},{24,28},{28,24},{1,5},{5... | collective-permute-start | bytes 172040 | tf_op jit(solution)/shard_map/ppermute | solution.py:32
  81.5 2.3 %copy-start.11 = (bf16[112,256]{1,0:T(8,128)(2,1)}, bf16[112,256]{1,0:T(8,128)(2,1)S(1)}, u32[]{:S(2)}) copy-start(bf16[112,256]{1,0:T(8,128)(2,1)S(1)} %collective-permute-done.27.refs_12_) | copy-start | bytes 172036
  85.9 6.6 %collective-permute-start.33 = (f32[4,4,1024]{2,1,0:T(4,128)}, f32[4,4,1024]{2,1,0:T(4,128)S(1)}, u32[]{:S(2)}, u32[]{:S(2)}) collective-permute-start(f32[4,4,1024]{2,1,0:T(4,128)} %get-tuple-element.73), channel_id=1, source_target_pairs={{0,3},{1,2},{2,1},{3,0},{4,7},{5,6},{6,5},{7,4},{8,11},{9,10},{10,... | collective-permute-start | bytes 196616 | tf_op jit(solution)/shard_map/ppermute | solution.py:32
  87.4 5.1 %collective-permute-start.32 = (f32[4,4,1024]{2,1,0:T(4,128)}, f32[4,4,1024]{2,1,0:T(4,128)S(1)}, u32[]{:S(2)}, u32[]{:S(2)}) collective-permute-start(f32[4,4,1024]{2,1,0:T(4,128)} %get-tuple-element.72), channel_id=1, source_target_pairs={{0,2},{1,3},{2,0},{3,1},{4,6},{5,7},{6,4},{7,5},{8,10},{9,11},{10,... | collective-permute-start | bytes 196616 | tf_op jit(solution)/shard_map/ppermute | solution.py:32
  88.0 4.7 %copy-start.29 = (f32[4,4,1024]{2,1,0:T(4,128)S(1)}, f32[4,4,1024]{2,1,0:T(4,128)}, u32[]{:S(2)}) copy-start(f32[4,4,1024]{2,1,0:T(4,128)} %get-tuple-element.70) | copy-start | bytes 196612
  88.0 4.7 %collective-permute-start.31 = (f32[4,4,1024]{2,1,0:T(4,128)}, f32[4,4,1024]{2,1,0:T(4,128)S(1)}, u32[]{:S(2)}, u32[]{:S(2)}) collective-permute-start(f32[4,4,1024]{2,1,0:T(4,128)} %get-tuple-element.71), channel_id=1, source_target_pairs={{0,1},{1,0},{2,3},{3,2},{4,5},{5,4},{6,7},{7,6},{8,9},{9,8},{10,11... | collective-permute-start | bytes 196616 | tf_op jit(solution)/shard_map/ppermute | solution.py:32
  (6 other events, 6.6 us)
